TPU v7x, 8 devices: a whole 2x2x1 slice. The times are simulated.
8 devices in a mesh: dp: 2 (over z, y), sp: 4 (over x, core).
Axes of the slice: x: 2, y: 2, z: 1, core: 2. Of those that a mesh axis runs over, the one named last changes fastest.
Arguments:
- tokens: bfloat16 [128, 2048], P('dp'), parts along dimension 0
- positions: int32 [128], P('dp'), parts along dimension 0
- k_cache: bfloat16 [128, 1024, 4, 128], P('dp', 'sp'), parts along dimension 0
- v_cache: bfloat16 [128, 1024, 4, 128], P('dp', 'sp'), parts along dimension 0
- w_q: bfloat16 [2048, 4096], replicated
- w_k: bfloat16 [2048, 512], replicated
- w_v: bfloat16 [2048, 512], replicated
- w_o: bfloat16 [4096, 2048], replicated
- attn_norm: bfloat16 [2048], replicated
- q_norm: bfloat16 [128], replicated
- k_norm: bfloat16 [128], replicated
Outputs:
- output 1: bfloat16 [128, 2048], P('dp'), parts along dimension 0
- output 2: bfloat16 [128, 1024, 4, 128], P('dp', 'sp'), parts along dimension 0
- output 3: bfloat16 [128, 1024, 4, 128], P('dp', 'sp'), parts along dimension 0
- output 4: bfloat16 [128, 2, 4, 128], P('dp'), parts along dimension 0
There are 2 independent parts. A program takes and returns all parts, laid end to end along the dimension named above; an argument that names none is the same for every part.
All inputs are finite; a program needn't handle non-finite values.
Results may differ from a plain program's by a relative error of at most 0.00658002.
Values sent between devices are 32-bit elements.
A program may use at most 1 GiB of HBM per device.

v0:
```python
import jax
import jax.numpy as jnp
from jax import lax
from jax.sharding import PartitionSpec as P

NORM_EPS = 1e-6
ROPE_THETA = 1000000.0
NEG_FILL = -1e30


def rms_scale(values, gain):
    return values * lax.rsqrt(jnp.mean(values * values, axis=-1, keepdims=True) + NORM_EPS) * gain.astype(jnp.float32)


def rope_table(positions, head_dim):
    inv_freq = ROPE_THETA ** (-jnp.arange(head_dim // 2, dtype=jnp.float32) * 2.0 / head_dim)
    angles = positions.astype(jnp.float32)[:, None] * inv_freq[None, :]
    return jnp.cos(angles)[:, None, :], jnp.sin(angles)[:, None, :]


def norm_rope(proj, gain, cos_table, sin_table):
    normed = rms_scale(proj.astype(jnp.float32), gain)
    half_dim = proj.shape[-1] // 2
    first_half = normed[..., :half_dim]
    second_half = normed[..., half_dim:]
    rotated = jnp.concatenate([first_half * cos_table - second_half * sin_table, second_half * cos_table + first_half * sin_table], axis=-1)
    return rotated.astype(jnp.bfloat16)


def project_token(tokens, positions, w_q, w_k, w_v, attn_norm, q_norm, k_norm):
    seq_count = tokens.shape[0]
    head_dim = q_norm.shape[0]
    hidden = rms_scale(tokens.astype(jnp.float32), attn_norm).astype(jnp.bfloat16)
    q_proj = jnp.dot(hidden, w_q, preferred_element_type=jnp.float32).astype(jnp.bfloat16).reshape(seq_count, -1, head_dim)
    k_proj = jnp.dot(hidden, w_k, preferred_element_type=jnp.float32).astype(jnp.bfloat16).reshape(seq_count, -1, head_dim)
    v_new = jnp.dot(hidden, w_v, preferred_element_type=jnp.float32).astype(jnp.bfloat16).reshape(seq_count, -1, head_dim)
    cos_table, sin_table = rope_table(positions, head_dim)
    return norm_rope(q_proj, q_norm, cos_table, sin_table), norm_rope(k_proj, k_norm, cos_table, sin_table), v_new


def local_attention(q_rot, k_rot, v_new, positions, k_loc, v_loc, shard_start):
    seq_count, slot_count, kv_heads, head_dim = k_loc.shape
    q_per_kv = q_rot.shape[1] // kv_heads
    score_scale = head_dim ** -0.5
    slot_ids = shard_start + jnp.arange(slot_count)
    write_mask = (slot_ids[None, :] == positions[:, None])[:, :, None, None]
    k_upd = jnp.where(write_mask, k_rot[:, None], k_loc)
    v_upd = jnp.where(write_mask, v_new[:, None], v_loc)
    q_grp = q_rot.reshape(seq_count, kv_heads, q_per_kv, head_dim)
    scores = jnp.einsum('bkgd,btkd->bkgt', q_grp, k_upd, preferred_element_type=jnp.float32) * score_scale
    live_mask = (slot_ids[None, :] <= positions[:, None])[:, None, None, :]
    local_peak = jnp.max(jnp.where(live_mask, scores, NEG_FILL), axis=-1)
    weights = jnp.where(live_mask, jnp.exp(scores - local_peak[..., None]), 0.0)
    local_sum = jnp.sum(weights, axis=-1)
    local_out = jnp.einsum('bkgt,btkd->bkgd', weights.astype(jnp.bfloat16), v_upd, preferred_element_type=jnp.float32)
    return k_upd, v_upd, local_peak, local_sum, local_out


def solution(mesh):
    cache_spec = P('dp', 'sp', None, None)

    def device_step(tokens, positions, k_cache, v_cache, w_q, w_k, w_v, w_o, attn_norm, q_norm, k_norm):
        q_rot, k_rot, v_new = project_token(tokens, positions, w_q, w_k, w_v, attn_norm, q_norm, k_norm)
        head_dim = q_norm.shape[0]
        shard_start = lax.axis_index('sp') * k_cache.shape[1]
        k_upd, v_upd, local_peak, local_sum, local_out = local_attention(q_rot, k_rot, v_new, positions, k_cache, v_cache, shard_start)
        global_peak = lax.pmax(local_peak, 'sp')
        factor = jnp.exp(local_peak - global_peak)
        packed = jnp.concatenate([local_out * factor[..., None], (local_sum * factor)[..., None]], axis=-1)
        summed = lax.psum(packed, 'sp')
        attn_out = (summed[..., :head_dim] / summed[..., head_dim:]).astype(jnp.bfloat16).reshape(tokens.shape[0], -1)
        block_out = (tokens.astype(jnp.float32) + jnp.dot(attn_out, w_o, preferred_element_type=jnp.float32)).astype(jnp.bfloat16)
        return block_out, k_upd, v_upd, jnp.stack([k_rot, v_new], axis=1)

    return jax.shard_map(device_step, mesh=mesh, in_specs=(P('dp', None), P('dp'), cache_spec, cache_spec, P(), P(), P(), P(), P(), P(), P()), out_specs=(P('dp', None), cache_spec, cache_spec, P('dp', None, None, None)), check_vma=False)
```

profile of v0, /device:TPU:0, one launch (start us, length us, event | category | flops | bytes accessed | tf_op | source)
XLA Modules:
  0.0 161.1 jit_solution(2432320942993113133)
XLA Ops:
  7.3 0.8 convert_element_type.66
  8.1 0.7 convert_element_type.71
  9.4 1.1 fusion.19
  10.5 0.7 convert_element_type.61
  11.2 1.3 broadcast_compare_fusion.1
  12.6 1.5 convolution_convert_fusion.1
  14.7 2.1 %fusion.12 = f32[64,512]{1,0:T(8,128)S(1)} fusion(bf16[2048,512]{1,0:T(8,128)(2,1)} %param.16, bf16[64,2048]{1,0:T(8,128)(2,1)S(1)} %copy-done.3, f32[2048]{0:T(1024)S(1)} %convert_element_type.61, f32[64]{0:T(128)S(1)} %add_rsqrt_fusion.2), kind=kOutput, calls=%fused_computation.19 | convolution fusion | flops 134807552 | bytes 2498816 | tf_op jit(solution)/shard_map/dot_general | solution.py:35
  17.0 9.0 %fusion.8 = f32[8,8,32,128]{3,1,2,0:T(8,128)S(1)} fusion(bf16[2048,4096]{1,0:T(8,128)(2,1)} %param.15, bf16[64,2048]{1,0:T(8,128)(2,1)S(1)} %copy-done.3, f32[2048]{0:T(1024)S(1)} %convert_element_type.61, f32[64]{0:T(128)S(1)} %add_rsqrt_fusion.2), kind=kOutput, calls=%fused_computation.15 | convolution fusion | flops 1074790400 | bytes 18096384 | tf_op jit(solution)/shard_map/dot_general | solution.py:34
  28.2 3.0 %copy-done.2 = bf16[64,256,4,128]{3,2,1,0:T(4,128)(2,1)S(1)} copy-done((bf16[64,256,4,128]{3,2,1,0:T(4,128)(2,1)S(1)}, bf16[64,256,4,128]{3,2,1,0:T(4,128)(2,1)}, u32[]{:S(2)}) %copy-start.2) | copy-done | bytes 16777240
  31.3 1.4 slice-done.3
  32.7 24.4 %broadcast_select_fusion = (bf16[64,256,4,128]{3,2,1,0:T(4,128)(2,1)}, bf16[64,256,4,128]{3,2,1,0:T(4,128)(2,1)}) fusion(bf16[64,256,4,128]{3,2,1,0:T(4,128)(2,1)S(1)} %bitcast.26, pred[64,256]{1,0:T(8,128)(4,1)S(1)} %copy-done.10, bf16[64,4,128]{2,1,0:T(4,128)(2,1)S(1)} %broadcast_in_dim.71, bf16[64,256,4,128]{3,2,1,0:T(4,128)(2,1)S(1)} %copy-done.2, ...), kind=kLoop, calls=%fused_computation.4 | loop fusion | flops 16777216 | bytes 67256320 | tf_op jit(solution)/shard_map/jit(_where)/select_n | solution.py:48
  57.1 9.3 %select_reduce_fusion = (f32[64,4,8]{2,1,0:T(4,128)S(1)}, f32[64,4,8,256]{3,2,1,0:T(8,128)S(1)}) fusion(pred[64,256]{1,0:T(8,128)(4,1)S(1)} %get-tuple-element.12, bf16[64,256,4,128]{3,2,1,0:T(4,128)(2,1)} %get-tuple-element.11, bf16[64,4,8,64]{3,2,1,0:T(8,128)(2,1)S(1)} %get-tuple-element.7, bf16[64,4,8,64]{3,2,1,0:T(8,128)(2,1)S(1)} %get-tuple-element.6), kind=kOutput, calls=%fused_computation.12 | convolution fusion | flops 136837120 | bytes 19423232 | tf_op jit(solution)/shard_map/bkgd,btkd->bkgt/dot_general | solution.py:50
  66.4 15.0 %pmax.7 = f32[64,4,8]{2,1,0:T(4,128)S(1)} all-reduce(f32[64,4,8]{2,1,0:T(4,128)S(1)} %get-tuple-element.16), channel_id=1, replica_groups=mesh['dp'=2,'sp'=4] {'sp'}, use_global_device_ids=true, to_apply=%region_4.5 | all-reduce | flops 2048 | bytes 16384 | tf_op jit(solution)/shard_map/pmax | solution.py:67
  81.4 0.9 fusion.6
  82.3 0.8 multiply_bitcast_fusion
  83.1 2.5 %copy.50 = f32[64,4,8,1]{3,2,1,0:T(8,128)S(1)} copy(f32[64,4,8,1]{2,1,0,3:T(4,128)} %get-tuple-element.4) | data formatting | bytes 16384 | tf_op jit(solution)/shard_map/broadcast_in_dim | solution.py:69
  85.5 8.1 %fusion.9 = f32[64,4,8,128]{3,2,1,0:T(8,128)S(1)} fusion(bf16[64,256,4,128]{3,2,1,0:T(4,128)(2,1)} %get-tuple-element.10, f32[64,4,8,256]{3,2,1,0:T(8,128)S(1)} %get-tuple-element.17, f32[64,4,8]{2,1,0:T(4,128)S(1)} %get-tuple-element.16, pred[64,256]{1,0:T(8,128)(4,1)S(1)} %get-tuple-element.12, f32[64,4,8]{2,1,0:T(4,128)} %get-tuple-element.5), kind=kOutput, calls=%fused_computation.16 | convolution fusion | flops 136577024 | bytes 19955712 | tf_op jit(solution)/shard_map/bkgt,btkd->bkgd/dot_general | solution.py:55
  93.6 1.5 pad_maximum_fusion
  95.2 0.8 copy-done.9
  96.0 0.8 pad_maximum_fusion.1
  96.8 44.2 %all-reduce.2.cloned.1.call-done = f32[64,4,8,129]{3,2,1,0:T(8,128)} async-done(((f32[64,4,8,129]{3,2,1,0:T(8,128)}), f32[64,4,8,129]{3,2,1,0:T(8,128)}) %all-reduce.2.cloned.1.call-update) | async-done | bytes 1056784 | tf_op jit(solution)/shard_map/psum | solution.py:70
  141.0 1.2 slice-done.4
  143.0 1.6 fusion.14
  144.6 9.6 %fusion.5 = bf16[64,2048]{1,0:T(8,128)(2,1)} fusion(bf16[4096,2048]{1,0:T(8,128)(2,1)} %param.18, bf16[64,2048]{1,0:T(8,128)(2,1)S(1)} %copy-done.3, bf16[8,8,32,128]{3,2,1,0:T(8,128)(2,1)S(1)} %bitcast.28), kind=kOutput, calls=%fused_computation.9 | convolution fusion | flops 1074135040 | bytes 17825792 | tf_op jit(solution)/shard_map/dot_general | solution.py:72
  (51 shorter events, 4.4 us)
Async XLA Ops:
  7.2 5.4 %copy-start = (bf16[2048,512]{1,0:T(8,128)(2,1)S(1)}, bf16[2048,512]{1,0:T(8,128)(2,1)}, u32[]{:S(2)}) copy-start(bf16[2048,512]{1,0:T(8,128)(2,1)} %param.17) | copy-start | bytes 6291460
  7.2 7.5 %copy-start.3 = (bf16[64,2048]{1,0:T(8,128)(2,1)S(1)}, bf16[64,2048]{1,0:T(8,128)(2,1)}, u32[]{:S(2)}) copy-start(bf16[64,2048]{1,0:T(8,128)(2,1)} %param.11) | copy-start | bytes 786436
  7.2 133.8 %all-reduce.2.cloned.1.call-start = ((), (), s32[]{:S(2)}) async-start(), calls=%async_computation | async-start | bytes 4194304 | tf_op jit(solution)/shard_map/psum | solution.py:70
  14.0 0.6 copy-start.8
  17.0 11.2 %slice-start = ((s8[16777216]{0:T(1024)(128)(4,1)}), s8[4194304]{0:T(1024)(128)(4,1)S(1)}, s32[]{:S(2)}) async-start(s8[16777216]{0:T(1024)(128)(4,1)} %bitcast.25), calls=%async_computation.1 | async-start | bytes 8388608
  17.0 11.2 %slice-start.1 = ((s8[16777216]{0:T(1024)(128)(4,1)}), s8[4194304]{0:T(1024)(128)(4,1)S(1)}, s32[]{:S(2)}) async-start(s8[16777216]{0:T(1024)(128)(4,1)} %bitcast.25), calls=%async_computation.2 | async-start | bytes 8388608
  17.0 11.2 %slice-start.2 = ((s8[16777216]{0:T(1024)(128)(4,1)}), s8[4194304]{0:T(1024)(128)(4,1)S(1)}, s32[]{:S(2)}) async-start(s8[16777216]{0:T(1024)(128)(4,1)} %bitcast.25), calls=%async_computation.3 | async-start | bytes 8388608
  17.0 14.2 %copy-start.2 = (bf16[64,256,4,128]{3,2,1,0:T(4,128)(2,1)S(1)}, bf16[64,256,4,128]{3,2,1,0:T(4,128)(2,1)}, u32[]{:S(2)}) copy-start(bf16[64,256,4,128]{3,2,1,0:T(4,128)(2,1)} %param.13) | copy-start | bytes 50331652
  26.1 6.6 %slice-start.3 = ((s8[16777216]{0:T(1024)(128)(4,1)}), s8[4194304]{0:T(1024)(128)(4,1)S(1)}, s32[]{:S(2)}) async-start(s8[16777216]{0:T(1024)(128)(4,1)} %bitcast.25), calls=%async_computation.4 | async-start | bytes 8388608
  27.3 5.3 %copy-start.10 = (pred[64,256]{1,0:T(8,128)(4,1)S(1)}, pred[64,256]{1,0:T(8,128)(4,1)}, u32[]{:S(2)}) copy-start(pred[64,256]{1,0:T(8,128)(4,1)} %get-tuple-element.13) | copy-start | bytes 49156
  27.5 29.6 %copy-start.4 = (bf16[64,4,64]{2,1,0:T(4,128)(2,1)}, bf16[64,4,64]{2,1,0:T(4,128)(2,1)S(1)}, u32[]{:S(2)}) copy-start(bf16[64,4,64]{2,1,0:T(4,128)(2,1)S(1)} %get-tuple-element.8) | copy-start | bytes 98308
  27.5 29.6 %copy-start.6 = (bf16[64,4,64]{2,1,0:T(4,128)(2,1)}, bf16[64,4,64]{2,1,0:T(4,128)(2,1)S(1)}, u32[]{:S(2)}) copy-start(bf16[64,4,64]{2,1,0:T(4,128)(2,1)S(1)} %get-tuple-element.9) | copy-start | bytes 98308
  95.1 0.8 copy-start.9
  95.1 0.9 copy-start.5
  95.1 0.9 copy-start.7
  141.0 1.2 slice-start.4
  144.6 9.7 %copy-start.1 = (bf16[2048,512]{1,0:T(8,128)(2,1)S(1)}, bf16[2048,512]{1,0:T(8,128)(2,1)}, u32[]{:S(2)}) copy-start(bf16[2048,512]{1,0:T(8,128)(2,1)} %param.17) | copy-start | bytes 6291460
Sparse Core Ops, SparseCore 0:
  95.3 45.6 all-reduce.1
where the time goes:
time: 162 us; the launch traced here: 161 us
  waiting for transfers between devices  44.2 us (27%)
  matrix products  39.7 us (25%)
  other arithmetic  37.2 us (23%)
  blocking collectives  15 us (9%)
  between operations  14.3 us (9%)
  local copies, waits for them, and re-layouts  10.6 us (7%)
    psum x1, waiting for transfers between devices, device_step(): summed = lax.psum(packed, 'sp')  44.2 us
    select_n x1, other arithmetic, local_attention(): v_upd = jnp.where(write_mask, v_new[:, None], v_loc)  24.4 us
    pmax x1, blocking collectives, device_step(): global_peak = lax.pmax(local_peak, 'sp')  15 us
    dot_general x1, matrix products, device_step(): jnp.dot(attn_out, w_o, preferred_element_type=jnp.float32)  9.64 us
    dot_general x1, matrix products, local_attention(): jnp.einsum('bkgd,btkd->bkgt', q_grp, k_upd, preferred_element_type=jnp.fl...  9.32 us
    dot_general x1, matrix products, project_token(): jnp.dot(hidden, w_q, preferred_element_type=jnp.float32)  9.04 us
    dot_general x1, matrix products, local_attention(): jnp.einsum('bkgt,btkd->bkgd', weights.astype(jnp.bfloat16), v_upd, prefer...  8.07 us
    unnamed x31, local copies, waits for them, and re-layouts  6.15 us
  transfers between devices with their start and end apart: 1, of which 1 were waited for; matrix products, arithmetic and copies ran while one was open for 0% of the time, Pallas kernels for 0%

commit v1 on v0

v1 whole, which is shorter than its diff:
```python
import functools

import jax
import jax.numpy as jnp
import numpy as np
from jax import lax
from jax.experimental import pallas as pl
from jax.experimental.pallas import tpu as pltpu
from jax.sharding import PartitionSpec as P

NORM_EPS = 1e-6
ROPE_THETA = 1000000.0
MESH = pl.DeviceIdType.MESH
BF16 = jnp.bfloat16
F32 = jnp.float32

SEQS = 64
DIM = 2048
HD = 128
KVH = 4
HALF = 16
SLOTS = 256
ROWS = SLOTS * KVH
BLK = 8
NBLK = SEQS // BLK
WCH = 512
PIECE = (HALF + 1) * BLK
VMEM_LIMIT = 26 * 2**20
EXP_SCALE = HD ** -0.5 * 1.4426950408889634
NEG = -jnp.inf


def bcast_col(tile, col):
    return jnp.broadcast_to(tile[:, col:col + 1], (tile.shape[0], HD))


def attend_kernel(pos_s, tok, aux, wq, wk, wv, wo, kc, vc,
                  kv, vv, rep, bout,
                  w_s, hid, ang, cosr, sinr, qmine, qmate, colslot, opart, drx, comb, xrx, ofin, pbuf, prx,
                  wsem, ksem, vsem, wosem, qs, qr, ds_, dr, xs, xr, ps, pr):
    me = lax.axis_index('sp')
    core = lax.rem(me, 2)
    chip = me // 2
    mate = {'sp': me + 1 - 2 * core}
    peer = {'sp': me + 2 - 4 * chip}

    def w_copy(n):
        if n < 4:
            src = wq.at[:, pl.ds(pl.multiple_of(core * (HALF * HD) + n * WCH, WCH), WCH)]
        else:
            src = (wk, wv)[n - 4]
        return pltpu.make_async_copy(src, w_s.at[n], wsem.at[n])

    def wo_copy(n):
        src = wo.at[pl.ds(pl.multiple_of(core * (HALF * HD), HD), HALF * HD), pl.ds(n * WCH, WCH)]
        return pltpu.make_async_copy(src, w_s.at[n], wosem.at[n])

    def k_copy(i):
        return pltpu.make_async_copy(kc.at[pl.ds(i * BLK, BLK)], kv.at[pl.ds(i * BLK, BLK)], ksem.at[i])

    def v_copy(i):
        return pltpu.make_async_copy(vc.at[pl.ds(i * BLK, BLK)], vv.at[pl.ds(i * BLK, BLK)], vsem.at[i])

    def q_send():
        return pltpu.make_async_remote_copy(qmine, qmate, qs, qr, device_id=mate, device_id_type=MESH)

    def d_send(i):
        return pltpu.make_async_remote_copy(opart.at[i, pl.ds(PIECE, PIECE)], drx.at[i], ds_.at[i], dr.at[i],
                                            device_id=mate, device_id_type=MESH)

    def x_send(i):
        return pltpu.make_async_remote_copy(comb.at[i], xrx.at[i], xs.at[i], xr.at[i],
                                            device_id=peer, device_id_type=MESH)

    def p_send(n):
        return pltpu.make_async_remote_copy(pbuf.at[n], prx.at[n], ps.at[n], pr.at[n],
                                            device_id=mate, device_id_type=MESH)

    for n in range(6):
        w_copy(n).start()

    barrier = pltpu.get_barrier_semaphore()
    for other in (mate, peer):
        pl.semaphore_signal(barrier, inc=1, device_id=other, device_id_type=MESH)

    t = tok[...].astype(F32)
    inv = lax.rsqrt(jnp.sum(t * t, axis=-1, keepdims=True) * (1.0 / DIM) + NORM_EPS)
    for j in range(DIM // HD):
        sl = slice(j * HD, (j + 1) * HD)
        hid[:, sl] = (tok[:, sl].astype(F32) * inv * aux[j:j + 1, :]).astype(BF16)

    lane1 = lax.broadcasted_iota(jnp.int32, (1, HD), 1)
    freq = aux[DIM // HD + 2:DIM // HD + 3, :]

    def angle(b, carry):
        ang[pl.ds(b, 1), :] = freq * pos_s[b].astype(F32)
        return carry

    lax.fori_loop(0, SEQS, angle, 0)
    cosr[...] = jnp.cos(ang[...])
    sinr[...] = jnp.sin(ang[...]) * jnp.where(lane1 < HD // 2, -1.0, 1.0)

    row = lax.broadcasted_iota(jnp.int32, (2 * HALF, ROWS), 0)
    col = lax.broadcasted_iota(jnp.int32, (2 * HALF, ROWS), 1)
    half_of_row = jnp.where(row < HALF, core, 1 - core)
    kv_of_row = half_of_row * 2 + lax.rem(row, HALF) // 8
    colslot[...] = jnp.where(lax.rem(col, KVH) == kv_of_row, col // KVH, 1 << 20)

    qgain = aux[DIM // HD:DIM // HD + 1, :]
    kgain = aux[DIM // HD + 1:DIM // HD + 2, :]

    def norm_rope(x, gain):
        y = x * lax.rsqrt(jnp.mean(x * x, axis=-1, keepdims=True) + NORM_EPS) * gain
        y = y * cosr[...] + pltpu.roll(y, HD // 2, 1) * sinr[...]
        return y.astype(BF16).astype(F32)

    for n in range(6):
        w_copy(n).wait()
        k_copy(n).start()
        v_copy(n).start()
        proj = jnp.dot(hid[...], w_s[n], preferred_element_type=F32).astype(BF16).astype(F32)
        for j in range(WCH // HD):
            x = proj[:, j * HD:(j + 1) * HD]
            if n < 4:
                qmine[pl.ds(n * 4 + j, SEQS, stride=HALF), :] = norm_rope(x, qgain)
            else:
                y = norm_rope(x, kgain) if n == 4 else x
                for c in range(4):
                    rep[n - 4, pl.ds(c * KVH + j, SEQS, stride=4 * KVH), :] = y
        if n == 4:
            pl.semaphore_wait(barrier, 2)
            q_send().start()
    for i in range(6, NBLK):
        k_copy(i).start()
        v_copy(i).start()
    for n in range(4):
        wo_copy(n).start()
    start = me * SLOTS
    lane = lax.broadcasted_iota(jnp.int32, (HALF, HD), 1)
    lrow = lax.broadcasted_iota(jnp.int32, (HALF, HD), 0)
    lane8 = lax.broadcasted_iota(jnp.int32, (BLK, HD), 1)
    q_send().wait()

    def attend(i):
        k_copy(i).wait()
        v_copy(i).wait()
        ob = opart.at[i]
        for pair in range(BLK // 2):
            bs = [i * BLK + 2 * pair + z for z in range(2)]
            qf = [jnp.concatenate([qmine[pl.ds(pl.multiple_of(b * HALF, HALF), HALF), :],
                                   qmate[pl.ds(pl.multiple_of(b * HALF, HALF), HALF), :]], axis=0) for b in bs]
            zero = jnp.zeros((2 * HALF, HD), BF16)
            lhs = jnp.concatenate([jnp.concatenate([qf[0].astype(BF16), zero], axis=1),
                                   jnp.concatenate([zero, qf[1].astype(BF16)], axis=1)], axis=0)
            keys = jnp.concatenate([kv[bs[0]], kv[bs[1]]], axis=1)
            s = lax.dot_general(lhs, keys, (((1,), (1,)), ((), ())), preferred_element_type=F32)
            probs, extra, sums, peaks = [], [], [], []
            for z in range(2):
                b = bs[z]
                rel = pos_s[b] - start
                owner = jnp.logical_and(rel >= 0, rel < SLOTS)
                knew = jnp.concatenate(
                    [jnp.broadcast_to(rep[0, pl.ds(b * 4 * KVH + h, 1), :], (8, HD))
                     for h in (2 * core, 2 * core + 1, 2 - 2 * core, 3 - 2 * core)], axis=0)
                snew = jnp.sum(qf[z] * knew, axis=-1, keepdims=True)
                snew = jnp.where(owner, snew, NEG)
                sm = jnp.where(colslot[...] < rel, s[z * 2 * HALF:(z + 1) * 2 * HALF], NEG)
                peak = jnp.maximum(jnp.max(sm, axis=-1, keepdims=True), snew)
                safe = jnp.where(peak == NEG, 0.0, peak)
                p = jnp.exp2((sm - safe) * EXP_SCALE)
                pn = jnp.exp2((snew - safe) * EXP_SCALE)
                probs.append(p.astype(BF16))
                extra.append(pn.astype(BF16).astype(F32))
                sums.append(jnp.sum(p, axis=-1, keepdims=True) + pn)
                peaks.append(peak)
            values = jnp.concatenate([vv[bs[0]], vv[bs[1]]], axis=1)
            mixed = jnp.dot(jnp.concatenate(probs, axis=0), values, preferred_element_type=F32)
            for z in range(2):
                b = bs[z]
                vnew = jnp.concatenate(
                    [jnp.broadcast_to(rep[1, pl.ds(b * 4 * KVH + h, 1), :], (8, HD))
                     for h in (2 * core, 2 * core + 1, 2 - 2 * core, 3 - 2 * core)], axis=0)
                o = mixed[z * 2 * HALF:(z + 1) * 2 * HALF, z * HD:(z + 1) * HD] + extra[z] * vnew
                bb = 2 * pair + z
                for h in range(2):
                    hs = slice(h * HALF, (h + 1) * HALF)
                    ob[pl.ds(h * PIECE + bb, HALF, stride=BLK), :] = o[hs]
                    st = jnp.where(lane == lrow, peaks[z][hs], jnp.where(lane == lrow + HALF, sums[z][hs], 0.0))
                    ob[pl.ds(h * PIECE + HALF * BLK + bb, 1), :] = jnp.sum(st, axis=0, keepdims=True)

    def combine(i):
        d_send(i).wait_recv()
        s0 = opart[i, pl.ds(HALF * BLK, BLK), :]
        s1 = drx[i, pl.ds(HALF * BLK, BLK), :]
        peak = jnp.maximum(s0, s1)
        safe = jnp.where(peak == NEG, 0.0, peak)
        f0 = jnp.exp2((s0 - safe) * EXP_SCALE)
        f1 = jnp.exp2((s1 - safe) * EXP_SCALE)
        total = f0 * pltpu.roll(s0, HD - HALF, 1) + f1 * pltpu.roll(s1, HD - HALF, 1)
        comb[i, pl.ds(HALF * BLK, BLK), :] = jnp.where(
            lane8 < HALF, peak, jnp.where(lane8 < 2 * HALF, pltpu.roll(total, HALF, 1), 0.0))
        for j in range(HALF):
            rows = pl.ds(j * BLK, BLK)
            comb[i, rows, :] = bcast_col(f0, j) * opart[i, rows, :] + bcast_col(f1, j) * drx[i, rows, :]

    def finish(i):
        x_send(i).wait_recv()
        first = chip == 0

        def ordered(rows):
            mine, other = comb[i, rows, :], xrx[i, rows, :]
            return jnp.where(first, mine, other), jnp.where(first, other, mine)

        s0, s1 = ordered(pl.ds(HALF * BLK, BLK))
        peak = jnp.maximum(s0, s1)
        f0 = jnp.exp2((s0 - peak) * EXP_SCALE)
        f1 = jnp.exp2((s1 - peak) * EXP_SCALE)
        total = f0 * pltpu.roll(s0, HD - HALF, 1) + f1 * pltpu.roll(s1, HD - HALF, 1)
        g0, g1 = f0 / total, f1 / total
        for j in range(HALF):
            a, b = ordered(pl.ds(j * BLK, BLK))
            ofin[pl.ds(pl.multiple_of(i * BLK, BLK), BLK), j * HD:(j + 1) * HD] = bcast_col(g0, j) * a + bcast_col(g1, j) * b

    def step(i, carry):
        @pl.when(i < NBLK)
        def _():
            attend(i)

        @pl.when(jnp.logical_and(i >= 1, i < NBLK + 1))
        def _():
            combine(i - 1)

        @pl.when(i < NBLK)
        def _():
            d_send(i).start()

        @pl.when(i >= 3)
        def _():
            finish(i - 3)

        @pl.when(jnp.logical_and(i >= 1, i < NBLK + 1))
        def _():
            x_send(i - 1).start()

        return carry

    lax.fori_loop(0, NBLK + 3, step, 0)

    lhs = ofin[...].astype(BF16)
    for n in range(4):
        wo_copy(n).wait()
        pbuf[n] = jnp.dot(lhs, w_s[n], preferred_element_type=F32)
        p_send(n).start()
    for n in range(4):
        p_send(n).wait_recv()
        sl = slice(n * WCH, (n + 1) * WCH)
        bout[:, sl] = (tok[:, sl].astype(F32) + (pbuf[n] + prx[n])).astype(BF16)

    def drain(i, carry):
        d_send(i).wait_send()
        x_send(i).wait_send()
        return carry

    lax.fori_loop(0, NBLK, drain, 0)
    for n in range(4):
        p_send(n).wait_send()


def write_kernel(pos_s, kv, vv, rep, bin_, ko, vo, bo, nkv, kva, vva, ksem, vsem):
    start = lax.axis_index('sp') * SLOTS
    slot16 = lax.broadcasted_iota(jnp.int32, (4 * KVH, HD), 0) // KVH

    def put(i):
        for bb in range(BLK):
            b = i * BLK + bb
            rel = pos_s[b] - start

            @pl.when(jnp.logical_and(rel >= 0, rel < SLOTS))
            def _():
                base = pl.multiple_of(rel // 4 * (4 * KVH), 4 * KVH)
                mask = slot16 == lax.rem(rel, 4)
                for z, ref in enumerate((kv, vv)):
                    new = rep[z, pl.ds(b * 4 * KVH, 4 * KVH), :]
                    old = ref[b, pl.ds(base, 4 * KVH), :].astype(F32)
                    ref[b, pl.ds(base, 4 * KVH), :] = jnp.where(mask, new, old).astype(BF16)

    def copies(i):
        r = pl.ds(i * BLK, BLK)
        return (pltpu.make_async_copy(kv.at[r], ko.at[r], ksem.at[i]),
                pltpu.make_async_copy(vv.at[r], vo.at[r], vsem.at[i]))

    for i in range(NBLK + 1):
        if i < NBLK:
            put(i)
        if i > 0:
            for c in copies(i - 1):
                c.start()
    bo[...] = bin_[...]
    for b in range(SEQS):
        nkv[b] = jnp.concatenate([rep[0, pl.ds(b * 4 * KVH, KVH), :], rep[1, pl.ds(b * 4 * KVH, KVH), :]], axis=0).astype(BF16)
    for i in range(NBLK):
        for c in copies(i):
            c.wait()


def solution(mesh):
    cache_spec = P('dp', 'sp', None, None)
    inv_freq = (np.float64(ROPE_THETA) ** (-np.arange(HD // 2) * 2.0 / HD)).astype(np.float32)
    freq2 = np.concatenate([inv_freq, inv_freq])
    vm = pl.BlockSpec(memory_space=pltpu.VMEM)
    hbm = pl.BlockSpec(memory_space=pl.ANY)
    sm = pl.BlockSpec(memory_space=pltpu.SMEM)
    dma = pltpu.SemaphoreType.DMA

    def device_step(tokens, positions, k_cache, v_cache, w_q, w_k, w_v, w_o, attn_norm, q_norm, k_norm):
        aux = jnp.concatenate([attn_norm.astype(F32), q_norm.astype(F32), k_norm.astype(F32), freq2,
                               jnp.zeros((5 * HD,), F32)]).reshape(24, HD)
        in_hbm = lambda x: pltpu.with_memory_space_constraint(x, pltpu.HBM)
        in_vmem = lambda x: pltpu.with_memory_space_constraint(x, pltpu.VMEM)
        rows = (SEQS, ROWS, HD)
        kv, vv, rep, bout = pl.pallas_call(
            attend_kernel,
            out_shape=(pltpu.VMEM(rows, BF16), pltpu.VMEM(rows, BF16),
                       pltpu.VMEM((2, SEQS * 4 * KVH, HD), F32), pltpu.VMEM((SEQS, DIM), BF16)),
            in_specs=[sm, vm, vm] + [hbm] * 6,
            out_specs=(vm, vm, vm, vm),
            scratch_shapes=[
                pltpu.VMEM((6, DIM, WCH), BF16),
                pltpu.VMEM((SEQS, DIM), BF16),
                pltpu.VMEM((SEQS, HD), F32), pltpu.VMEM((SEQS, HD), F32), pltpu.VMEM((SEQS, HD), F32),
                pltpu.VMEM((SEQS * HALF, HD), F32), pltpu.VMEM((SEQS * HALF, HD), F32),
                pltpu.VMEM((2 * HALF, ROWS), jnp.int32),
                pltpu.VMEM((NBLK, 2 * PIECE, HD), F32),
                pltpu.VMEM((NBLK, PIECE, HD), F32), pltpu.VMEM((NBLK, PIECE, HD), F32), pltpu.VMEM((NBLK, PIECE, HD), F32),
                pltpu.VMEM((SEQS, HALF * HD), F32),
                pltpu.VMEM((4, SEQS, WCH), F32), pltpu.VMEM((4, SEQS, WCH), F32),
                dma((6,)), dma((NBLK,)), dma((NBLK,)), dma((4,)), dma, dma,
                dma((NBLK,)), dma((NBLK,)), dma((NBLK,)), dma((NBLK,)), dma((4,)), dma((4,)),
            ],
            compiler_params=pltpu.CompilerParams(collective_id=0, has_side_effects=True, vmem_limit_bytes=VMEM_LIMIT),
            name='attend',
        )(positions, tokens, aux, in_hbm(w_q), in_hbm(w_k), in_hbm(w_v), in_hbm(w_o),
          in_hbm(k_cache.reshape(rows)), in_hbm(v_cache.reshape(rows)))
        k_out, v_out, block_out, new_kv, _, _ = pl.pallas_call(
            write_kernel,
            out_shape=(pltpu.HBM(rows, BF16), pltpu.HBM(rows, BF16), jax.ShapeDtypeStruct((SEQS, DIM), BF16),
                       jax.ShapeDtypeStruct((SEQS, 2 * KVH, HD), BF16), pltpu.VMEM(rows, BF16), pltpu.VMEM(rows, BF16)),
            in_specs=[sm, vm, vm, vm, vm],
            out_specs=(hbm, hbm, vm, vm, vm, vm),
            input_output_aliases={1: 4, 2: 5},
            scratch_shapes=[dma((NBLK,)), dma((NBLK,))],
            compiler_params=pltpu.CompilerParams(vmem_limit_bytes=VMEM_LIMIT),
            name='write',
        )(positions, in_vmem(kv), in_vmem(vv), in_vmem(rep), in_vmem(bout))
        return block_out, k_out.reshape(k_cache.shape), v_out.reshape(v_cache.shape), new_kv.reshape(SEQS, 2, KVH, HD)

    return jax.shard_map(device_step, mesh=mesh, in_specs=(P('dp', None), P('dp'), cache_spec, cache_spec, P(), P(), P(), P(), P(), P(), P()), out_specs=(P('dp', None), cache_spec, cache_spec, P('dp', None, None, None)), check_vma=False)
```

time: 162 us -> 52.3 us (0.32)
  Pallas kernels: 0 us -> 48.2 us
  waiting for transfers between devices: 44.2 us -> 0 us
  matrix products: 39.7 us -> 0 us
  other arithmetic: 37.2 us -> 2.01 us
  blocking collectives: 15 us -> 0 us
  between operations: 14.3 us -> 0.65 us
  local copies, waits for them, and re-layouts: 10.6 us -> 1.26 us
    pallas_call x0 -> x2, Pallas kernels: none -> 48.2 us  [the longest x1 35.6 us: device_step(): pl.pallas_call(attend_kernel, out_shape=(pltpu.VMEM(rows, BF16), pltpu.VM...]
    psum x1 -> x0, waiting for transfers between devices: 44.2 us -> none  [device_step(): summed = lax.psum(packed, 'sp')]
    dot_general x6 -> x0, matrix products: 39.7 us -> none  [the longest x1 9.64 us: device_step(): jnp.dot(attn_out, w_o, preferred_element_type=jnp.float32)]
    select_n x1 -> x0, other arithmetic: 24.4 us -> none  [local_attention(): v_upd = jnp.where(write_mask, v_new[:, None], v_loc)]
    pmax x1 -> x0, blocking collectives: 15 us -> none  [device_step(): global_peak = lax.pmax(local_peak, 'sp')]
    unnamed x31 -> x3, local copies, waits for them, and re-layouts: 6.15 us -> 1.26 us
    convert_element_type x5 -> x0, other arithmetic: 4.38 us -> none  [the longest x3 2.16 us: rms_scale(): gain.astype(jnp.float32)]
    broadcast_in_dim x2 -> x0, local copies, waits for them, and re-layouts: 2.48 us -> none  [the longest x1 2.45 us: device_step(): (local_sum * factor)[..., None]]
  transfers between devices with their start and end apart: 1 -> 0, of which waited for: 1 -> 0; matrix products, arithmetic and copies ran while one was open for 0% -> 0% of each run, Pallas kernels for 0% -> 0%
where the time goes in v1:
time: 52.3 us; the launch traced here: 52.1 us
  Pallas kernels  48.2 us (92%)
  other arithmetic  2.01 us (4%)
  local copies, waits for them, and re-layouts  1.26 us (2%)
  between operations  0.65 us (1%)
    pallas_call x1, Pallas kernels, device_step(): pl.pallas_call(attend_kernel, out_shape=(pltpu.VMEM(rows, BF16), pltpu.VM...  35.6 us
    pallas_call x1, Pallas kernels, device_step(): pl.pallas_call(write_kernel, out_shape=(pltpu.HBM(rows, BF16), pltpu.HBM(...  12.6 us
    unnamed x3, other arithmetic  2.01 us
    unnamed x3, local copies, waits for them, and re-layouts  1.26 us

profile of v1, /device:TPU:0, one launch (start us, length us, event | category | flops | bytes accessed | tf_op | source)
XLA Modules:
  0.0 52.1 jit_solution(17230031049843288134)
XLA Ops:
  0.6 0.7 %convert_dynamic-update-slice_fusion = f32[3072]{0:T(1024)S(1)} fusion(bf16[2048]{0:T(1024)(128)(2,1)} %param.20), kind=kLoop, calls=%fused_computation | loop fusion | flops 2047 | bytes 12288
  1.3 0.7 %constant_dynamic-update-slice_fusion.3 = f32[3072]{0:T(1024)S(1)} fusion(f32[3072]{0:T(1024)S(1)} %convert_dynamic-update-slice_fusion, bf16[128]{0:T(256)(128)(2,1)} %param.21), kind=kLoop, calls=%fused_computation.4 | loop fusion | flops 128 | bytes 768
  2.0 0.7 %constant_dynamic-update-slice_fusion.2 = f32[3072]{0:T(1024)S(1)} fusion(f32[3072]{0:T(1024)S(1)} %constant_dynamic-update-slice_fusion.3, bf16[128]{0:T(256)(128)(2,1)} %param.22), kind=kLoop, calls=%fused_computation.3 | loop fusion | flops 128 | bytes 768
  2.6 0.7 %constant_dynamic-update-slice_fusion.1 = f32[3072]{0:T(1024)S(1)} fusion(f32[3072]{0:T(1024)S(1)} %constant_dynamic-update-slice_fusion.2, f32[128]{0:T(128)} %constant.4.clone), kind=kLoop, calls=%fused_computation.2 | loop fusion | bytes 1024
  3.3 0.0 copy-start
  3.3 0.6 %copy-done = f32[3072]{0:T(1024)} copy-done((f32[3072]{0:T(1024)}, f32[3072]{0:T(1024)S(1)}, u32[]{:S(2)}) %copy-start) | copy-done | bytes 12312
  3.9 35.6 %attend.1 = (bf16[64,1024,128]{2,1,0:T(8,128)(2,1)S(1)}, bf16[64,1024,128]{2,1,0:T(8,128)(2,1)S(1)}, f32[2,1024,128]{2,1,0:T(8,128)S(1)}, bf16[64,2048]{1,0:T(8,128)(2,1)S(1)}) custom-call(s32[64]{0:T(128)} %pos_s.3, bf16[64,2048]{1,0:T(8,128)(2,1)} %tok.1, f32[24,128]{1,0:T(8,128)} %bitcast.8, bf16[2048,4096]{1,0:T(8,128)(2,1)} %wq.1, ...), custom_call_target="tpu_custom_call" | custom-call | tf_op jit(solution)/shard_map/attend/pallas_call | solution.py:321
  39.5 12.6 %write.1 = (bf16[64,1024,128]{2,1,0:T(8,128)(2,1)}, bf16[64,1024,128]{2,1,0:T(8,128)(2,1)}, bf16[64,2048]{1,0:T(8,128)(2,1)}, bf16[64,8,128]{2,1,0:T(8,128)(2,1)...) custom-call(s32[64]{0:T(128)} %pos_s.3, ...), custom_call_target="tpu_custom_call", output_to_operand_aliasing={{4}: (1, {}), {5}: (2, {})} | custom-call | tf_op jit(solution)/shard_map/write/pallas_call | solution.py:344
  (1 shorter events, 0.0 us)
Async XLA Ops:
  3.3 0.6 %copy-start = (f32[3072]{0:T(1024)}, f32[3072]{0:T(1024)S(1)}, u32[]{:S(2)}) copy-start(f32[3072]{0:T(1024)S(1)} %constant_dynamic-update-slice_fusion) | copy-start | bytes 36868

commit v2 on v1

--- a/solution.py
+++ b/solution.py
@@ -23,6 +23,7 @@
 ROWS = SLOTS * KVH
 BLK = 8
 NBLK = SEQS // BLK
+LAG = 6
 WCH = 512
 PIECE = (HALF + 1) * BLK
 VMEM_LIMIT = 26 * 2**20
@@ -34,9 +35,9 @@
     return jnp.broadcast_to(tile[:, col:col + 1], (tile.shape[0], HD))
 
 
-def attend_kernel(pos_s, tok, aux, wq, wk, wv, wo, kc, vc,
+def attend_kernel(pos_h, tok_h, an_h, qn_h, kn_h, freq_h, wq, wk, wv, wo, kc, vc,
                   kv, vv, rep, bout,
-                  w_s, hid, ang, cosr, sinr, qmine, qmate, colslot, opart, drx, comb, xrx, ofin, pbuf, prx,
+                  pos_s, tok, an, qn, kn, freq, insem, w_s, hid, ang, cosr, sinr, qmine, qmate, colslot, opart, drx, comb, xrx, ofin, pbuf, prx,
                   wsem, ksem, vsem, wosem, qs, qr, ds_, dr, xs, xr, ps, pr):
     me = lax.axis_index('sp')
     core = lax.rem(me, 2)
@@ -76,6 +77,10 @@
         return pltpu.make_async_remote_copy(pbuf.at[n], prx.at[n], ps.at[n], pr.at[n],
                                             device_id=mate, device_id_type=MESH)
 
+    small = [pltpu.make_async_copy(a, b, insem.at[z]) for z, (a, b) in enumerate(
+        ((tok_h, tok), (pos_h, pos_s), (an_h, an), (qn_h, qn), (kn_h, kn), (freq_h, freq)))]
+    for c in small:
+        c.start()
     for n in range(6):
         w_copy(n).start()
 
@@ -83,17 +88,20 @@
     for other in (mate, peer):
         pl.semaphore_signal(barrier, inc=1, device_id=other, device_id_type=MESH)
 
+    for c in small:
+        c.wait()
+
     t = tok[...].astype(F32)
     inv = lax.rsqrt(jnp.sum(t * t, axis=-1, keepdims=True) * (1.0 / DIM) + NORM_EPS)
+    gains = an[...].astype(F32)
     for j in range(DIM // HD):
         sl = slice(j * HD, (j + 1) * HD)
-        hid[:, sl] = (tok[:, sl].astype(F32) * inv * aux[j:j + 1, :]).astype(BF16)
+        hid[:, sl] = (tok[:, sl].astype(F32) * inv * gains[j:j + 1, :]).astype(BF16)
 
     lane1 = lax.broadcasted_iota(jnp.int32, (1, HD), 1)
-    freq = aux[DIM // HD + 2:DIM // HD + 3, :]
 
     def angle(b, carry):
-        ang[pl.ds(b, 1), :] = freq * pos_s[b].astype(F32)
+        ang[pl.ds(b, 1), :] = freq[...] * pos_s[b].astype(F32)
         return carry
 
     lax.fori_loop(0, SEQS, angle, 0)
@@ -106,8 +114,8 @@
     kv_of_row = half_of_row * 2 + lax.rem(row, HALF) // 8
     colslot[...] = jnp.where(lax.rem(col, KVH) == kv_of_row, col // KVH, 1 << 20)
 
-    qgain = aux[DIM // HD:DIM // HD + 1, :]
-    kgain = aux[DIM // HD + 1:DIM // HD + 2, :]
+    qgain = qn[...].astype(F32)
+    kgain = kn[...].astype(F32)
 
     def norm_rope(x, gain):
         y = x * lax.rsqrt(jnp.mean(x * x, axis=-1, keepdims=True) + NORM_EPS) * gain
@@ -127,7 +135,7 @@
                 y = norm_rope(x, kgain) if n == 4 else x
                 for c in range(4):
                     rep[n - 4, pl.ds(c * KVH + j, SEQS, stride=4 * KVH), :] = y
-        if n == 4:
+        if n == 3:
             pl.semaphore_wait(barrier, 2)
             q_send().start()
     for i in range(6, NBLK):
@@ -234,9 +242,9 @@
         def _():
             d_send(i).start()
 
-        @pl.when(i >= 3)
-        def _():
-            finish(i - 3)
+        @pl.when(i >= LAG)
+        def _():
+            finish(i - LAG)
 
         @pl.when(jnp.logical_and(i >= 1, i < NBLK + 1))
         def _():
@@ -244,7 +252,7 @@
 
         return carry
 
-    lax.fori_loop(0, NBLK + 3, step, 0)
+    lax.fori_loop(0, NBLK + LAG, step, 0)
 
     lhs = ofin[...].astype(BF16)
     for n in range(4):
@@ -266,11 +274,26 @@
         p_send(n).wait_send()
 
 
-def write_kernel(pos_s, kv, vv, rep, bin_, ko, vo, bo, nkv, kva, vva, ksem, vsem):
+def write_kernel(pos_h, kv, vv, rep, bin_, ko, vo, bo, nkv, kva, vva, pos_s, nkv_s, patch, ksem, vsem, psem, osem):
     start = lax.axis_index('sp') * SLOTS
     slot16 = lax.broadcasted_iota(jnp.int32, (4 * KVH, HD), 0) // KVH
 
-    def put(i):
+    def copies(i):
+        r = pl.ds(i * BLK, BLK)
+        return (pltpu.make_async_copy(kv.at[r], ko.at[r], ksem.at[i]),
+                pltpu.make_async_copy(vv.at[r], vo.at[r], vsem.at[i]))
+
+    pos_copy = pltpu.make_async_copy(pos_h, pos_s, osem.at[0])
+    pos_copy.start()
+    out_copy = pltpu.make_async_copy(bin_, bo, osem.at[1])
+    out_copy.start()
+    for c in copies(0):
+        c.start()
+    for b in range(SEQS):
+        nkv_s[b] = jnp.concatenate([rep[0, pl.ds(b * 4 * KVH, KVH), :], rep[1, pl.ds(b * 4 * KVH, KVH), :]], axis=0).astype(BF16)
+    pos_copy.wait()
+
+    def each(i, do):
         for bb in range(BLK):
             b = i * BLK + bb
             rel = pos_s[b] - start
@@ -279,26 +302,40 @@
             def _():
                 base = pl.multiple_of(rel // 4 * (4 * KVH), 4 * KVH)
                 mask = slot16 == lax.rem(rel, 4)
-                for z, ref in enumerate((kv, vv)):
-                    new = rep[z, pl.ds(b * 4 * KVH, 4 * KVH), :]
-                    old = ref[b, pl.ds(base, 4 * KVH), :].astype(F32)
-                    ref[b, pl.ds(base, 4 * KVH), :] = jnp.where(mask, new, old).astype(BF16)
-
-    def copies(i):
-        r = pl.ds(i * BLK, BLK)
-        return (pltpu.make_async_copy(kv.at[r], ko.at[r], ksem.at[i]),
-                pltpu.make_async_copy(vv.at[r], vo.at[r], vsem.at[i]))
-
-    for i in range(NBLK + 1):
-        if i < NBLK:
-            put(i)
-        if i > 0:
+                for z, (ref, out) in enumerate(((kv, ko), (vv, vo))):
+                    do(b, z, base, mask, ref, out)
+
+    def merged(b, z, base, mask, ref):
+        new = rep[z, pl.ds(b * 4 * KVH, 4 * KVH), :]
+        old = ref[b, pl.ds(base, 4 * KVH), :].astype(F32)
+        return jnp.where(mask, new, old).astype(BF16)
+
+    def put(b, z, base, mask, ref, out):
+        ref[b, pl.ds(base, 4 * KVH), :] = merged(b, z, base, mask, ref)
+
+    def stage(b, z, base, mask, ref, out):
+        patch[z, b] = merged(b, z, base, mask, ref)
+
+    def patch_copy(b, z, base, out):
+        return pltpu.make_async_copy(patch.at[z, b], out.at[b, pl.ds(base, 4 * KVH)], psem.at[z, b])
+
+    for i in range(1, NBLK):
+        each(i, put)
+        if i > 1:
             for c in copies(i - 1):
                 c.start()
-    bo[...] = bin_[...]
-    for b in range(SEQS):
-        nkv[b] = jnp.concatenate([rep[0, pl.ds(b * 4 * KVH, KVH), :], rep[1, pl.ds(b * 4 * KVH, KVH), :]], axis=0).astype(BF16)
-    for i in range(NBLK):
+    nkv_copy = pltpu.make_async_copy(nkv_s, nkv, osem.at[2])
+    nkv_copy.start()
+    each(0, stage)
+    for c in copies(NBLK - 1):
+        c.start()
+    for c in copies(0):
+        c.wait()
+    each(0, lambda b, z, base, mask, ref, out: patch_copy(b, z, base, out).start())
+    out_copy.wait()
+    nkv_copy.wait()
+    each(0, lambda b, z, base, mask, ref, out: patch_copy(b, z, base, out).wait())
+    for i in range(1, NBLK):
         for c in copies(i):
             c.wait()
 
@@ -309,12 +346,9 @@
     freq2 = np.concatenate([inv_freq, inv_freq])
     vm = pl.BlockSpec(memory_space=pltpu.VMEM)
     hbm = pl.BlockSpec(memory_space=pl.ANY)
-    sm = pl.BlockSpec(memory_space=pltpu.SMEM)
     dma = pltpu.SemaphoreType.DMA
 
     def device_step(tokens, positions, k_cache, v_cache, w_q, w_k, w_v, w_o, attn_norm, q_norm, k_norm):
-        aux = jnp.concatenate([attn_norm.astype(F32), q_norm.astype(F32), k_norm.astype(F32), freq2,
-                               jnp.zeros((5 * HD,), F32)]).reshape(24, HD)
         in_hbm = lambda x: pltpu.with_memory_space_constraint(x, pltpu.HBM)
         in_vmem = lambda x: pltpu.with_memory_space_constraint(x, pltpu.VMEM)
         rows = (SEQS, ROWS, HD)
@@ -322,9 +356,11 @@
             attend_kernel,
             out_shape=(pltpu.VMEM(rows, BF16), pltpu.VMEM(rows, BF16),
                        pltpu.VMEM((2, SEQS * 4 * KVH, HD), F32), pltpu.VMEM((SEQS, DIM), BF16)),
-            in_specs=[sm, vm, vm] + [hbm] * 6,
+            in_specs=[hbm] * 12,
             out_specs=(vm, vm, vm, vm),
             scratch_shapes=[
+                pltpu.SMEM((SEQS,), jnp.int32), pltpu.VMEM((SEQS, DIM), BF16), pltpu.VMEM((DIM // HD, HD), BF16),
+                pltpu.VMEM((1, HD), BF16), pltpu.VMEM((1, HD), BF16), pltpu.VMEM((1, HD), F32), dma((6,)),
                 pltpu.VMEM((6, DIM, WCH), BF16),
                 pltpu.VMEM((SEQS, DIM), BF16),
                 pltpu.VMEM((SEQS, HD), F32), pltpu.VMEM((SEQS, HD), F32), pltpu.VMEM((SEQS, HD), F32),
@@ -339,19 +375,22 @@
             ],
             compiler_params=pltpu.CompilerParams(collective_id=0, has_side_effects=True, vmem_limit_bytes=VMEM_LIMIT),
             name='attend',
-        )(positions, tokens, aux, in_hbm(w_q), in_hbm(w_k), in_hbm(w_v), in_hbm(w_o),
+        )(in_hbm(positions), in_hbm(tokens), in_hbm(attn_norm.reshape(DIM // HD, HD)), in_hbm(q_norm.reshape(1, HD)),
+          in_hbm(k_norm.reshape(1, HD)), in_hbm(jnp.asarray(freq2).reshape(1, HD)), in_hbm(w_q), in_hbm(w_k), in_hbm(w_v), in_hbm(w_o),
           in_hbm(k_cache.reshape(rows)), in_hbm(v_cache.reshape(rows)))
         k_out, v_out, block_out, new_kv, _, _ = pl.pallas_call(
             write_kernel,
-            out_shape=(pltpu.HBM(rows, BF16), pltpu.HBM(rows, BF16), jax.ShapeDtypeStruct((SEQS, DIM), BF16),
-                       jax.ShapeDtypeStruct((SEQS, 2 * KVH, HD), BF16), pltpu.VMEM(rows, BF16), pltpu.VMEM(rows, BF16)),
-            in_specs=[sm, vm, vm, vm, vm],
-            out_specs=(hbm, hbm, vm, vm, vm, vm),
+            out_shape=(pltpu.HBM(rows, BF16), pltpu.HBM(rows, BF16), pltpu.HBM((SEQS, DIM), BF16),
+                       pltpu.HBM((SEQS, 2 * KVH, HD), BF16), pltpu.VMEM(rows, BF16), pltpu.VMEM(rows, BF16)),
+            in_specs=[hbm, vm, vm, vm, vm],
+            out_specs=(hbm, hbm, hbm, hbm, vm, vm),
             input_output_aliases={1: 4, 2: 5},
-            scratch_shapes=[dma((NBLK,)), dma((NBLK,))],
+            scratch_shapes=[pltpu.SMEM((SEQS,), jnp.int32), pltpu.VMEM((SEQS, 2 * KVH, HD), BF16),
+                            pltpu.VMEM((2, BLK, 4 * KVH, HD), BF16),
+                            dma((NBLK,)), dma((NBLK,)), dma((2, BLK)), dma((3,))],
             compiler_params=pltpu.CompilerParams(vmem_limit_bytes=VMEM_LIMIT),
             name='write',
-        )(positions, in_vmem(kv), in_vmem(vv), in_vmem(rep), in_vmem(bout))
+        )(in_hbm(positions), in_vmem(kv), in_vmem(vv), in_vmem(rep), in_vmem(bout))
         return block_out, k_out.reshape(k_cache.shape), v_out.reshape(v_cache.shape), new_kv.reshape(SEQS, 2, KVH, HD)
 
     return jax.shard_map(device_step, mesh=mesh, in_specs=(P('dp', None), P('dp'), cache_spec, cache_spec, P(), P(), P(), P(), P(), P(), P()), out_specs=(P('dp', None), cache_spec, cache_spec, P('dp', None, None, None)), check_vma=False)

time: 52.3 us -> 48.5 us (0.927)
  other arithmetic: 2.01 us -> 0 us
  local copies, waits for them, and re-layouts: 1.26 us -> 0 us
    unnamed x3 -> x0, other arithmetic: 2.01 us -> none
    pallas_call x1, Pallas kernels: 12.6 us -> 11.3 us  [device_step(): pl.pallas_call(write_kernel, out_shape=(pltpu.HBM(rows, BF16), pltpu.HBM(...]
    unnamed x3 -> x0, local copies, waits for them, and re-layouts: 1.26 us -> none
    pallas_call x1, Pallas kernels: 35.6 us -> 36.4 us  [device_step(): pl.pallas_call(attend_kernel, out_shape=(pltpu.VMEM(rows, BF16), pltpu.VM...]
where the time goes in v2:
time: 48.5 us; the launch traced here: 48.4 us
  Pallas kernels  47.7 us (98%)
  between operations  0.64 us (1%)
    pallas_call x1, Pallas kernels, device_step(): pl.pallas_call(attend_kernel, out_shape=(pltpu.VMEM(rows, BF16), pltpu.VM...  36.4 us
    pallas_call x1, Pallas kernels, device_step(): pl.pallas_call(write_kernel, out_shape=(pltpu.HBM(rows, BF16), pltpu.HBM(...  11.3 us

profile of v2, /device:TPU:0, one launch (start us, length us, event | category | flops | bytes accessed | tf_op | source)
XLA Modules:
  0.0 48.4 jit_solution(17635894386587781528)
XLA Ops:
  0.6 36.4 %attend.1 = (bf16[64,1024,128]{2,1,0:T(8,128)(2,1)S(1)}, bf16[64,1024,128]{2,1,0:T(8,128)(2,1)S(1)}, f32[2,1024,128]{2,1,0:T(8,128)S(1)}, bf16[64,2048]{1,0:T(8,128)(2,1)S(1)}) custom-call(s32[64]{0:T(128)} %pos_h.3, bf16[64,2048]{1,0:T(8,128)(2,1)} %tok_h.1, bf16[16,128]{1,0:T(8,128)(2,1)} %bitcast.10, bf16[1,128]{1,0:T(2,128)(2,1)} %bitcast.11, ...), custom_call_target="tpu_custom_call" | custom-call | tf_op jit(solution)/shard_map/attend/pallas_call | solution.py:355
  37.0 11.3 %write.1 = (bf16[64,1024,128]{2,1,0:T(8,128)(2,1)}, bf16[64,1024,128]{2,1,0:T(8,128)(2,1)}, bf16[64,2048]{1,0:T(8,128)(2,1)}, bf16[64,8,128]{2,1,0:T(8,128)(2,1)...) custom-call(s32[64]{0:T(128)} %pos_h.3, ...), custom_call_target="tpu_custom_call", output_to_operand_aliasing={{4}: (1, {}), {5}: (2, {})} | custom-call | tf_op jit(solution)/shard_map/write/pallas_call | solution.py:381

commit v3 on v2

--- a/solution.py
+++ b/solution.py
@@ -23,6 +23,7 @@
 ROWS = SLOTS * KVH
 BLK = 8
 NBLK = SEQS // BLK
+AHEAD = 2
 LAG = 6
 WCH = 512
 PIECE = (HALF + 1) * BLK
@@ -81,7 +82,7 @@
         ((tok_h, tok), (pos_h, pos_s), (an_h, an), (qn_h, qn), (kn_h, kn), (freq_h, freq)))]
     for c in small:
         c.start()
-    for n in range(6):
+    for n in range(AHEAD):
         w_copy(n).start()
 
     barrier = pltpu.get_barrier_semaphore()
@@ -124,8 +125,11 @@
 
     for n in range(6):
         w_copy(n).wait()
-        k_copy(n).start()
-        v_copy(n).start()
+        if n + AHEAD < 6:
+            w_copy(n + AHEAD).start()
+        else:
+            k_copy(n + AHEAD - 6).start()
+            v_copy(n + AHEAD - 6).start()
         proj = jnp.dot(hid[...], w_s[n], preferred_element_type=F32).astype(BF16).astype(F32)
         for j in range(WCH // HD):
             x = proj[:, j * HD:(j + 1) * HD]
@@ -138,11 +142,6 @@
         if n == 3:
             pl.semaphore_wait(barrier, 2)
             q_send().start()
-    for i in range(6, NBLK):
-        k_copy(i).start()
-        v_copy(i).start()
-    for n in range(4):
-        wo_copy(n).start()
     start = me * SLOTS
     lane = lax.broadcasted_iota(jnp.int32, (HALF, HD), 1)
     lrow = lax.broadcasted_iota(jnp.int32, (HALF, HD), 0)
@@ -152,6 +151,17 @@
     def attend(i):
         k_copy(i).wait()
         v_copy(i).wait()
+
+        @pl.when(i + AHEAD < NBLK)
+        def _():
+            k_copy(i + AHEAD).start()
+            v_copy(i + AHEAD).start()
+
+        @pl.when(i + AHEAD == NBLK)
+        def _():
+            for n in range(4):
+                wo_copy(n).start()
+
         ob = opart.at[i]
         for pair in range(BLK // 2):
             bs = [i * BLK + 2 * pair + z for z in range(2)]

time: 48.5 us -> 47.2 us (0.973)
  Pallas kernels: 47.7 us -> 46.4 us
    pallas_call x1, Pallas kernels: 36.4 us -> 35.1 us  [device_step(): pl.pallas_call(attend_kernel, out_shape=(pltpu.VMEM(rows, BF16), pltpu.VM...]
where the time goes in v3:
time: 47.2 us; the launch traced here: 47.1 us
  Pallas kernels  46.4 us (98%)
  between operations  0.64 us (1%)
    pallas_call x1, Pallas kernels, device_step(): pl.pallas_call(attend_kernel, out_shape=(pltpu.VMEM(rows, BF16), pltpu.VM...  35.1 us
    pallas_call x1, Pallas kernels, device_step(): pl.pallas_call(write_kernel, out_shape=(pltpu.HBM(rows, BF16), pltpu.HBM(...  11.3 us

profile of v3, /device:TPU:0, one launch (start us, length us, event | category | flops | bytes accessed | tf_op | source)
XLA Modules:
  0.0 47.1 jit_solution(15976359100861776650)
XLA Ops:
  0.6 35.1 %attend.1 = (bf16[64,1024,128]{2,1,0:T(8,128)(2,1)S(1)}, bf16[64,1024,128]{2,1,0:T(8,128)(2,1)S(1)}, f32[2,1024,128]{2,1,0:T(8,128)S(1)}, bf16[64,2048]{1,0:T(8,128)(2,1)S(1)}) custom-call(s32[64]{0:T(128)} %pos_h.3, bf16[64,2048]{1,0:T(8,128)(2,1)} %tok_h.1, bf16[16,128]{1,0:T(8,128)(2,1)} %bitcast.10, bf16[1,128]{1,0:T(2,128)(2,1)} %bitcast.11, ...), custom_call_target="tpu_custom_call" | custom-call | tf_op jit(solution)/shard_map/attend/pallas_call | solution.py:365
  35.7 11.3 %write.1 = (bf16[64,1024,128]{2,1,0:T(8,128)(2,1)}, bf16[64,1024,128]{2,1,0:T(8,128)(2,1)}, bf16[64,2048]{1,0:T(8,128)(2,1)}, bf16[64,8,128]{2,1,0:T(8,128)(2,1)...) custom-call(s32[64]{0:T(128)} %pos_h.3, ...), custom_call_target="tpu_custom_call", output_to_operand_aliasing={{4}: (1, {}), {5}: (2, {})} | custom-call | tf_op jit(solution)/shard_map/write/pallas_call | solution.py:391

commit v4 on v3

--- a/solution.py
+++ b/solution.py
@@ -24,7 +24,7 @@
 BLK = 8
 NBLK = SEQS // BLK
 AHEAD = 2
-LAG = 6
+LAG = 2
 WCH = 512
 PIECE = (HALF + 1) * BLK
 VMEM_LIMIT = 26 * 2**20
@@ -38,7 +38,7 @@
 
 def attend_kernel(pos_h, tok_h, an_h, qn_h, kn_h, freq_h, wq, wk, wv, wo, kc, vc,
                   kv, vv, rep, bout,
-                  pos_s, tok, an, qn, kn, freq, insem, w_s, hid, ang, cosr, sinr, qmine, qmate, colslot, opart, drx, comb, xrx, ofin, pbuf, prx,
+                  pos_s, tok, an, qn, kn, freq, insem, w_s, hid, ang, cosr, sinr, qmine, qmate, colslot, opart, drx, comb, xrx, ofin, pbuf, prx, sc, pr_s,
                   wsem, ksem, vsem, wosem, qs, qr, ds_, dr, xs, xr, ps, pr):
     me = lax.axis_index('sp')
     core = lax.rem(me, 2)
@@ -149,65 +149,62 @@
     q_send().wait()
 
     def attend(i):
-        k_copy(i).wait()
-        v_copy(i).wait()
-
-        @pl.when(i + AHEAD < NBLK)
-        def _():
-            k_copy(i + AHEAD).start()
-            v_copy(i + AHEAD).start()
-
-        @pl.when(i + AHEAD == NBLK)
-        def _():
-            for n in range(4):
-                wo_copy(n).start()
-
         ob = opart.at[i]
-        for pair in range(BLK // 2):
+        def load_q(pair):
             bs = [i * BLK + 2 * pair + z for z in range(2)]
-            qf = [jnp.concatenate([qmine[pl.ds(pl.multiple_of(b * HALF, HALF), HALF), :],
-                                   qmate[pl.ds(pl.multiple_of(b * HALF, HALF), HALF), :]], axis=0) for b in bs]
+            return bs, [jnp.concatenate([qmine[pl.ds(pl.multiple_of(b * HALF, HALF), HALF), :],
+                                         qmate[pl.ds(pl.multiple_of(b * HALF, HALF), HALF), :]], axis=0) for b in bs]
+
+        def new_rows(z, b):
+            return jnp.concatenate([jnp.broadcast_to(rep[z, pl.ds(b * 4 * KVH + h, 1), :], (8, HD))
+                                    for h in (2 * core, 2 * core + 1, 2 - 2 * core, 3 - 2 * core)], axis=0)
+
+        def scores(pair):
+            bs, qf = load_q(pair)
             zero = jnp.zeros((2 * HALF, HD), BF16)
             lhs = jnp.concatenate([jnp.concatenate([qf[0].astype(BF16), zero], axis=1),
                                    jnp.concatenate([zero, qf[1].astype(BF16)], axis=1)], axis=0)
             keys = jnp.concatenate([kv[bs[0]], kv[bs[1]]], axis=1)
-            s = lax.dot_general(lhs, keys, (((1,), (1,)), ((), ())), preferred_element_type=F32)
-            probs, extra, sums, peaks = [], [], [], []
+            sc[pair % 2] = lax.dot_general(lhs, keys, (((1,), (1,)), ((), ())), preferred_element_type=F32)
+
+        def soft(pair):
+            bs, qf = load_q(pair)
+            out = []
             for z in range(2):
                 b = bs[z]
                 rel = pos_s[b] - start
                 owner = jnp.logical_and(rel >= 0, rel < SLOTS)
-                knew = jnp.concatenate(
-                    [jnp.broadcast_to(rep[0, pl.ds(b * 4 * KVH + h, 1), :], (8, HD))
-                     for h in (2 * core, 2 * core + 1, 2 - 2 * core, 3 - 2 * core)], axis=0)
-                snew = jnp.sum(qf[z] * knew, axis=-1, keepdims=True)
-                snew = jnp.where(owner, snew, NEG)
-                sm = jnp.where(colslot[...] < rel, s[z * 2 * HALF:(z + 1) * 2 * HALF], NEG)
+                snew = jnp.where(owner, jnp.sum(qf[z] * new_rows(0, b), axis=-1, keepdims=True), NEG)
+                sm = jnp.where(colslot[...] < rel, sc[pair % 2, z * 2 * HALF:(z + 1) * 2 * HALF], NEG)
                 peak = jnp.maximum(jnp.max(sm, axis=-1, keepdims=True), snew)
                 safe = jnp.where(peak == NEG, 0.0, peak)
                 p = jnp.exp2((sm - safe) * EXP_SCALE)
                 pn = jnp.exp2((snew - safe) * EXP_SCALE)
-                probs.append(p.astype(BF16))
-                extra.append(pn.astype(BF16).astype(F32))
-                sums.append(jnp.sum(p, axis=-1, keepdims=True) + pn)
-                peaks.append(peak)
+                pr_s[pair % 2, z * 2 * HALF:(z + 1) * 2 * HALF, :] = p.astype(BF16)
+                out.append((pn.astype(BF16).astype(F32), jnp.sum(p, axis=-1, keepdims=True) + pn, peak))
+            return out
+
+        def mix(pair, st3):
+            bs = [i * BLK + 2 * pair + z for z in range(2)]
             values = jnp.concatenate([vv[bs[0]], vv[bs[1]]], axis=1)
-            mixed = jnp.dot(jnp.concatenate(probs, axis=0), values, preferred_element_type=F32)
+            mixed = jnp.dot(pr_s[pair % 2], values, preferred_element_type=F32)
             for z in range(2):
-                b = bs[z]
-                vnew = jnp.concatenate(
-                    [jnp.broadcast_to(rep[1, pl.ds(b * 4 * KVH + h, 1), :], (8, HD))
-                     for h in (2 * core, 2 * core + 1, 2 - 2 * core, 3 - 2 * core)], axis=0)
-                o = mixed[z * 2 * HALF:(z + 1) * 2 * HALF, z * HD:(z + 1) * HD] + extra[z] * vnew
+                extra, total, peak = st3[z]
+                o = mixed[z * 2 * HALF:(z + 1) * 2 * HALF, z * HD:(z + 1) * HD] + extra * new_rows(1, bs[z])
                 bb = 2 * pair + z
                 for h in range(2):
                     hs = slice(h * HALF, (h + 1) * HALF)
                     ob[pl.ds(h * PIECE + bb, HALF, stride=BLK), :] = o[hs]
-                    st = jnp.where(lane == lrow, peaks[z][hs], jnp.where(lane == lrow + HALF, sums[z][hs], 0.0))
+                    st = jnp.where(lane == lrow, peak[hs], jnp.where(lane == lrow + HALF, total[hs], 0.0))
                     ob[pl.ds(h * PIECE + HALF * BLK + bb, 1), :] = jnp.sum(st, axis=0, keepdims=True)
 
+        scores(0)
+        for pair in range(BLK // 2):
+            if pair + 1 < BLK // 2:
+                scores(pair + 1)
+            mix(pair, soft(pair))
+
     def combine(i):
-        d_send(i).wait_recv()
         s0 = opart[i, pl.ds(HALF * BLK, BLK), :]
         s1 = drx[i, pl.ds(HALF * BLK, BLK), :]
         peak = jnp.maximum(s0, s1)
@@ -222,7 +219,6 @@
             comb[i, rows, :] = bcast_col(f0, j) * opart[i, rows, :] + bcast_col(f1, j) * drx[i, rows, :]
 
     def finish(i):
-        x_send(i).wait_recv()
         first = chip == 0
 
         def ordered(rows):
@@ -239,30 +235,52 @@
             a, b = ordered(pl.ds(j * BLK, BLK))
             ofin[pl.ds(pl.multiple_of(i * BLK, BLK), BLK), j * HD:(j + 1) * HD] = bcast_col(g0, j) * a + bcast_col(g1, j) * b
 
-    def step(i, carry):
-        @pl.when(i < NBLK)
+    def fetch(i):
+        k_copy(i).wait()
+        v_copy(i).wait()
+
+        @pl.when(i + AHEAD < NBLK)
         def _():
-            attend(i)
-
-        @pl.when(jnp.logical_and(i >= 1, i < NBLK + 1))
+            k_copy(i + AHEAD).start()
+            v_copy(i + AHEAD).start()
+
+        @pl.when(i + AHEAD == NBLK)
         def _():
-            combine(i - 1)
-
-        @pl.when(i < NBLK)
-        def _():
-            d_send(i).start()
-
-        @pl.when(i >= LAG)
-        def _():
-            finish(i - LAG)
-
-        @pl.when(jnp.logical_and(i >= 1, i < NBLK + 1))
-        def _():
-            x_send(i - 1).start()
-
-        return carry
-
-    lax.fori_loop(0, NBLK + LAG, step, 0)
+            for n in range(4):
+                wo_copy(n).start()
+
+    def early(i, carry):
+        fetch(i)
+        attend(i)
+        d_send(i).start()
+        return carry
+
+    def steady(i, carry):
+        fetch(i)
+        d_send(i - LAG).wait_recv()
+        combine(i - LAG)
+        attend(i)
+        d_send(i).start()
+        x_send(i - LAG).start()
+        return carry
+
+    lax.fori_loop(0, LAG, early, 0)
+    lax.fori_loop(LAG, NBLK, steady, 0)
+
+    def late(i, carry):
+        d_send(i).wait_recv()
+        combine(i)
+        x_send(i).start()
+        return carry
+
+    lax.fori_loop(NBLK - LAG, NBLK, late, 0)
+
+    def last(i, carry):
+        x_send(i).wait_recv()
+        finish(i)
+        return carry
+
+    lax.fori_loop(0, NBLK, last, 0)
 
     lhs = ofin[...].astype(BF16)
     for n in range(4):
@@ -380,6 +398,7 @@
                 pltpu.VMEM((NBLK, PIECE, HD), F32), pltpu.VMEM((NBLK, PIECE, HD), F32), pltpu.VMEM((NBLK, PIECE, HD), F32),
                 pltpu.VMEM((SEQS, HALF * HD), F32),
                 pltpu.VMEM((4, SEQS, WCH), F32), pltpu.VMEM((4, SEQS, WCH), F32),
+                pltpu.VMEM((2, 4 * HALF, ROWS), F32), pltpu.VMEM((2, 4 * HALF, ROWS), BF16),
                 dma((6,)), dma((NBLK,)), dma((NBLK,)), dma((4,)), dma, dma,
                 dma((NBLK,)), dma((NBLK,)), dma((NBLK,)), dma((NBLK,)), dma((4,)), dma((4,)),
             ],

time: 47.2 us -> 43.8 us (0.928)
  Pallas kernels: 46.4 us -> 43 us
    pallas_call x1, Pallas kernels: 35.1 us -> 31.7 us  [device_step(): pl.pallas_call(attend_kernel, out_shape=(pltpu.VMEM(rows, BF16), pltpu.VM...]
where the time goes in v4:
time: 43.8 us; the launch traced here: 43.7 us
  Pallas kernels  43 us (98%)
  between operations  0.64 us (1%)
    pallas_call x1, Pallas kernels, device_step(): pl.pallas_call(attend_kernel, out_shape=(pltpu.VMEM(rows, BF16), pltpu.VM...  31.7 us
    pallas_call x1, Pallas kernels, device_step(): pl.pallas_call(write_kernel, out_shape=(pltpu.HBM(rows, BF16), pltpu.HBM(...  11.3 us

profile of v4, /device:TPU:0, one launch (start us, length us, event | category | flops | bytes accessed | tf_op | source)
XLA Modules:
  0.0 43.7 jit_solution(9671523157426247728)
XLA Ops:
  0.6 31.7 %attend.1 = (bf16[64,1024,128]{2,1,0:T(8,128)(2,1)S(1)}, bf16[64,1024,128]{2,1,0:T(8,128)(2,1)S(1)}, f32[2,1024,128]{2,1,0:T(8,128)S(1)}, bf16[64,2048]{1,0:T(8,128)(2,1)S(1)}) custom-call(s32[64]{0:T(128)} %pos_h.3, bf16[64,2048]{1,0:T(8,128)(2,1)} %tok_h.1, bf16[16,128]{1,0:T(8,128)(2,1)} %bitcast.10, bf16[1,128]{1,0:T(2,128)(2,1)} %bitcast.11, ...), custom_call_target="tpu_custom_call" | custom-call | tf_op jit(solution)/shard_map/attend/pallas_call | solution.py:383
  32.3 11.3 %write.1 = (bf16[64,1024,128]{2,1,0:T(8,128)(2,1)}, bf16[64,1024,128]{2,1,0:T(8,128)(2,1)}, bf16[64,2048]{1,0:T(8,128)(2,1)}, bf16[64,8,128]{2,1,0:T(8,128)(2,1)...) custom-call(s32[64]{0:T(128)} %pos_h.3, ...), custom_call_target="tpu_custom_call", output_to_operand_aliasing={{4}: (1, {}), {5}: (2, {})} | custom-call | tf_op jit(solution)/shard_map/write/pallas_call | solution.py:410

commit v5 on v4

--- a/solution.py
+++ b/solution.py
@@ -24,10 +24,12 @@
 BLK = 8
 NBLK = SEQS // BLK
 AHEAD = 2
+NX = 4
+RING = 3
 LAG = 2
 WCH = 512
 PIECE = (HALF + 1) * BLK
-VMEM_LIMIT = 26 * 2**20
+VMEM_LIMIT = 16 * 2**20
 EXP_SCALE = HD ** -0.5 * 1.4426950408889634
 NEG = -jnp.inf
 
@@ -37,9 +39,9 @@
 
 
 def attend_kernel(pos_h, tok_h, an_h, qn_h, kn_h, freq_h, wq, wk, wv, wo, kc, vc,
-                  kv, vv, rep, bout,
-                  pos_s, tok, an, qn, kn, freq, insem, w_s, hid, ang, cosr, sinr, qmine, qmate, colslot, opart, drx, comb, xrx, ofin, pbuf, prx, sc, pr_s,
-                  wsem, ksem, vsem, wosem, qs, qr, ds_, dr, xs, xr, ps, pr):
+                  kv, vv, rep, wo_v, comb_a, comb_b, xrx,
+                  pos_s, tok, an, qn, kn, freq, insem, w_s, hid, ang, cosr, sinr, qmine, qmate, colslot, opart, drx, sc, pr_s,
+                  wsem, ksem, vsem, wosem, qs, qr, ds_, dr, xs, xr):
     me = lax.axis_index('sp')
     core = lax.rem(me, 2)
     chip = me // 2
@@ -51,11 +53,11 @@
             src = wq.at[:, pl.ds(pl.multiple_of(core * (HALF * HD) + n * WCH, WCH), WCH)]
         else:
             src = (wk, wv)[n - 4]
-        return pltpu.make_async_copy(src, w_s.at[n], wsem.at[n])
+        return pltpu.make_async_copy(src, w_s.at[n % RING], wsem.at[n])
 
     def wo_copy(n):
         src = wo.at[pl.ds(pl.multiple_of(core * (HALF * HD), HD), HALF * HD), pl.ds(n * WCH, WCH)]
-        return pltpu.make_async_copy(src, w_s.at[n], wosem.at[n])
+        return pltpu.make_async_copy(src, wo_v.at[n], wosem.at[n])
 
     def k_copy(i):
         return pltpu.make_async_copy(kc.at[pl.ds(i * BLK, BLK)], kv.at[pl.ds(i * BLK, BLK)], ksem.at[i])
@@ -71,12 +73,8 @@
                                             device_id=mate, device_id_type=MESH)
 
     def x_send(i):
-        return pltpu.make_async_remote_copy(comb.at[i], xrx.at[i], xs.at[i], xr.at[i],
+        return pltpu.make_async_remote_copy(comb_a.at[i], xrx.at[i], xs.at[i], xr.at[i],
                                             device_id=peer, device_id_type=MESH)
-
-    def p_send(n):
-        return pltpu.make_async_remote_copy(pbuf.at[n], prx.at[n], ps.at[n], pr.at[n],
-                                            device_id=mate, device_id_type=MESH)
 
     small = [pltpu.make_async_copy(a, b, insem.at[z]) for z, (a, b) in enumerate(
         ((tok_h, tok), (pos_h, pos_s), (an_h, an), (qn_h, qn), (kn_h, kn), (freq_h, freq)))]
@@ -130,7 +128,7 @@
         else:
             k_copy(n + AHEAD - 6).start()
             v_copy(n + AHEAD - 6).start()
-        proj = jnp.dot(hid[...], w_s[n], preferred_element_type=F32).astype(BF16).astype(F32)
+        proj = jnp.dot(hid[...], w_s[n % RING], preferred_element_type=F32).astype(BF16).astype(F32)
         for j in range(WCH // HD):
             x = proj[:, j * HD:(j + 1) * HD]
             if n < 4:
@@ -204,7 +202,7 @@
                 scores(pair + 1)
             mix(pair, soft(pair))
 
-    def combine(i):
+    def combine(i, comb, at):
         s0 = opart[i, pl.ds(HALF * BLK, BLK), :]
         s1 = drx[i, pl.ds(HALF * BLK, BLK), :]
         peak = jnp.maximum(s0, s1)
@@ -212,28 +210,11 @@
         f0 = jnp.exp2((s0 - safe) * EXP_SCALE)
         f1 = jnp.exp2((s1 - safe) * EXP_SCALE)
         total = f0 * pltpu.roll(s0, HD - HALF, 1) + f1 * pltpu.roll(s1, HD - HALF, 1)
-        comb[i, pl.ds(HALF * BLK, BLK), :] = jnp.where(
+        comb[at, pl.ds(HALF * BLK, BLK), :] = jnp.where(
             lane8 < HALF, peak, jnp.where(lane8 < 2 * HALF, pltpu.roll(total, HALF, 1), 0.0))
         for j in range(HALF):
             rows = pl.ds(j * BLK, BLK)
-            comb[i, rows, :] = bcast_col(f0, j) * opart[i, rows, :] + bcast_col(f1, j) * drx[i, rows, :]
-
-    def finish(i):
-        first = chip == 0
-
-        def ordered(rows):
-            mine, other = comb[i, rows, :], xrx[i, rows, :]
-            return jnp.where(first, mine, other), jnp.where(first, other, mine)
-
-        s0, s1 = ordered(pl.ds(HALF * BLK, BLK))
-        peak = jnp.maximum(s0, s1)
-        f0 = jnp.exp2((s0 - peak) * EXP_SCALE)
-        f1 = jnp.exp2((s1 - peak) * EXP_SCALE)
-        total = f0 * pltpu.roll(s0, HD - HALF, 1) + f1 * pltpu.roll(s1, HD - HALF, 1)
-        g0, g1 = f0 / total, f1 / total
-        for j in range(HALF):
-            a, b = ordered(pl.ds(j * BLK, BLK))
-            ofin[pl.ds(pl.multiple_of(i * BLK, BLK), BLK), j * HD:(j + 1) * HD] = bcast_col(g0, j) * a + bcast_col(g1, j) * b
+            comb[at, rows, :] = bcast_col(f0, j) * opart[i, rows, :] + bcast_col(f1, j) * drx[i, rows, :]
 
     def fetch(i):
         k_copy(i).wait()
@@ -255,54 +236,96 @@
         d_send(i).start()
         return carry
 
-    def steady(i, carry):
+    def sending(i, carry):
         fetch(i)
         d_send(i - LAG).wait_recv()
-        combine(i - LAG)
+        combine(i - LAG, comb_a, i - LAG)
         attend(i)
         d_send(i).start()
         x_send(i - LAG).start()
         return carry
 
-    lax.fori_loop(0, LAG, early, 0)
-    lax.fori_loop(LAG, NBLK, steady, 0)
+    def keeping(i, carry):
+        fetch(i)
+        d_send(i - LAG).wait_recv()
+        combine(i - LAG, comb_b, i - LAG - NX)
+        attend(i)
+        d_send(i).start()
+        return carry
 
     def late(i, carry):
         d_send(i).wait_recv()
-        combine(i)
-        x_send(i).start()
-        return carry
-
+        combine(i, comb_b, i - NX)
+        return carry
+
+    lax.fori_loop(0, LAG, early, 0)
+    lax.fori_loop(LAG, LAG + NX, sending, 0)
+    lax.fori_loop(LAG + NX, NBLK, keeping, 0)
     lax.fori_loop(NBLK - LAG, NBLK, late, 0)
 
-    def last(i, carry):
-        x_send(i).wait_recv()
-        finish(i)
-        return carry
-
-    lax.fori_loop(0, NBLK, last, 0)
-
-    lhs = ofin[...].astype(BF16)
     for n in range(4):
         wo_copy(n).wait()
-        pbuf[n] = jnp.dot(lhs, w_s[n], preferred_element_type=F32)
+
+    def drain(i, carry):
+        d_send(i).wait_send()
+        return carry
+
+    def drain_x(i, carry):
+        x_send(i).wait()
+        return carry
+
+    lax.fori_loop(0, NBLK, drain, 0)
+    lax.fori_loop(0, NX, drain_x, 0)
+
+
+def last_merge(chip, comb, other_ref, i, ofin, at):
+    first = chip == 0
+
+    def ordered(rows):
+        mine, other = comb[i, rows, :], other_ref[i, rows, :]
+        return jnp.where(first, mine, other), jnp.where(first, other, mine)
+
+    s0, s1 = ordered(pl.ds(HALF * BLK, BLK))
+    peak = jnp.maximum(s0, s1)
+    f0 = jnp.exp2((s0 - peak) * EXP_SCALE)
+    f1 = jnp.exp2((s1 - peak) * EXP_SCALE)
+    total = f0 * pltpu.roll(s0, HD - HALF, 1) + f1 * pltpu.roll(s1, HD - HALF, 1)
+    g0, g1 = f0 / total, f1 / total
+    for j in range(HALF):
+        a, b = ordered(pl.ds(j * BLK, BLK))
+        ofin[at * BLK:(at + 1) * BLK, j * HD:(j + 1) * HD] = bcast_col(g0, j) * a + bcast_col(g1, j) * b
+
+
+def finish_kernel(tok_h, wo_v, oa, comb_b, xrx_b, bout, tok, ofin, pbuf, prx, insem, ps, pr):
+    me = lax.axis_index('sp')
+    core = lax.rem(me, 2)
+    mate = {'sp': me + 1 - 2 * core}
+    tok_copy = pltpu.make_async_copy(tok_h, tok, insem)
+    tok_copy.start()
+    barrier = pltpu.get_barrier_semaphore()
+    pl.semaphore_signal(barrier, inc=1, device_id=mate, device_id_type=MESH)
+    for i in range(NBLK - NX):
+        last_merge(me // 2, comb_b, xrx_b, i, ofin, i)
+    lhs = jnp.concatenate([oa[...].astype(BF16), ofin[...].astype(BF16)], axis=0)
+    pl.semaphore_wait(barrier, 1)
+
+    def p_send(n):
+        return pltpu.make_async_remote_copy(pbuf.at[n], prx.at[n], ps.at[n], pr.at[n],
+                                            device_id=mate, device_id_type=MESH)
+
+    for n in range(4):
+        pbuf[n] = jnp.dot(lhs, wo_v[n], preferred_element_type=F32)
         p_send(n).start()
+    tok_copy.wait()
     for n in range(4):
         p_send(n).wait_recv()
         sl = slice(n * WCH, (n + 1) * WCH)
         bout[:, sl] = (tok[:, sl].astype(F32) + (pbuf[n] + prx[n])).astype(BF16)
-
-    def drain(i, carry):
-        d_send(i).wait_send()
-        x_send(i).wait_send()
-        return carry
-
-    lax.fori_loop(0, NBLK, drain, 0)
     for n in range(4):
         p_send(n).wait_send()
 
 
-def write_kernel(pos_h, kv, vv, rep, bin_, ko, vo, bo, nkv, kva, vva, pos_s, nkv_s, patch, ksem, vsem, psem, osem):
+def write_kernel(pos_h, kv, vv, rep, comb_a, xrx, wo_v, ko, vo, nkv, oa, kva, vva, pos_s, nkv_s, patch, ksem, vsem, psem, osem):
     start = lax.axis_index('sp') * SLOTS
     slot16 = lax.broadcasted_iota(jnp.int32, (4 * KVH, HD), 0) // KVH
 
@@ -313,8 +336,6 @@
 
     pos_copy = pltpu.make_async_copy(pos_h, pos_s, osem.at[0])
     pos_copy.start()
-    out_copy = pltpu.make_async_copy(bin_, bo, osem.at[1])
-    out_copy.start()
     for c in copies(0):
         c.start()
     for b in range(SEQS):
@@ -352,15 +373,16 @@
         if i > 1:
             for c in copies(i - 1):
                 c.start()
-    nkv_copy = pltpu.make_async_copy(nkv_s, nkv, osem.at[2])
+    nkv_copy = pltpu.make_async_copy(nkv_s, nkv, osem.at[1])
     nkv_copy.start()
     each(0, stage)
     for c in copies(NBLK - 1):
         c.start()
+    for i in range(NX):
+        last_merge(lax.axis_index('sp') // 2, comb_a, xrx, i, oa, i)
     for c in copies(0):
         c.wait()
     each(0, lambda b, z, base, mask, ref, out: patch_copy(b, z, base, out).start())
-    out_copy.wait()
     nkv_copy.wait()
     each(0, lambda b, z, base, mask, ref, out: patch_copy(b, z, base, out).wait())
     for i in range(1, NBLK):
@@ -380,46 +402,58 @@
         in_hbm = lambda x: pltpu.with_memory_space_constraint(x, pltpu.HBM)
         in_vmem = lambda x: pltpu.with_memory_space_constraint(x, pltpu.VMEM)
         rows = (SEQS, ROWS, HD)
-        kv, vv, rep, bout = pl.pallas_call(
+        piece = (PIECE, HD)
+        kv, vv, rep, wo_v, comb_a, comb_b, xrx_a = pl.pallas_call(
             attend_kernel,
             out_shape=(pltpu.VMEM(rows, BF16), pltpu.VMEM(rows, BF16),
-                       pltpu.VMEM((2, SEQS * 4 * KVH, HD), F32), pltpu.VMEM((SEQS, DIM), BF16)),
+                       pltpu.VMEM((2, SEQS * 4 * KVH, HD), F32), pltpu.VMEM((4, HALF * HD, WCH), BF16),
+                       pltpu.VMEM((NX,) + piece, F32), pltpu.VMEM((NBLK - NX,) + piece, F32), pltpu.VMEM((NX,) + piece, F32)),
             in_specs=[hbm] * 12,
-            out_specs=(vm, vm, vm, vm),
+            out_specs=(vm,) * 7,
             scratch_shapes=[
                 pltpu.SMEM((SEQS,), jnp.int32), pltpu.VMEM((SEQS, DIM), BF16), pltpu.VMEM((DIM // HD, HD), BF16),
                 pltpu.VMEM((1, HD), BF16), pltpu.VMEM((1, HD), BF16), pltpu.VMEM((1, HD), F32), dma((6,)),
-                pltpu.VMEM((6, DIM, WCH), BF16),
+                pltpu.VMEM((RING, DIM, WCH), BF16),
                 pltpu.VMEM((SEQS, DIM), BF16),
                 pltpu.VMEM((SEQS, HD), F32), pltpu.VMEM((SEQS, HD), F32), pltpu.VMEM((SEQS, HD), F32),
                 pltpu.VMEM((SEQS * HALF, HD), F32), pltpu.VMEM((SEQS * HALF, HD), F32),
                 pltpu.VMEM((2 * HALF, ROWS), jnp.int32),
                 pltpu.VMEM((NBLK, 2 * PIECE, HD), F32),
-                pltpu.VMEM((NBLK, PIECE, HD), F32), pltpu.VMEM((NBLK, PIECE, HD), F32), pltpu.VMEM((NBLK, PIECE, HD), F32),
-                pltpu.VMEM((SEQS, HALF * HD), F32),
-                pltpu.VMEM((4, SEQS, WCH), F32), pltpu.VMEM((4, SEQS, WCH), F32),
+                pltpu.VMEM((NBLK,) + piece, F32),
                 pltpu.VMEM((2, 4 * HALF, ROWS), F32), pltpu.VMEM((2, 4 * HALF, ROWS), BF16),
                 dma((6,)), dma((NBLK,)), dma((NBLK,)), dma((4,)), dma, dma,
-                dma((NBLK,)), dma((NBLK,)), dma((NBLK,)), dma((NBLK,)), dma((4,)), dma((4,)),
+                dma((NBLK,)), dma((NBLK,)), dma((NX,)), dma((NX,)),
             ],
             compiler_params=pltpu.CompilerParams(collective_id=0, has_side_effects=True, vmem_limit_bytes=VMEM_LIMIT),
             name='attend',
         )(in_hbm(positions), in_hbm(tokens), in_hbm(attn_norm.reshape(DIM // HD, HD)), in_hbm(q_norm.reshape(1, HD)),
           in_hbm(k_norm.reshape(1, HD)), in_hbm(jnp.asarray(freq2).reshape(1, HD)), in_hbm(w_q), in_hbm(w_k), in_hbm(w_v), in_hbm(w_o),
           in_hbm(k_cache.reshape(rows)), in_hbm(v_cache.reshape(rows)))
-        k_out, v_out, block_out, new_kv, _, _ = pl.pallas_call(
+        xrx_b = lax.ppermute(comb_b, 'sp', [(0, 2), (2, 0), (1, 3), (3, 1)])
+        k_out, v_out, new_kv, oa, _, _ = pl.pallas_call(
             write_kernel,
-            out_shape=(pltpu.HBM(rows, BF16), pltpu.HBM(rows, BF16), pltpu.HBM((SEQS, DIM), BF16),
-                       pltpu.HBM((SEQS, 2 * KVH, HD), BF16), pltpu.VMEM(rows, BF16), pltpu.VMEM(rows, BF16)),
-            in_specs=[hbm, vm, vm, vm, vm],
-            out_specs=(hbm, hbm, hbm, hbm, vm, vm),
+            out_shape=(pltpu.HBM(rows, BF16), pltpu.HBM(rows, BF16), pltpu.HBM((SEQS, 2 * KVH, HD), BF16),
+                       pltpu.VMEM((NX * BLK, HALF * HD), F32), pltpu.VMEM(rows, BF16), pltpu.VMEM(rows, BF16)),
+            in_specs=[hbm, vm, vm, vm, vm, vm, vm],
+            out_specs=(hbm, hbm, hbm, vm, vm, vm),
             input_output_aliases={1: 4, 2: 5},
             scratch_shapes=[pltpu.SMEM((SEQS,), jnp.int32), pltpu.VMEM((SEQS, 2 * KVH, HD), BF16),
                             pltpu.VMEM((2, BLK, 4 * KVH, HD), BF16),
-                            dma((NBLK,)), dma((NBLK,)), dma((2, BLK)), dma((3,))],
+                            dma((NBLK,)), dma((NBLK,)), dma((2, BLK)), dma((2,))],
             compiler_params=pltpu.CompilerParams(vmem_limit_bytes=VMEM_LIMIT),
+            cost_estimate=pl.CostEstimate(flops=10**10, bytes_accessed=2**25, transcendentals=0),
             name='write',
-        )(in_hbm(positions), in_vmem(kv), in_vmem(vv), in_vmem(rep), in_vmem(bout))
+        )(in_hbm(positions), in_vmem(kv), in_vmem(vv), in_vmem(rep), in_vmem(comb_a), in_vmem(xrx_a), in_vmem(wo_v))
+        block_out = pl.pallas_call(
+            finish_kernel,
+            out_shape=jax.ShapeDtypeStruct((SEQS, DIM), BF16),
+            in_specs=[hbm, vm, vm, vm, vm],
+            out_specs=vm,
+            scratch_shapes=[pltpu.VMEM((SEQS, DIM), BF16), pltpu.VMEM(((NBLK - NX) * BLK, HALF * HD), F32),
+                            pltpu.VMEM((4, SEQS, WCH), F32), pltpu.VMEM((4, SEQS, WCH), F32), dma, dma((4,)), dma((4,))],
+            compiler_params=pltpu.CompilerParams(collective_id=1, has_side_effects=True, vmem_limit_bytes=VMEM_LIMIT),
+            name='finish',
+        )(in_hbm(tokens), in_vmem(wo_v), in_vmem(oa), in_vmem(comb_b), xrx_b)
         return block_out, k_out.reshape(k_cache.shape), v_out.reshape(v_cache.shape), new_kv.reshape(SEQS, 2, KVH, HD)
 
     return jax.shard_map(device_step, mesh=mesh, in_specs=(P('dp', None), P('dp'), cache_spec, cache_spec, P(), P(), P(), P(), P(), P(), P()), out_specs=(P('dp', None), cache_spec, cache_spec, P('dp', None, None, None)), check_vma=False)

time: 43.8 us -> 39.5 us (0.902)
  Pallas kernels: 43 us -> 37.2 us
  starting transfers between devices: 0 us -> 0.81 us
  local copies, waits for them, and re-layouts: 0 us -> 0.71 us
    pallas_call x1, Pallas kernels: 31.7 us -> 22.5 us  [device_step(): pl.pallas_call(attend_kernel, out_shape=(pltpu.VMEM(rows, BF16), pltpu.VM...]
    pallas_call x0 -> x1, Pallas kernels: none -> 3.51 us  [device_step(): pl.pallas_call(finish_kernel, out_shape=jax.ShapeDtypeStruct((SEQS, DIM),...]
    ppermute x0 -> x1, starting transfers between devices: none -> 0.81 us  [device_step(): xrx_b = lax.ppermute(comb_b, 'sp', [(0, 2), (2, 0), (1, 3), (3, 1)])]
    unnamed x0 -> x1, local copies, waits for them, and re-layouts: none -> 0.71 us
  transfers between devices with their start and end apart: 0 -> 1, of which waited for: 0 -> 0; matrix products, arithmetic and copies ran while one was open for 0% -> 0% of each run, Pallas kernels for 0% -> 29%
where the time goes in v5:
time: 39.5 us; the launch traced here: 39.4 us
  Pallas kernels  37.2 us (94%)
  starting transfers between devices  0.81 us (2%)
  local copies, waits for them, and re-layouts  0.71 us (2%)
  between operations  0.67 us (2%)
    pallas_call x1, Pallas kernels, device_step(): pl.pallas_call(attend_kernel, out_shape=(pltpu.VMEM(rows, BF16), pltpu.VM...  22.5 us
    pallas_call x1, Pallas kernels, device_step(): pl.pallas_call(write_kernel, out_shape=(pltpu.HBM(rows, BF16), pltpu.HBM(...  11.2 us
    pallas_call x1, Pallas kernels, device_step(): pl.pallas_call(finish_kernel, out_shape=jax.ShapeDtypeStruct((SEQS, DIM),...  3.51 us
    ppermute x1, starting transfers between devices, device_step(): xrx_b = lax.ppermute(comb_b, 'sp', [(0, 2), (2, 0), (1, 3), (3, 1)])  0.81 us
  transfers between devices with their start and end apart: 1, of which 0 were waited for; matrix products, arithmetic and copies ran while one was open for 0% of the time, Pallas kernels for 29%

profile of v5, /device:TPU:0, one launch (start us, length us, event | category | flops | bytes accessed | tf_op | source)
XLA Modules:
  0.0 39.4 jit_solution(17906702847531218787)
XLA Ops:
  0.6 22.5 %attend.1 = (bf16[64,1024,128]{2,1,0:T(8,128)(2,1)S(1)}, bf16[64,1024,128]{2,1,0:T(8,128)(2,1)S(1)}, f32[2,1024,128]{2,1,0:T(8,128)S(1)}, bf16[4,2048,512]{2,1,0...) custom-call(s32[64]{0:T(128)} %pos_h.3, ...), custom_call_target="tpu_custom_call" | custom-call | tf_op jit(solution)/shard_map/attend/pallas_call | solution.py:406
  23.1 0.8 %collective-permute-start = (f32[4,136,128]{2,1,0:T(8,128)S(1)}, f32[4,136,128]{2,1,0:T(8,128)S(1)}, u32[]{:S(2)}, u32[]{:S(2)}) collective-permute-start(f32[4,136,128]{2,1,0:T(8,128)S(1)} %get-tuple-element.22.comb_b), channel_id=1, source_target_pairs={{0,2},{2,0},{1,3},{3,1},{4,6},{6,4},{5,7},{7,5}} | collective-permute-start | bytes 835592 | tf_op jit(solution)/shard_map/ppermute | solution.py:432
  23.9 11.2 %write.1 = (bf16[64,1024,128]{2,1,0:T(8,128)(2,1)}, bf16[64,1024,128]{2,1,0:T(8,128)(2,1)}, bf16[64,8,128]{2,1,0:T(8,128)(2,1)}, f32[32,2048]{1,0:T(8,128)S(1)},...) custom-call(s32[64]{0:T(128)} %pos_h.3, ...), custom_call_target="tpu_custom_call", output_to_operand_aliasing={{4}: (1, {}), {5}: (2, {})} | custom-call | flops 10000000000 | bytes 33554432 | tf_op jit(solution)/shard_map/write/pallas_call | solution.py:433
  35.2 0.0 collective-permute-done.xrx_b
  35.2 3.5 %finish.1 = bf16[64,2048]{1,0:T(8,128)(2,1)S(1)} custom-call(bf16[64,2048]{1,0:T(8,128)(2,1)} %tok_h.3, bf16[4,2048,512]{2,1,0:T(8,128)(2,1)S(1)} %get-tuple-element.15.wo_v, f32[32,2048]{1,0:T(8,128)S(1)} %get-tuple-element.21.oa, f32[4,136,128]{2,1,0:T(8,128)S(1)} %get-tuple-element.22.comb_b, f32[4,136,128]{2,1,0:T(8,128)S(1)} %collective-permute-done.xrx_b), custom_call_target="tpu_custom_call" | custom-call | tf_op jit(solution)/shard_map/finish/pallas_call | solution.py:447
  38.7 0.7 %copy.21 = bf16[64,2048]{1,0:T(8,128)(2,1)} copy(bf16[64,2048]{1,0:T(8,128)(2,1)S(1)} %finish.1) | data formatting | bytes 524288
Async XLA Ops:
  23.1 12.1 %collective-permute-start = (f32[4,136,128]{2,1,0:T(8,128)S(1)}, f32[4,136,128]{2,1,0:T(8,128)S(1)}, u32[]{:S(2)}, u32[]{:S(2)}) collective-permute-start(f32[4,136,128]{2,1,0:T(8,128)S(1)} %get-tuple-element.22.comb_b), channel_id=1, source_target_pairs={{0,2},{2,0},{1,3},{3,1},{4,6},{6,4},{5,7},{7,5}} | collective-permute-start | bytes 835592 | tf_op jit(solution)/shard_map/ppermute | solution.py:432

commit v6 on v5

--- a/solution.py
+++ b/solution.py
@@ -25,11 +25,12 @@
 NBLK = SEQS // BLK
 AHEAD = 2
 NX = 4
+NA, NB = 6, 7
 RING = 3
 LAG = 2
 WCH = 512
 PIECE = (HALF + 1) * BLK
-VMEM_LIMIT = 16 * 2**20
+VMEM_LIMIT = 14 * 2**20
 EXP_SCALE = HD ** -0.5 * 1.4426950408889634
 NEG = -jnp.inf
 
@@ -296,43 +297,41 @@
         ofin[at * BLK:(at + 1) * BLK, j * HD:(j + 1) * HD] = bcast_col(g0, j) * a + bcast_col(g1, j) * b
 
 
-def finish_kernel(tok_h, wo_v, oa, comb_b, xrx_b, bout, tok, ofin, pbuf, prx, insem, ps, pr):
-    me = lax.axis_index('sp')
-    core = lax.rem(me, 2)
-    mate = {'sp': me + 1 - 2 * core}
-    tok_copy = pltpu.make_async_copy(tok_h, tok, insem)
-    tok_copy.start()
-    barrier = pltpu.get_barrier_semaphore()
-    pl.semaphore_signal(barrier, inc=1, device_id=mate, device_id_type=MESH)
+def block_copies(i, kv, vv, ko, vo, ksem, vsem):
+    r = pl.ds(i * BLK, BLK)
+    return (pltpu.make_async_copy(kv.at[r], ko.at[r], ksem.at[i]),
+            pltpu.make_async_copy(vv.at[r], vo.at[r], vsem.at[i]))
+
+
+def product_kernel(kv, vv, ki, vi, oa, comb_b, xrx_b, wo_v, ko, vo, part, ofin, ksem, vsem):
+    for i in range(NA, NB):
+        for c in block_copies(i, kv, vv, ko, vo, ksem, vsem):
+            c.start()
     for i in range(NBLK - NX):
-        last_merge(me // 2, comb_b, xrx_b, i, ofin, i)
+        last_merge(lax.axis_index('sp') // 2, comb_b, xrx_b, i, ofin, i)
     lhs = jnp.concatenate([oa[...].astype(BF16), ofin[...].astype(BF16)], axis=0)
-    pl.semaphore_wait(barrier, 1)
-
-    def p_send(n):
-        return pltpu.make_async_remote_copy(pbuf.at[n], prx.at[n], ps.at[n], pr.at[n],
-                                            device_id=mate, device_id_type=MESH)
-
     for n in range(4):
-        pbuf[n] = jnp.dot(lhs, wo_v[n], preferred_element_type=F32)
-        p_send(n).start()
-    tok_copy.wait()
-    for n in range(4):
-        p_send(n).wait_recv()
-        sl = slice(n * WCH, (n + 1) * WCH)
-        bout[:, sl] = (tok[:, sl].astype(F32) + (pbuf[n] + prx[n])).astype(BF16)
-    for n in range(4):
-        p_send(n).wait_send()
-
-
-def write_kernel(pos_h, kv, vv, rep, comb_a, xrx, wo_v, ko, vo, nkv, oa, kva, vva, pos_s, nkv_s, patch, ksem, vsem, psem, osem):
+        part[:, n * WCH:(n + 1) * WCH] = jnp.dot(lhs, wo_v[n], preferred_element_type=F32)
+    for i in range(NA, NB):
+        for c in block_copies(i, kv, vv, ko, vo, ksem, vsem):
+            c.wait()
+
+
+def rest_kernel(kv, vv, ki, vi, ko, vo, ksem, vsem):
+    for i in range(NB, NBLK):
+        for c in block_copies(i, kv, vv, ko, vo, ksem, vsem):
+            c.start()
+    for i in range(NB, NBLK):
+        for c in block_copies(i, kv, vv, ko, vo, ksem, vsem):
+            c.wait()
+
+
+def write_kernel(pos_h, kv, vv, rep, comb_a, xrx, wo_v, ko, vo, nkv, oa, kva, vva, wo_a, pos_s, nkv_s, patch, ksem, vsem, psem, osem):
     start = lax.axis_index('sp') * SLOTS
     slot16 = lax.broadcasted_iota(jnp.int32, (4 * KVH, HD), 0) // KVH
 
     def copies(i):
-        r = pl.ds(i * BLK, BLK)
-        return (pltpu.make_async_copy(kv.at[r], ko.at[r], ksem.at[i]),
-                pltpu.make_async_copy(vv.at[r], vo.at[r], vsem.at[i]))
+        return block_copies(i, kv, vv, ko, vo, ksem, vsem)
 
     pos_copy = pltpu.make_async_copy(pos_h, pos_s, osem.at[0])
     pos_copy.start()
@@ -370,14 +369,12 @@
 
     for i in range(1, NBLK):
         each(i, put)
-        if i > 1:
+        if 1 < i <= NA:
             for c in copies(i - 1):
                 c.start()
     nkv_copy = pltpu.make_async_copy(nkv_s, nkv, osem.at[1])
     nkv_copy.start()
     each(0, stage)
-    for c in copies(NBLK - 1):
-        c.start()
     for i in range(NX):
         last_merge(lax.axis_index('sp') // 2, comb_a, xrx, i, oa, i)
     for c in copies(0):
@@ -385,7 +382,7 @@
     each(0, lambda b, z, base, mask, ref, out: patch_copy(b, z, base, out).start())
     nkv_copy.wait()
     each(0, lambda b, z, base, mask, ref, out: patch_copy(b, z, base, out).wait())
-    for i in range(1, NBLK):
+    for i in range(1, NA):
         for c in copies(i):
             c.wait()
 
@@ -430,13 +427,14 @@
           in_hbm(k_norm.reshape(1, HD)), in_hbm(jnp.asarray(freq2).reshape(1, HD)), in_hbm(w_q), in_hbm(w_k), in_hbm(w_v), in_hbm(w_o),
           in_hbm(k_cache.reshape(rows)), in_hbm(v_cache.reshape(rows)))
         xrx_b = lax.ppermute(comb_b, 'sp', [(0, 2), (2, 0), (1, 3), (3, 1)])
-        k_out, v_out, new_kv, oa, _, _ = pl.pallas_call(
+        k_out, v_out, new_kv, oa, kv, vv, wo_v = pl.pallas_call(
             write_kernel,
             out_shape=(pltpu.HBM(rows, BF16), pltpu.HBM(rows, BF16), pltpu.HBM((SEQS, 2 * KVH, HD), BF16),
-                       pltpu.VMEM((NX * BLK, HALF * HD), F32), pltpu.VMEM(rows, BF16), pltpu.VMEM(rows, BF16)),
+                       pltpu.VMEM((NX * BLK, HALF * HD), F32), pltpu.VMEM(rows, BF16), pltpu.VMEM(rows, BF16),
+                       pltpu.VMEM((4, HALF * HD, WCH), BF16)),
             in_specs=[hbm, vm, vm, vm, vm, vm, vm],
-            out_specs=(hbm, hbm, hbm, vm, vm, vm),
-            input_output_aliases={1: 4, 2: 5},
+            out_specs=(hbm, hbm, hbm, vm, vm, vm, vm),
+            input_output_aliases={1: 4, 2: 5, 6: 6},
             scratch_shapes=[pltpu.SMEM((SEQS,), jnp.int32), pltpu.VMEM((SEQS, 2 * KVH, HD), BF16),
                             pltpu.VMEM((2, BLK, 4 * KVH, HD), BF16),
                             dma((NBLK,)), dma((NBLK,)), dma((2, BLK)), dma((2,))],
@@ -444,16 +442,30 @@
             cost_estimate=pl.CostEstimate(flops=10**10, bytes_accessed=2**25, transcendentals=0),
             name='write',
         )(in_hbm(positions), in_vmem(kv), in_vmem(vv), in_vmem(rep), in_vmem(comb_a), in_vmem(xrx_a), in_vmem(wo_v))
-        block_out = pl.pallas_call(
-            finish_kernel,
-            out_shape=jax.ShapeDtypeStruct((SEQS, DIM), BF16),
-            in_specs=[hbm, vm, vm, vm, vm],
-            out_specs=vm,
-            scratch_shapes=[pltpu.VMEM((SEQS, DIM), BF16), pltpu.VMEM(((NBLK - NX) * BLK, HALF * HD), F32),
-                            pltpu.VMEM((4, SEQS, WCH), F32), pltpu.VMEM((4, SEQS, WCH), F32), dma, dma((4,)), dma((4,))],
-            compiler_params=pltpu.CompilerParams(collective_id=1, has_side_effects=True, vmem_limit_bytes=VMEM_LIMIT),
-            name='finish',
-        )(in_hbm(tokens), in_vmem(wo_v), in_vmem(oa), in_vmem(comb_b), xrx_b)
+        k_out, v_out, part = pl.pallas_call(
+            product_kernel,
+            out_shape=(pltpu.HBM(rows, BF16), pltpu.HBM(rows, BF16), pltpu.VMEM((SEQS, DIM), F32)),
+            in_specs=[vm, vm, hbm, hbm, vm, vm, vm, vm],
+            out_specs=(hbm, hbm, vm),
+            input_output_aliases={2: 0, 3: 1},
+            scratch_shapes=[pltpu.VMEM(((NBLK - NX) * BLK, HALF * HD), F32), dma((NBLK,)), dma((NBLK,))],
+            compiler_params=pltpu.CompilerParams(vmem_limit_bytes=VMEM_LIMIT),
+            cost_estimate=pl.CostEstimate(flops=2 * SEQS * DIM * DIM, bytes_accessed=2**22, transcendentals=0),
+            name='product',
+        )(in_vmem(kv), in_vmem(vv), k_out, v_out, in_vmem(oa), in_vmem(comb_b), in_vmem(xrx_b), in_vmem(wo_v))
+        other = lax.ppermute(part, 'sp', [(0, 1), (1, 0), (2, 3), (3, 2)])
+        k_out, v_out = pl.pallas_call(
+            rest_kernel,
+            out_shape=(pltpu.HBM(rows, BF16), pltpu.HBM(rows, BF16)),
+            in_specs=[vm, vm, hbm, hbm],
+            out_specs=(hbm, hbm),
+            input_output_aliases={2: 0, 3: 1},
+            scratch_shapes=[dma((NBLK,)), dma((NBLK,))],
+            compiler_params=pltpu.CompilerParams(vmem_limit_bytes=VMEM_LIMIT),
+            cost_estimate=pl.CostEstimate(flops=10**9, bytes_accessed=2**22, transcendentals=0),
+            name='rest',
+        )(in_vmem(kv), in_vmem(vv), k_out, v_out)
+        block_out = (tokens.astype(F32) + (part + other)).astype(BF16)
         return block_out, k_out.reshape(k_cache.shape), v_out.reshape(v_cache.shape), new_kv.reshape(SEQS, 2, KVH, HD)
 
     return jax.shard_map(device_step, mesh=mesh, in_specs=(P('dp', None), P('dp'), cache_spec, cache_spec, P(), P(), P(), P(), P(), P(), P()), out_specs=(P('dp', None), cache_spec, cache_spec, P('dp', None, None, None)), check_vma=False)

time: 39.5 us -> 37.9 us (0.959)
  Pallas kernels: 37.2 us -> 35.5 us
  other arithmetic: 0 us -> 0.77 us
  local copies, waits for them, and re-layouts: 0.71 us -> 0.01 us
    pallas_call x1, Pallas kernels: 11.2 us -> 8.68 us  [device_step(): pl.pallas_call(write_kernel, out_shape=(pltpu.HBM(rows, BF16), pltpu.HBM(...]
    pallas_call x1 -> x2, Pallas kernels: 3.51 us -> 4.32 us  [the longest x1 2.17 us: device_step(): pl.pallas_call(product_kernel, out_shape=(pltpu.HBM(rows, BF16), pltpu.HB...]
    convert_element_type x0 -> x1, other arithmetic: none -> 0.77 us  [device_step(): block_out = (tokens.astype(F32) + (part + other)).astype(BF16)]
    unnamed x1 -> x2, local copies, waits for them, and re-layouts: 0.71 us -> 0.01 us
  transfers between devices with their start and end apart: 1 -> 2, of which waited for: 0 -> 0; matrix products, arithmetic and copies ran while one was open for 0% -> 0% of each run, Pallas kernels for 29% -> 29%
where the time goes in v6:
time: 37.9 us; the launch traced here: 37.8 us
  Pallas kernels  35.5 us (94%)
  starting transfers between devices  0.91 us (2%)
  other arithmetic  0.77 us (2%)
  between operations  0.69 us (2%)
    pallas_call x1, Pallas kernels, device_step(): pl.pallas_call(attend_kernel, out_shape=(pltpu.VMEM(rows, BF16), pltpu.VM...  22.5 us
    pallas_call x1, Pallas kernels, device_step(): pl.pallas_call(write_kernel, out_shape=(pltpu.HBM(rows, BF16), pltpu.HBM(...  8.68 us
    pallas_call x1, Pallas kernels, device_step(): pl.pallas_call(product_kernel, out_shape=(pltpu.HBM(rows, BF16), pltpu.HB...  2.17 us
    pallas_call x1, Pallas kernels, device_step(): pl.pallas_call(rest_kernel, out_shape=(pltpu.HBM(rows, BF16), pltpu.HBM(r...  2.15 us
    ppermute x1, starting transfers between devices, device_step(): xrx_b = lax.ppermute(comb_b, 'sp', [(0, 2), (2, 0), (1, 3), (3, 1)])  0.81 us
    convert_element_type x1, other arithmetic, device_step(): block_out = (tokens.astype(F32) + (part + other)).astype(BF16)  0.77 us
  transfers between devices with their start and end apart: 2, of which 0 were waited for; matrix products, arithmetic and copies ran while one was open for 0% of the time, Pallas kernels for 29%

profile of v6, /device:TPU:0, one launch (start us, length us, event | category | flops | bytes accessed | tf_op | source)
XLA Modules:
  0.0 37.8 jit_solution(15486938994862596170)
XLA Ops:
  0.6 22.5 %attend.1 = (bf16[64,1024,128]{2,1,0:T(8,128)(2,1)S(1)}, bf16[64,1024,128]{2,1,0:T(8,128)(2,1)S(1)}, f32[2,1024,128]{2,1,0:T(8,128)S(1)}, bf16[4,2048,512]{2,1,0...) custom-call(s32[64]{0:T(128)} %pos_h.3, ...), custom_call_target="tpu_custom_call" | custom-call | tf_op jit(solution)/shard_map/attend/pallas_call | solution.py:403
  23.1 0.8 %collective-permute-start = (f32[4,136,128]{2,1,0:T(8,128)S(1)}, f32[4,136,128]{2,1,0:T(8,128)S(1)}, u32[]{:S(2)}, u32[]{:S(2)}) collective-permute-start(f32[4,136,128]{2,1,0:T(8,128)S(1)} %get-tuple-element.34.comb_b), channel_id=1, source_target_pairs={{0,2},{2,0},{1,3},{3,1},{4,6},{6,4},{5,7},{7,5}} | collective-permute-start | bytes 835592 | tf_op jit(solution)/shard_map/ppermute | solution.py:429
  23.9 8.7 %write.1 = (bf16[64,1024,128]{2,1,0:T(8,128)(2,1)}, bf16[64,1024,128]{2,1,0:T(8,128)(2,1)}, bf16[64,8,128]{2,1,0:T(8,128)(2,1)}, f32[32,2048]{1,0:T(8,128)S(1)},...) custom-call(s32[64]{0:T(128)} %pos_h.3, ...), custom_call_target="tpu_custom_call", output_to_operand_aliasing={{4}: (1, {}), {5}: (2, {}), {6}: (6, {})} | custom-call | flops 10000000000 | bytes 33554432 | tf_op jit(solution)/shard_map/write/pallas_call | solution.py:430
  32.6 0.0 collective-permute-done.xrx_b
  32.6 2.2 %product.1 = (bf16[64,1024,128]{2,1,0:T(8,128)(2,1)}, bf16[64,1024,128]{2,1,0:T(8,128)(2,1)}, f32[64,2048]{1,0:T(8,128)S(1)}) custom-call(bf16[64,1024,128]{2,1,0:T(8,128)(2,1)S(1)} %get-tuple-element.29.kv, bf16[64,1024,128]{2,1,0:T(8,128)(2,1)S(1)} %get-tuple-element.30.vv, ...), custom_call_target="tpu_custom_call", output_to_operand_aliasing={{0}: (2, {}), {1}: (3, {})} | custom-call | flops 536870912 | bytes 4194304 | tf_op jit(solution)/shard_map/product/pallas_call | solution.py:445
  34.8 0.1 collective-permute-start.1
  34.9 0.0 copy-start
  34.9 2.1 %rest.1 = (bf16[64,1024,128]{2,1,0:T(8,128)(2,1)}, bf16[64,1024,128]{2,1,0:T(8,128)(2,1)}) custom-call(bf16[64,1024,128]{2,1,0:T(8,128)(2,1)S(1)} %get-tuple-element.29.kv, bf16[64,1024,128]{2,1,0:T(8,128)(2,1)S(1)} %get-tuple-element.30.vv, bf16[64,1024,128]{2,1,0:T(8,128)(2,1)} %get-tuple-element.37.ki, ...), custom_call_target="tpu_custom_call", output_to_operand_aliasing={{0}: (2, {}), {1}: (3, {})} | custom-call | flops 1000000000 | bytes 4194304 | tf_op jit(solution)/shard_map/rest/pallas_call | solution.py:457
  37.0 0.0 collective-permute-done.1
  37.1 0.0 copy-done
  37.1 0.8 %add_convert_fusion = bf16[64,2048]{1,0:T(8,128)(2,1)} fusion(f32[64,2048]{1,0:T(8,128)S(1)} %get-tuple-element.36, f32[64,2048]{1,0:T(8,128)S(1)} %collective-permute-done.1, bf16[64,2048]{1,0:T(8,128)(2,1)S(1)} %copy-done), kind=kLoop, calls=%fused_computation | loop fusion | flops 524288 | bytes 1572864 | tf_op jit(solution)/shard_map/convert_element_type | solution.py:468
Async XLA Ops:
  23.1 9.5 %collective-permute-start = (f32[4,136,128]{2,1,0:T(8,128)S(1)}, f32[4,136,128]{2,1,0:T(8,128)S(1)}, u32[]{:S(2)}, u32[]{:S(2)}) collective-permute-start(f32[4,136,128]{2,1,0:T(8,128)S(1)} %get-tuple-element.34.comb_b), channel_id=1, source_target_pairs={{0,2},{2,0},{1,3},{3,1},{4,6},{6,4},{5,7},{7,5}} | collective-permute-start | bytes 835592 | tf_op jit(solution)/shard_map/ppermute | solution.py:429
  34.8 2.3 %collective-permute-start.1 = (f32[64,2048]{1,0:T(8,128)S(1)}, f32[64,2048]{1,0:T(8,128)S(1)}, u32[]{:S(2)}, u32[]{:S(2)}) collective-permute-start(f32[64,2048]{1,0:T(8,128)S(1)} %get-tuple-element.36), channel_id=1, source_target_pairs={{0,1},{1,0},{2,3},{3,2},{4,5},{5,4},{6,7},{7,6}} | collective-permute-start | bytes 1572872 | tf_op jit(solution)/shard_map/ppermute | solution.py:456
  34.9 2.2 %copy-start = (bf16[64,2048]{1,0:T(8,128)(2,1)S(1)}, bf16[64,2048]{1,0:T(8,128)(2,1)}, u32[]{:S(2)}) copy-start(bf16[64,2048]{1,0:T(8,128)(2,1)} %tok_h.1) | copy-start | bytes 786436

commit v7 on v6

--- a/solution.py
+++ b/solution.py
@@ -26,7 +26,9 @@
 AHEAD = 2
 NX = 4
 NA, NB = 6, 7
-RING = 3
+NW = 5
+WAHEAD = 3
+RING = 4
 LAG = 2
 WCH = 512
 PIECE = (HALF + 1) * BLK
@@ -41,7 +43,7 @@
 
 def attend_kernel(pos_h, tok_h, an_h, qn_h, kn_h, freq_h, wq, wk, wv, wo, kc, vc,
                   kv, vv, rep, wo_v, comb_a, comb_b, xrx,
-                  pos_s, tok, an, qn, kn, freq, insem, w_s, hid, ang, cosr, sinr, qmine, qmate, colslot, opart, drx, sc, pr_s,
+                  pos_s, tok, an, qn, kn, freq, insem, proj, w_s, hid, ang, cosr, sinr, qmine, qmate, colslot, opart, drx, sc, pr_s,
                   wsem, ksem, vsem, wosem, qs, qr, ds_, dr, xs, xr):
     me = lax.axis_index('sp')
     core = lax.rem(me, 2)
@@ -49,12 +51,22 @@
     mate = {'sp': me + 1 - 2 * core}
     peer = {'sp': me + 2 - 4 * chip}
 
-    def w_copy(n):
+    def w_copy(n, src=None):
         if n < 4:
             src = wq.at[:, pl.ds(pl.multiple_of(core * (HALF * HD) + n * WCH, WCH), WCH)]
+        return pltpu.make_async_copy(src, w_s.at[n % RING], wsem.at[n])
+
+    def w_start(n):
+        if n < 4:
+            w_copy(n).start()
         else:
-            src = (wk, wv)[n - 4]
-        return pltpu.make_async_copy(src, w_s.at[n % RING], wsem.at[n])
+            @pl.when(core == 0)
+            def _():
+                w_copy(n, wk).start()
+
+            @pl.when(core == 1)
+            def _():
+                w_copy(n, wv).start()
 
     def wo_copy(n):
         src = wo.at[pl.ds(pl.multiple_of(core * (HALF * HD), HD), HALF * HD), pl.ds(n * WCH, WCH)]
@@ -66,8 +78,11 @@
     def v_copy(i):
         return pltpu.make_async_copy(vc.at[pl.ds(i * BLK, BLK)], vv.at[pl.ds(i * BLK, BLK)], vsem.at[i])
 
-    def q_send():
-        return pltpu.make_async_remote_copy(qmine, qmate, qs, qr, device_id=mate, device_id_type=MESH)
+    def q_send(h):
+        return pltpu.make_async_remote_copy(qmine.at[h], qmate.at[h], qs.at[h], qr.at[h], device_id=mate, device_id_type=MESH)
+
+    def new_send():
+        return pltpu.make_async_remote_copy(rep.at[core], rep.at[core], qs.at[2], qr.at[2], device_id=mate, device_id_type=MESH)
 
     def d_send(i):
         return pltpu.make_async_remote_copy(opart.at[i, pl.ds(PIECE, PIECE)], drx.at[i], ds_.at[i], dr.at[i],
@@ -81,16 +96,32 @@
         ((tok_h, tok), (pos_h, pos_s), (an_h, an), (qn_h, qn), (kn_h, kn), (freq_h, freq)))]
     for c in small:
         c.start()
-    for n in range(AHEAD):
-        w_copy(n).start()
+    for n in range(WAHEAD):
+        w_start(n)
 
     barrier = pltpu.get_barrier_semaphore()
     for other in (mate, peer):
         pl.semaphore_signal(barrier, inc=1, device_id=other, device_id_type=MESH)
 
-    for c in small:
+    for c in small[1:]:
         c.wait()
-
+    lane1 = lax.broadcasted_iota(jnp.int32, (1, HD), 1)
+
+    def angle(b, carry):
+        ang[pl.ds(b, 1), :] = freq[...] * pos_s[b].astype(F32)
+        return carry
+
+    lax.fori_loop(0, SEQS, angle, 0, unroll=8)
+    cosr[...] = jnp.cos(ang[...])
+    sinr[...] = jnp.sin(ang[...]) * jnp.where(lane1 < HD // 2, -1.0, 1.0)
+
+    row = lax.broadcasted_iota(jnp.int32, (2 * HALF, ROWS), 0)
+    col = lax.broadcasted_iota(jnp.int32, (2 * HALF, ROWS), 1)
+    half_of_row = jnp.where(row < HALF, core, 1 - core)
+    kv_of_row = half_of_row * 2 + lax.rem(row, HALF) // 8
+    colslot[...] = jnp.where(lax.rem(col, KVH) == kv_of_row, col // KVH, 1 << 20)
+
+    small[0].wait()
     t = tok[...].astype(F32)
     inv = lax.rsqrt(jnp.sum(t * t, axis=-1, keepdims=True) * (1.0 / DIM) + NORM_EPS)
     gains = an[...].astype(F32)
@@ -98,22 +129,6 @@
         sl = slice(j * HD, (j + 1) * HD)
         hid[:, sl] = (tok[:, sl].astype(F32) * inv * gains[j:j + 1, :]).astype(BF16)
 
-    lane1 = lax.broadcasted_iota(jnp.int32, (1, HD), 1)
-
-    def angle(b, carry):
-        ang[pl.ds(b, 1), :] = freq[...] * pos_s[b].astype(F32)
-        return carry
-
-    lax.fori_loop(0, SEQS, angle, 0)
-    cosr[...] = jnp.cos(ang[...])
-    sinr[...] = jnp.sin(ang[...]) * jnp.where(lane1 < HD // 2, -1.0, 1.0)
-
-    row = lax.broadcasted_iota(jnp.int32, (2 * HALF, ROWS), 0)
-    col = lax.broadcasted_iota(jnp.int32, (2 * HALF, ROWS), 1)
-    half_of_row = jnp.where(row < HALF, core, 1 - core)
-    kv_of_row = half_of_row * 2 + lax.rem(row, HALF) // 8
-    colslot[...] = jnp.where(lax.rem(col, KVH) == kv_of_row, col // KVH, 1 << 20)
-
     qgain = qn[...].astype(F32)
     kgain = kn[...].astype(F32)
 
@@ -122,40 +137,51 @@
         y = y * cosr[...] + pltpu.roll(y, HD // 2, 1) * sinr[...]
         return y.astype(BF16).astype(F32)
 
-    for n in range(6):
-        w_copy(n).wait()
-        if n + AHEAD < 6:
-            w_copy(n + AHEAD).start()
-        else:
-            k_copy(n + AHEAD - 6).start()
-            v_copy(n + AHEAD - 6).start()
-        proj = jnp.dot(hid[...], w_s[n % RING], preferred_element_type=F32).astype(BF16).astype(F32)
+    def post(n):
         for j in range(WCH // HD):
-            x = proj[:, j * HD:(j + 1) * HD]
+            x = proj[n % 2, :, j * HD:(j + 1) * HD].astype(BF16).astype(F32)
             if n < 4:
-                qmine[pl.ds(n * 4 + j, SEQS, stride=HALF), :] = norm_rope(x, qgain)
+                qmine.at[n // 2][pl.ds(n % 2 * 4 + j, SEQS, stride=8), :] = norm_rope(x, qgain)
             else:
-                y = norm_rope(x, kgain) if n == 4 else x
-                for c in range(4):
-                    rep[n - 4, pl.ds(c * KVH + j, SEQS, stride=4 * KVH), :] = y
-        if n == 3:
+                rep.at[core][pl.ds(j, SEQS, stride=KVH), :] = jnp.where(core == 0, norm_rope(x, kgain), x)
+
+    for n in range(NW):
+        w_copy(n, wk).wait()
+        if n + WAHEAD < NW:
+            w_start(n + WAHEAD)
+        elif n + WAHEAD - NW < AHEAD:
+            k_copy(n + WAHEAD - NW).start()
+            v_copy(n + WAHEAD - NW).start()
+        proj[n % 2] = jnp.dot(hid[...], w_s[n % RING], preferred_element_type=F32)
+        if n > 0:
+            post(n - 1)
+        if n == 2:
             pl.semaphore_wait(barrier, 2)
-            q_send().start()
+            q_send(0).start()
+        if n == 4:
+            q_send(1).start()
+    for i in range(WAHEAD, AHEAD):
+        k_copy(i).start()
+        v_copy(i).start()
+    post(NW - 1)
+    new_send().start()
     start = me * SLOTS
     lane = lax.broadcasted_iota(jnp.int32, (HALF, HD), 1)
     lrow = lax.broadcasted_iota(jnp.int32, (HALF, HD), 0)
     lane8 = lax.broadcasted_iota(jnp.int32, (BLK, HD), 1)
-    q_send().wait()
+    for h in range(2):
+        q_send(h).wait()
+    new_send().wait()
 
     def attend(i):
         ob = opart.at[i]
         def load_q(pair):
             bs = [i * BLK + 2 * pair + z for z in range(2)]
-            return bs, [jnp.concatenate([qmine[pl.ds(pl.multiple_of(b * HALF, HALF), HALF), :],
-                                         qmate[pl.ds(pl.multiple_of(b * HALF, HALF), HALF), :]], axis=0) for b in bs]
+            return bs, [jnp.concatenate([ref[h, pl.ds(pl.multiple_of(b * 8, 8), 8), :]
+                                         for ref in (qmine, qmate) for h in range(2)], axis=0) for b in bs]
 
         def new_rows(z, b):
-            return jnp.concatenate([jnp.broadcast_to(rep[z, pl.ds(b * 4 * KVH + h, 1), :], (8, HD))
+            return jnp.concatenate([jnp.broadcast_to(rep[z, pl.ds(b * KVH + h, 1), :], (8, HD))
                                     for h in (2 * core, 2 * core + 1, 2 - 2 * core, 3 - 2 * core)], axis=0)
 
         def scores(pair):
@@ -338,7 +364,7 @@
     for c in copies(0):
         c.start()
     for b in range(SEQS):
-        nkv_s[b] = jnp.concatenate([rep[0, pl.ds(b * 4 * KVH, KVH), :], rep[1, pl.ds(b * 4 * KVH, KVH), :]], axis=0).astype(BF16)
+        nkv_s[b] = jnp.concatenate([rep[0, pl.ds(b * KVH, KVH), :], rep[1, pl.ds(b * KVH, KVH), :]], axis=0).astype(BF16)
     pos_copy.wait()
 
     def each(i, do):
@@ -354,7 +380,7 @@
                     do(b, z, base, mask, ref, out)
 
     def merged(b, z, base, mask, ref):
-        new = rep[z, pl.ds(b * 4 * KVH, 4 * KVH), :]
+        new = jnp.concatenate([rep[z, pl.ds(b * KVH, KVH), :]] * 4, axis=0)
         old = ref[b, pl.ds(base, 4 * KVH), :].astype(F32)
         return jnp.where(mask, new, old).astype(BF16)
 
@@ -403,22 +429,23 @@
         kv, vv, rep, wo_v, comb_a, comb_b, xrx_a = pl.pallas_call(
             attend_kernel,
             out_shape=(pltpu.VMEM(rows, BF16), pltpu.VMEM(rows, BF16),
-                       pltpu.VMEM((2, SEQS * 4 * KVH, HD), F32), pltpu.VMEM((4, HALF * HD, WCH), BF16),
+                       pltpu.VMEM((2, SEQS * KVH, HD), F32), pltpu.VMEM((4, HALF * HD, WCH), BF16),
                        pltpu.VMEM((NX,) + piece, F32), pltpu.VMEM((NBLK - NX,) + piece, F32), pltpu.VMEM((NX,) + piece, F32)),
             in_specs=[hbm] * 12,
             out_specs=(vm,) * 7,
             scratch_shapes=[
                 pltpu.SMEM((SEQS,), jnp.int32), pltpu.VMEM((SEQS, DIM), BF16), pltpu.VMEM((DIM // HD, HD), BF16),
                 pltpu.VMEM((1, HD), BF16), pltpu.VMEM((1, HD), BF16), pltpu.VMEM((1, HD), F32), dma((6,)),
+                pltpu.VMEM((2, SEQS, WCH), F32),
                 pltpu.VMEM((RING, DIM, WCH), BF16),
                 pltpu.VMEM((SEQS, DIM), BF16),
                 pltpu.VMEM((SEQS, HD), F32), pltpu.VMEM((SEQS, HD), F32), pltpu.VMEM((SEQS, HD), F32),
-                pltpu.VMEM((SEQS * HALF, HD), F32), pltpu.VMEM((SEQS * HALF, HD), F32),
+                pltpu.VMEM((2, SEQS * 8, HD), F32), pltpu.VMEM((2, SEQS * 8, HD), F32),
                 pltpu.VMEM((2 * HALF, ROWS), jnp.int32),
                 pltpu.VMEM((NBLK, 2 * PIECE, HD), F32),
                 pltpu.VMEM((NBLK,) + piece, F32),
                 pltpu.VMEM((2, 4 * HALF, ROWS), F32), pltpu.VMEM((2, 4 * HALF, ROWS), BF16),
-                dma((6,)), dma((NBLK,)), dma((NBLK,)), dma((4,)), dma, dma,
+                dma((NW,)), dma((NBLK,)), dma((NBLK,)), dma((4,)), dma((3,)), dma((3,)),
                 dma((NBLK,)), dma((NBLK,)), dma((NX,)), dma((NX,)),
             ],
             compiler_params=pltpu.CompilerParams(collective_id=0, has_side_effects=True, vmem_limit_bytes=VMEM_LIMIT),

time: 37.9 us -> 36.9 us (0.974)
  Pallas kernels: 35.5 us -> 34.6 us
    pallas_call x1, Pallas kernels: 22.5 us -> 21.6 us  [device_step(): pl.pallas_call(attend_kernel, out_shape=(pltpu.VMEM(rows, BF16), pltpu.VM...]
where the time goes in v7:
time: 36.9 us; the launch traced here: 36.8 us
  Pallas kernels  34.6 us (94%)
  other arithmetic  0.77 us (2%)
  starting transfers between devices  0.71 us (2%)
  between operations  0.71 us (2%)
    pallas_call x1, Pallas kernels, device_step(): pl.pallas_call(attend_kernel, out_shape=(pltpu.VMEM(rows, BF16), pltpu.VM...  21.6 us
    pallas_call x1, Pallas kernels, device_step(): pl.pallas_call(write_kernel, out_shape=(pltpu.HBM(rows, BF16), pltpu.HBM(...  8.68 us
    pallas_call x1, Pallas kernels, device_step(): pl.pallas_call(product_kernel, out_shape=(pltpu.HBM(rows, BF16), pltpu.HB...  2.17 us
    pallas_call x1, Pallas kernels, device_step(): pl.pallas_call(rest_kernel, out_shape=(pltpu.HBM(rows, BF16), pltpu.HBM(r...  2.16 us
    convert_element_type x1, other arithmetic, device_step(): block_out = (tokens.astype(F32) + (part + other)).astype(BF16)  0.77 us
  transfers between devices with their start and end apart: 2, of which 0 were waited for; matrix products, arithmetic and copies ran while one was open for 0% of the time, Pallas kernels for 29%

profile of v7, /device:TPU:0, one launch (start us, length us, event | category | flops | bytes accessed | tf_op | source)
XLA Modules:
  0.0 36.8 jit_solution(11353782421525914611)
XLA Ops:
  0.6 21.6 %attend.1 = (bf16[64,1024,128]{2,1,0:T(8,128)(2,1)S(1)}, bf16[64,1024,128]{2,1,0:T(8,128)(2,1)S(1)}, f32[2,256,128]{2,1,0:T(8,128)S(1)}, bf16[4,2048,512]{2,1,0:...) custom-call(s32[64]{0:T(128)} %pos_h.3, ...), custom_call_target="tpu_custom_call" | custom-call | tf_op jit(solution)/shard_map/attend/pallas_call | solution.py:429
  22.2 0.7 %collective-permute-start = (f32[4,136,128]{2,1,0:T(8,128)S(1)}, f32[4,136,128]{2,1,0:T(8,128)S(1)}, u32[]{:S(2)}, u32[]{:S(2)}) collective-permute-start(f32[4,136,128]{2,1,0:T(8,128)S(1)} %get-tuple-element.34.comb_b), channel_id=1, source_target_pairs={{0,2},{2,0},{1,3},{3,1},{4,6},{6,4},{5,7},{7,5}} | collective-permute-start | bytes 835592 | tf_op jit(solution)/shard_map/ppermute | solution.py:456
  22.9 8.7 %write.1 = (bf16[64,1024,128]{2,1,0:T(8,128)(2,1)}, bf16[64,1024,128]{2,1,0:T(8,128)(2,1)}, bf16[64,8,128]{2,1,0:T(8,128)(2,1)}, f32[32,2048]{1,0:T(8,128)S(1)},...) custom-call(s32[64]{0:T(128)} %pos_h.3, ...), custom_call_target="tpu_custom_call", output_to_operand_aliasing={{4}: (1, {}), {5}: (2, {}), {6}: (6, {})} | custom-call | flops 10000000000 | bytes 33554432 | tf_op jit(solution)/shard_map/write/pallas_call | solution.py:457
  31.6 0.0 collective-permute-done.xrx_b
  31.6 2.2 %product.1 = (bf16[64,1024,128]{2,1,0:T(8,128)(2,1)}, bf16[64,1024,128]{2,1,0:T(8,128)(2,1)}, f32[64,2048]{1,0:T(8,128)S(1)}) custom-call(bf16[64,1024,128]{2,1,0:T(8,128)(2,1)S(1)} %get-tuple-element.29.kv, bf16[64,1024,128]{2,1,0:T(8,128)(2,1)S(1)} %get-tuple-element.30.vv, ...), custom_call_target="tpu_custom_call", output_to_operand_aliasing={{0}: (2, {}), {1}: (3, {})} | custom-call | flops 536870912 | bytes 4194304 | tf_op jit(solution)/shard_map/product/pallas_call | solution.py:472
  33.8 0.0 collective-permute-start.1
  33.8 0.0 copy-start
  33.8 2.2 %rest.1 = (bf16[64,1024,128]{2,1,0:T(8,128)(2,1)}, bf16[64,1024,128]{2,1,0:T(8,128)(2,1)}) custom-call(bf16[64,1024,128]{2,1,0:T(8,128)(2,1)S(1)} %get-tuple-element.29.kv, bf16[64,1024,128]{2,1,0:T(8,128)(2,1)S(1)} %get-tuple-element.30.vv, bf16[64,1024,128]{2,1,0:T(8,128)(2,1)} %get-tuple-element.37.ki, ...), custom_call_target="tpu_custom_call", output_to_operand_aliasing={{0}: (2, {}), {1}: (3, {})} | custom-call | flops 1000000000 | bytes 4194304 | tf_op jit(solution)/shard_map/rest/pallas_call | solution.py:484
  36.0 0.0 collective-permute-done.1
  36.0 0.0 copy-done
  36.0 0.8 %add_convert_fusion = bf16[64,2048]{1,0:T(8,128)(2,1)} fusion(f32[64,2048]{1,0:T(8,128)S(1)} %get-tuple-element.36, f32[64,2048]{1,0:T(8,128)S(1)} %collective-permute-done.1, bf16[64,2048]{1,0:T(8,128)(2,1)S(1)} %copy-done), kind=kLoop, calls=%fused_computation | loop fusion | flops 524288 | bytes 1572864 | tf_op jit(solution)/shard_map/convert_element_type | solution.py:495
Async XLA Ops:
  22.2 9.4 %collective-permute-start = (f32[4,136,128]{2,1,0:T(8,128)S(1)}, f32[4,136,128]{2,1,0:T(8,128)S(1)}, u32[]{:S(2)}, u32[]{:S(2)}) collective-permute-start(f32[4,136,128]{2,1,0:T(8,128)S(1)} %get-tuple-element.34.comb_b), channel_id=1, source_target_pairs={{0,2},{2,0},{1,3},{3,1},{4,6},{6,4},{5,7},{7,5}} | collective-permute-start | bytes 835592 | tf_op jit(solution)/shard_map/ppermute | solution.py:456
  33.8 2.2 %collective-permute-start.1 = (f32[64,2048]{1,0:T(8,128)S(1)}, f32[64,2048]{1,0:T(8,128)S(1)}, u32[]{:S(2)}, u32[]{:S(2)}) collective-permute-start(f32[64,2048]{1,0:T(8,128)S(1)} %get-tuple-element.36), channel_id=1, source_target_pairs={{0,1},{1,0},{2,3},{3,2},{4,5},{5,4},{6,7},{7,6}} | collective-permute-start | bytes 1572872 | tf_op jit(solution)/shard_map/ppermute | solution.py:483
  33.8 2.2 %copy-start = (bf16[64,2048]{1,0:T(8,128)(2,1)S(1)}, bf16[64,2048]{1,0:T(8,128)(2,1)}, u32[]{:S(2)}) copy-start(bf16[64,2048]{1,0:T(8,128)(2,1)} %tok_h.1) | copy-start | bytes 786436

commit v8 on v7

--- a/solution.py
+++ b/solution.py
@@ -23,9 +23,9 @@
 ROWS = SLOTS * KVH
 BLK = 8
 NBLK = SEQS // BLK
-AHEAD = 2
-NX = 4
-NA, NB = 6, 7
+AHEAD = 4
+NX = 3
+NA = 7
 NW = 5
 WAHEAD = 3
 RING = 4
@@ -160,7 +160,7 @@
             q_send(0).start()
         if n == 4:
             q_send(1).start()
-    for i in range(WAHEAD, AHEAD):
+    for i in range(min(WAHEAD, AHEAD), AHEAD):
         k_copy(i).start()
         v_copy(i).start()
     post(NW - 1)
@@ -173,10 +173,10 @@
         q_send(h).wait()
     new_send().wait()
 
-    def attend(i):
+    def attend(i, first=False):
         ob = opart.at[i]
-        def load_q(pair):
-            bs = [i * BLK + 2 * pair + z for z in range(2)]
+        def load_q(pair, at):
+            bs = [at * BLK + 2 * pair + z for z in range(2)]
             return bs, [jnp.concatenate([ref[h, pl.ds(pl.multiple_of(b * 8, 8), 8), :]
                                          for ref in (qmine, qmate) for h in range(2)], axis=0) for b in bs]
 
@@ -184,8 +184,8 @@
             return jnp.concatenate([jnp.broadcast_to(rep[z, pl.ds(b * KVH + h, 1), :], (8, HD))
                                     for h in (2 * core, 2 * core + 1, 2 - 2 * core, 3 - 2 * core)], axis=0)
 
-        def scores(pair):
-            bs, qf = load_q(pair)
+        def scores(pair, at):
+            bs, qf = load_q(pair, at)
             zero = jnp.zeros((2 * HALF, HD), BF16)
             lhs = jnp.concatenate([jnp.concatenate([qf[0].astype(BF16), zero], axis=1),
                                    jnp.concatenate([zero, qf[1].astype(BF16)], axis=1)], axis=0)
@@ -193,7 +193,7 @@
             sc[pair % 2] = lax.dot_general(lhs, keys, (((1,), (1,)), ((), ())), preferred_element_type=F32)
 
         def soft(pair):
-            bs, qf = load_q(pair)
+            bs, qf = load_q(pair, i)
             out = []
             for z in range(2):
                 b = bs[z]
@@ -223,10 +223,14 @@
                     st = jnp.where(lane == lrow, peak[hs], jnp.where(lane == lrow + HALF, total[hs], 0.0))
                     ob[pl.ds(h * PIECE + HALF * BLK + bb, 1), :] = jnp.sum(st, axis=0, keepdims=True)
 
-        scores(0)
+        if first:
+            scores(0, i)
+            return
         for pair in range(BLK // 2):
             if pair + 1 < BLK // 2:
-                scores(pair + 1)
+                scores(pair + 1, i)
+            else:
+                scores(0, jnp.minimum(i + 1, NBLK - 1))
             mix(pair, soft(pair))
 
     def combine(i, comb, at):
@@ -244,7 +248,10 @@
             comb[at, rows, :] = bcast_col(f0, j) * opart[i, rows, :] + bcast_col(f1, j) * drx[i, rows, :]
 
     def fetch(i):
-        k_copy(i).wait()
+        @pl.when(i + 1 < NBLK)
+        def _():
+            k_copy(i + 1).wait()
+
         v_copy(i).wait()
 
         @pl.when(i + AHEAD < NBLK)
@@ -285,6 +292,8 @@
         combine(i, comb_b, i - NX)
         return carry
 
+    k_copy(0).wait()
+    attend(0, first=True)
     lax.fori_loop(0, LAG, early, 0)
     lax.fori_loop(LAG, LAG + NX, sending, 0)
     lax.fori_loop(LAG + NX, NBLK, keeping, 0)
@@ -330,26 +339,19 @@
 
 
 def product_kernel(kv, vv, ki, vi, oa, comb_b, xrx_b, wo_v, ko, vo, part, ofin, ksem, vsem):
-    for i in range(NA, NB):
-        for c in block_copies(i, kv, vv, ko, vo, ksem, vsem):
-            c.start()
+    block_copies(NA, kv, vv, ko, vo, ksem, vsem)[0].start()
     for i in range(NBLK - NX):
         last_merge(lax.axis_index('sp') // 2, comb_b, xrx_b, i, ofin, i)
     lhs = jnp.concatenate([oa[...].astype(BF16), ofin[...].astype(BF16)], axis=0)
     for n in range(4):
         part[:, n * WCH:(n + 1) * WCH] = jnp.dot(lhs, wo_v[n], preferred_element_type=F32)
-    for i in range(NA, NB):
-        for c in block_copies(i, kv, vv, ko, vo, ksem, vsem):
-            c.wait()
+    block_copies(NA, kv, vv, ko, vo, ksem, vsem)[0].wait()
 
 
 def rest_kernel(kv, vv, ki, vi, ko, vo, ksem, vsem):
-    for i in range(NB, NBLK):
-        for c in block_copies(i, kv, vv, ko, vo, ksem, vsem):
-            c.start()
-    for i in range(NB, NBLK):
-        for c in block_copies(i, kv, vv, ko, vo, ksem, vsem):
-            c.wait()
+    copy = block_copies(NA, kv, vv, ko, vo, ksem, vsem)[1]
+    copy.start()
+    copy.wait()
 
 
 def write_kernel(pos_h, kv, vv, rep, comb_a, xrx, wo_v, ko, vo, nkv, oa, kva, vva, wo_a, pos_s, nkv_s, patch, ksem, vsem, psem, osem):

time: 36.9 us -> 36.9 us (level)
  Pallas kernels: 34.6 us -> 33.3 us
  starting transfers between devices: 0.71 us -> 1.62 us
  waiting for transfers between devices: 0.01 us -> 0.41 us
    pallas_call x1, Pallas kernels: 21.6 us -> 20.1 us  [device_step(): pl.pallas_call(attend_kernel, out_shape=(pltpu.VMEM(rows, BF16), pltpu.VM...]
    pallas_call x1, Pallas kernels: 8.68 us -> 9.94 us  [device_step(): pl.pallas_call(write_kernel, out_shape=(pltpu.HBM(rows, BF16), pltpu.HBM(...]
    ppermute x1, starting transfers between devices: 0.68 us -> 1.59 us  [device_step(): xrx_b = lax.ppermute(comb_b, 'sp', [(0, 2), (2, 0), (1, 3), (3, 1)])]
    pallas_call x1, Pallas kernels: 2.16 us -> 1.47 us  [device_step(): pl.pallas_call(rest_kernel, out_shape=(pltpu.HBM(rows, BF16), pltpu.HBM(r...]
    ppermute x1, waiting for transfers between devices: 0.01 us -> 0.41 us  [device_step(): other = lax.ppermute(part, 'sp', [(0, 1), (1, 0), (2, 3), (3, 2)])]
  transfers between devices with their start and end apart: 2 -> 2, of which waited for: 0 -> 1; matrix products, arithmetic and copies ran while one was open for 0% -> 0% of each run, Pallas kernels for 29% -> 31%
where the time goes in v8:
time: 36.9 us; the launch traced here: 36.8 us
  Pallas kernels  33.3 us (90%)
  starting transfers between devices  1.62 us (4%)
  other arithmetic  0.79 us (2%)
  between operations  0.69 us (2%)
  waiting for transfers between devices  0.41 us (1%)
    pallas_call x1, Pallas kernels, device_step(): pl.pallas_call(attend_kernel, out_shape=(pltpu.VMEM(rows, BF16), pltpu.VM...  20.1 us
    pallas_call x1, Pallas kernels, device_step(): pl.pallas_call(write_kernel, out_shape=(pltpu.HBM(rows, BF16), pltpu.HBM(...  9.94 us
    pallas_call x1, Pallas kernels, device_step(): pl.pallas_call(product_kernel, out_shape=(pltpu.HBM(rows, BF16), pltpu.HB...  1.84 us
    ppermute x1, starting transfers between devices, device_step(): xrx_b = lax.ppermute(comb_b, 'sp', [(0, 2), (2, 0), (1, 3), (3, 1)])  1.59 us
    pallas_call x1, Pallas kernels, device_step(): pl.pallas_call(rest_kernel, out_shape=(pltpu.HBM(rows, BF16), pltpu.HBM(r...  1.47 us
    convert_element_type x1, other arithmetic, device_step(): block_out = (tokens.astype(F32) + (part + other)).astype(BF16)  0.79 us
  transfers between devices with their start and end apart: 2, of which 1 were waited for; matrix products, arithmetic and copies ran while one was open for 0% of the time, Pallas kernels for 31%

profile of v8, /device:TPU:0, one launch (start us, length us, event | category | flops | bytes accessed | tf_op | source)
XLA Modules:
  0.0 36.8 jit_solution(5555055715857492019)
XLA Ops:
  0.6 20.1 %attend.1 = (bf16[64,1024,128]{2,1,0:T(8,128)(2,1)S(1)}, bf16[64,1024,128]{2,1,0:T(8,128)(2,1)S(1)}, f32[2,256,128]{2,1,0:T(8,128)S(1)}, bf16[4,2048,512]{2,1,0:...) custom-call(s32[64]{0:T(128)} %pos_h.3, ...), custom_call_target="tpu_custom_call" | custom-call | tf_op jit(solution)/shard_map/attend/pallas_call | solution.py:431
  20.7 1.6 %collective-permute-start = (f32[5,136,128]{2,1,0:T(8,128)S(1)}, f32[5,136,128]{2,1,0:T(8,128)S(1)}, u32[]{:S(2)}, u32[]{:S(2)}) collective-permute-start(f32[5,136,128]{2,1,0:T(8,128)S(1)} %get-tuple-element.34.comb_b), channel_id=1, source_target_pairs={{0,2},{2,0},{1,3},{3,1},{4,6},{6,4},{5,7},{7,5}} | collective-permute-start | bytes 1044488 | tf_op jit(solution)/shard_map/ppermute | solution.py:458
  22.3 9.9 %write.1 = (bf16[64,1024,128]{2,1,0:T(8,128)(2,1)}, bf16[64,1024,128]{2,1,0:T(8,128)(2,1)}, bf16[64,8,128]{2,1,0:T(8,128)(2,1)}, f32[24,2048]{1,0:T(8,128)S(1)},...) custom-call(s32[64]{0:T(128)} %pos_h.3, ...), custom_call_target="tpu_custom_call", output_to_operand_aliasing={{4}: (1, {}), {5}: (2, {}), {6}: (6, {})} | custom-call | flops 10000000000 | bytes 33554432 | tf_op jit(solution)/shard_map/write/pallas_call | solution.py:459
  32.2 0.0 collective-permute-done.xrx_b
  32.2 1.8 %product.1 = (bf16[64,1024,128]{2,1,0:T(8,128)(2,1)}, bf16[64,1024,128]{2,1,0:T(8,128)(2,1)}, f32[64,2048]{1,0:T(8,128)S(1)}) custom-call(bf16[64,1024,128]{2,1,0:T(8,128)(2,1)S(1)} %get-tuple-element.29.kv, bf16[64,1024,128]{2,1,0:T(8,128)(2,1)S(1)} %get-tuple-element.30.vv, ...), custom_call_target="tpu_custom_call", output_to_operand_aliasing={{0}: (2, {}), {1}: (3, {})} | custom-call | flops 536870912 | bytes 4194304 | tf_op jit(solution)/shard_map/product/pallas_call | solution.py:474
  34.1 0.0 collective-permute-start.1
  34.1 0.0 copy-start
  34.1 1.5 %rest.1 = (bf16[64,1024,128]{2,1,0:T(8,128)(2,1)}, bf16[64,1024,128]{2,1,0:T(8,128)(2,1)}) custom-call(bf16[64,1024,128]{2,1,0:T(8,128)(2,1)S(1)} %get-tuple-element.29.kv, bf16[64,1024,128]{2,1,0:T(8,128)(2,1)S(1)} %get-tuple-element.30.vv, bf16[64,1024,128]{2,1,0:T(8,128)(2,1)} %get-tuple-element.37.ki, ...), custom_call_target="tpu_custom_call", output_to_operand_aliasing={{0}: (2, {}), {1}: (3, {})} | custom-call | flops 1000000000 | bytes 4194304 | tf_op jit(solution)/shard_map/rest/pallas_call | solution.py:486
  35.6 0.4 %collective-permute-done.1 = f32[64,2048]{1,0:T(8,128)S(1)} collective-permute-done((f32[64,2048]{1,0:T(8,128)S(1)}, f32[64,2048]{1,0:T(8,128)S(1)}, u32[]{:S(2)}, u32[]{:S(2)}) %collective-permute-start.1) | collective-permute-done | bytes 524320 | tf_op jit(solution)/shard_map/ppermute | solution.py:485
  36.0 0.0 copy-done
  36.0 0.8 %add_convert_fusion = bf16[64,2048]{1,0:T(8,128)(2,1)} fusion(f32[64,2048]{1,0:T(8,128)S(1)} %get-tuple-element.36, f32[64,2048]{1,0:T(8,128)S(1)} %collective-permute-done.1, bf16[64,2048]{1,0:T(8,128)(2,1)S(1)} %copy-done), kind=kLoop, calls=%fused_computation | loop fusion | flops 524288 | bytes 1572864 | tf_op jit(solution)/shard_map/convert_element_type | solution.py:497
Async XLA Ops:
  20.7 11.5 %collective-permute-start = (f32[5,136,128]{2,1,0:T(8,128)S(1)}, f32[5,136,128]{2,1,0:T(8,128)S(1)}, u32[]{:S(2)}, u32[]{:S(2)}) collective-permute-start(f32[5,136,128]{2,1,0:T(8,128)S(1)} %get-tuple-element.34.comb_b), channel_id=1, source_target_pairs={{0,2},{2,0},{1,3},{3,1},{4,6},{6,4},{5,7},{7,5}} | collective-permute-start | bytes 1044488 | tf_op jit(solution)/shard_map/ppermute | solution.py:458
  34.1 1.9 %collective-permute-start.1 = (f32[64,2048]{1,0:T(8,128)S(1)}, f32[64,2048]{1,0:T(8,128)S(1)}, u32[]{:S(2)}, u32[]{:S(2)}) collective-permute-start(f32[64,2048]{1,0:T(8,128)S(1)} %get-tuple-element.36), channel_id=1, source_target_pairs={{0,1},{1,0},{2,3},{3,2},{4,5},{5,4},{6,7},{7,6}} | collective-permute-start | bytes 1572872 | tf_op jit(solution)/shard_map/ppermute | solution.py:485
  34.1 1.9 %copy-start = (bf16[64,2048]{1,0:T(8,128)(2,1)S(1)}, bf16[64,2048]{1,0:T(8,128)(2,1)}, u32[]{:S(2)}) copy-start(bf16[64,2048]{1,0:T(8,128)(2,1)} %tok_h.1) | copy-start | bytes 786436

commit v9 on v8

--- a/solution.py
+++ b/solution.py
@@ -23,9 +23,9 @@
 ROWS = SLOTS * KVH
 BLK = 8
 NBLK = SEQS // BLK
-AHEAD = 4
-NX = 3
-NA = 7
+AHEAD = 3
+NX = 4
+NA = 6
 NW = 5
 WAHEAD = 3
 RING = 4
@@ -259,7 +259,7 @@
             k_copy(i + AHEAD).start()
             v_copy(i + AHEAD).start()
 
-        @pl.when(i + AHEAD == NBLK)
+        @pl.when(i == NBLK - 1)
         def _():
             for n in range(4):
                 wo_copy(n).start()
@@ -339,19 +339,22 @@
 
 
 def product_kernel(kv, vv, ki, vi, oa, comb_b, xrx_b, wo_v, ko, vo, part, ofin, ksem, vsem):
-    block_copies(NA, kv, vv, ko, vo, ksem, vsem)[0].start()
+    for c in block_copies(NA, kv, vv, ko, vo, ksem, vsem):
+        c.start()
     for i in range(NBLK - NX):
         last_merge(lax.axis_index('sp') // 2, comb_b, xrx_b, i, ofin, i)
     lhs = jnp.concatenate([oa[...].astype(BF16), ofin[...].astype(BF16)], axis=0)
     for n in range(4):
         part[:, n * WCH:(n + 1) * WCH] = jnp.dot(lhs, wo_v[n], preferred_element_type=F32)
-    block_copies(NA, kv, vv, ko, vo, ksem, vsem)[0].wait()
+    for c in block_copies(NA, kv, vv, ko, vo, ksem, vsem):
+        c.wait()
 
 
 def rest_kernel(kv, vv, ki, vi, ko, vo, ksem, vsem):
-    copy = block_copies(NA, kv, vv, ko, vo, ksem, vsem)[1]
-    copy.start()
-    copy.wait()
+    for c in block_copies(NA + 1, kv, vv, ko, vo, ksem, vsem):
+        c.start()
+    for c in block_copies(NA + 1, kv, vv, ko, vo, ksem, vsem):
+        c.wait()
 
 
 def write_kernel(pos_h, kv, vv, rep, comb_a, xrx, wo_v, ko, vo, nkv, oa, kva, vva, wo_a, pos_s, nkv_s, patch, ksem, vsem, psem, osem):

time: 36.9 us -> 37.4 us (1.014)
  Pallas kernels: 33.3 us -> 34.6 us
  waiting for transfers between devices: 0.41 us -> 0.01 us
  starting transfers between devices: 1.62 us -> 1.24 us
    pallas_call x1, Pallas kernels: 20.1 us -> 21.6 us  [device_step(): pl.pallas_call(attend_kernel, out_shape=(pltpu.VMEM(rows, BF16), pltpu.VM...]
    pallas_call x1, Pallas kernels: 9.94 us -> 8.68 us  [device_step(): pl.pallas_call(write_kernel, out_shape=(pltpu.HBM(rows, BF16), pltpu.HBM(...]
    pallas_call x1, Pallas kernels: 1.47 us -> 2.15 us  [device_step(): pl.pallas_call(rest_kernel, out_shape=(pltpu.HBM(rows, BF16), pltpu.HBM(r...]
    ppermute x1, starting transfers between devices: 1.59 us -> 1.13 us  [device_step(): xrx_b = lax.ppermute(comb_b, 'sp', [(0, 2), (2, 0), (1, 3), (3, 1)])]
    ppermute x1, waiting for transfers between devices: 0.41 us -> 0.01 us  [device_step(): other = lax.ppermute(part, 'sp', [(0, 1), (1, 0), (2, 3), (3, 2)])]
  transfers between devices with their start and end apart: 2 -> 2, of which waited for: 1 -> 0; matrix products, arithmetic and copies ran while one was open for 0% -> 0% of each run, Pallas kernels for 31% -> 29%
where the time goes in v9:
time: 37.4 us; the launch traced here: 37.3 us
  Pallas kernels  34.6 us (93%)
  starting transfers between devices  1.24 us (3%)
  other arithmetic  0.77 us (2%)
  between operations  0.69 us (2%)
    pallas_call x1, Pallas kernels, device_step(): pl.pallas_call(attend_kernel, out_shape=(pltpu.VMEM(rows, BF16), pltpu.VM...  21.6 us
    pallas_call x1, Pallas kernels, device_step(): pl.pallas_call(write_kernel, out_shape=(pltpu.HBM(rows, BF16), pltpu.HBM(...  8.68 us
    pallas_call x1, Pallas kernels, device_step(): pl.pallas_call(product_kernel, out_shape=(pltpu.HBM(rows, BF16), pltpu.HB...  2.17 us
    pallas_call x1, Pallas kernels, device_step(): pl.pallas_call(rest_kernel, out_shape=(pltpu.HBM(rows, BF16), pltpu.HBM(r...  2.15 us
    ppermute x1, starting transfers between devices, device_step(): xrx_b = lax.ppermute(comb_b, 'sp', [(0, 2), (2, 0), (1, 3), (3, 1)])  1.13 us
    convert_element_type x1, other arithmetic, device_step(): block_out = (tokens.astype(F32) + (part + other)).astype(BF16)  0.77 us
  transfers between devices with their start and end apart: 2, of which 0 were waited for; matrix products, arithmetic and copies ran while one was open for 0% of the time, Pallas kernels for 29%

profile of v9, /device:TPU:0, one launch (start us, length us, event | category | flops | bytes accessed | tf_op | source)
XLA Modules:
  0.0 37.3 jit_solution(11217129839630186559)
XLA Ops:
  0.6 21.6 %attend.1 = (bf16[64,1024,128]{2,1,0:T(8,128)(2,1)S(1)}, bf16[64,1024,128]{2,1,0:T(8,128)(2,1)S(1)}, f32[2,256,128]{2,1,0:T(8,128)S(1)}, bf16[4,2048,512]{2,1,0:...) custom-call(s32[64]{0:T(128)} %pos_h.3, ...), custom_call_target="tpu_custom_call" | custom-call | tf_op jit(solution)/shard_map/attend/pallas_call | solution.py:434
  22.2 1.1 %collective-permute-start = (f32[4,136,128]{2,1,0:T(8,128)S(1)}, f32[4,136,128]{2,1,0:T(8,128)S(1)}, u32[]{:S(2)}, u32[]{:S(2)}) collective-permute-start(f32[4,136,128]{2,1,0:T(8,128)S(1)} %get-tuple-element.34.comb_b), channel_id=1, source_target_pairs={{0,2},{2,0},{1,3},{3,1},{4,6},{6,4},{5,7},{7,5}} | collective-permute-start | bytes 835592 | tf_op jit(solution)/shard_map/ppermute | solution.py:461
  23.3 8.7 %write.1 = (bf16[64,1024,128]{2,1,0:T(8,128)(2,1)}, bf16[64,1024,128]{2,1,0:T(8,128)(2,1)}, bf16[64,8,128]{2,1,0:T(8,128)(2,1)}, f32[32,2048]{1,0:T(8,128)S(1)},...) custom-call(s32[64]{0:T(128)} %pos_h.3, ...), custom_call_target="tpu_custom_call", output_to_operand_aliasing={{4}: (1, {}), {5}: (2, {}), {6}: (6, {})} | custom-call | flops 10000000000 | bytes 33554432 | tf_op jit(solution)/shard_map/write/pallas_call | solution.py:462
  32.0 0.0 collective-permute-done.xrx_b
  32.0 2.2 %product.1 = (bf16[64,1024,128]{2,1,0:T(8,128)(2,1)}, bf16[64,1024,128]{2,1,0:T(8,128)(2,1)}, f32[64,2048]{1,0:T(8,128)S(1)}) custom-call(bf16[64,1024,128]{2,1,0:T(8,128)(2,1)S(1)} %get-tuple-element.29.kv, bf16[64,1024,128]{2,1,0:T(8,128)(2,1)S(1)} %get-tuple-element.30.vv, ...), custom_call_target="tpu_custom_call", output_to_operand_aliasing={{0}: (2, {}), {1}: (3, {})} | custom-call | flops 536870912 | bytes 4194304 | tf_op jit(solution)/shard_map/product/pallas_call | solution.py:477
  34.2 0.1 collective-permute-start.1
  34.3 0.0 copy-start
  34.3 2.1 %rest.1 = (bf16[64,1024,128]{2,1,0:T(8,128)(2,1)}, bf16[64,1024,128]{2,1,0:T(8,128)(2,1)}) custom-call(bf16[64,1024,128]{2,1,0:T(8,128)(2,1)S(1)} %get-tuple-element.29.kv, bf16[64,1024,128]{2,1,0:T(8,128)(2,1)S(1)} %get-tuple-element.30.vv, bf16[64,1024,128]{2,1,0:T(8,128)(2,1)} %get-tuple-element.37.ki, ...), custom_call_target="tpu_custom_call", output_to_operand_aliasing={{0}: (2, {}), {1}: (3, {})} | custom-call | flops 1000000000 | bytes 4194304 | tf_op jit(solution)/shard_map/rest/pallas_call | solution.py:489
  36.5 0.0 collective-permute-done.1
  36.5 0.0 copy-done
  36.5 0.8 %add_convert_fusion = bf16[64,2048]{1,0:T(8,128)(2,1)} fusion(f32[64,2048]{1,0:T(8,128)S(1)} %get-tuple-element.36, f32[64,2048]{1,0:T(8,128)S(1)} %collective-permute-done.1, bf16[64,2048]{1,0:T(8,128)(2,1)S(1)} %copy-done), kind=kLoop, calls=%fused_computation | loop fusion | flops 524288 | bytes 1572864 | tf_op jit(solution)/shard_map/convert_element_type | solution.py:500
Async XLA Ops:
  22.2 9.8 %collective-permute-start = (f32[4,136,128]{2,1,0:T(8,128)S(1)}, f32[4,136,128]{2,1,0:T(8,128)S(1)}, u32[]{:S(2)}, u32[]{:S(2)}) collective-permute-start(f32[4,136,128]{2,1,0:T(8,128)S(1)} %get-tuple-element.34.comb_b), channel_id=1, source_target_pairs={{0,2},{2,0},{1,3},{3,1},{4,6},{6,4},{5,7},{7,5}} | collective-permute-start | bytes 835592 | tf_op jit(solution)/shard_map/ppermute | solution.py:461
  34.2 2.3 %collective-permute-start.1 = (f32[64,2048]{1,0:T(8,128)S(1)}, f32[64,2048]{1,0:T(8,128)S(1)}, u32[]{:S(2)}, u32[]{:S(2)}) collective-permute-start(f32[64,2048]{1,0:T(8,128)S(1)} %get-tuple-element.36), channel_id=1, source_target_pairs={{0,1},{1,0},{2,3},{3,2},{4,5},{5,4},{6,7},{7,6}} | collective-permute-start | bytes 1572872 | tf_op jit(solution)/shard_map/ppermute | solution.py:488
  34.3 2.2 %copy-start = (bf16[64,2048]{1,0:T(8,128)(2,1)S(1)}, bf16[64,2048]{1,0:T(8,128)(2,1)}, u32[]{:S(2)}) copy-start(bf16[64,2048]{1,0:T(8,128)(2,1)} %tok_h.1) | copy-start | bytes 786436

commit v10 on v9

--- a/solution.py
+++ b/solution.py
@@ -23,15 +23,17 @@
 ROWS = SLOTS * KVH
 BLK = 8
 NBLK = SEQS // BLK
-AHEAD = 3
-NX = 4
+AHEAD = 5
+NX = 8
 NA = 6
 NW = 5
 WAHEAD = 3
 RING = 4
-LAG = 2
+LAG = 3
 WCH = 512
-PIECE = (HALF + 1) * BLK
+CB = 4
+NCB = SEQS // CB
+PIECE = HALF * CB + 8
 VMEM_LIMIT = 14 * 2**20
 EXP_SCALE = HD ** -0.5 * 1.4426950408889634
 NEG = -jnp.inf
@@ -73,10 +75,10 @@
         return pltpu.make_async_copy(src, wo_v.at[n], wosem.at[n])
 
     def k_copy(i):
-        return pltpu.make_async_copy(kc.at[pl.ds(i * BLK, BLK)], kv.at[pl.ds(i * BLK, BLK)], ksem.at[i])
+        return pltpu.make_async_copy(kc.at[pl.ds(i * CB, CB)], kv.at[pl.ds(i * CB, CB)], ksem.at[i])
 
     def v_copy(i):
-        return pltpu.make_async_copy(vc.at[pl.ds(i * BLK, BLK)], vv.at[pl.ds(i * BLK, BLK)], vsem.at[i])
+        return pltpu.make_async_copy(vc.at[pl.ds(i * CB, CB)], vv.at[pl.ds(i * CB, CB)], vsem.at[i])
 
     def q_send(h):
         return pltpu.make_async_remote_copy(qmine.at[h], qmate.at[h], qs.at[h], qr.at[h], device_id=mate, device_id_type=MESH)
@@ -149,7 +151,7 @@
         w_copy(n, wk).wait()
         if n + WAHEAD < NW:
             w_start(n + WAHEAD)
-        elif n + WAHEAD - NW < AHEAD:
+        else:
             k_copy(n + WAHEAD - NW).start()
             v_copy(n + WAHEAD - NW).start()
         proj[n % 2] = jnp.dot(hid[...], w_s[n % RING], preferred_element_type=F32)
@@ -160,7 +162,7 @@
             q_send(0).start()
         if n == 4:
             q_send(1).start()
-    for i in range(min(WAHEAD, AHEAD), AHEAD):
+    for i in range(WAHEAD, AHEAD):
         k_copy(i).start()
         v_copy(i).start()
     post(NW - 1)
@@ -168,7 +170,7 @@
     start = me * SLOTS
     lane = lax.broadcasted_iota(jnp.int32, (HALF, HD), 1)
     lrow = lax.broadcasted_iota(jnp.int32, (HALF, HD), 0)
-    lane8 = lax.broadcasted_iota(jnp.int32, (BLK, HD), 1)
+    lane8 = lax.broadcasted_iota(jnp.int32, (8, HD), 1)
     for h in range(2):
         q_send(h).wait()
     new_send().wait()
@@ -176,7 +178,7 @@
     def attend(i, first=False):
         ob = opart.at[i]
         def load_q(pair, at):
-            bs = [at * BLK + 2 * pair + z for z in range(2)]
+            bs = [at * CB + 2 * pair + z for z in range(2)]
             return bs, [jnp.concatenate([ref[h, pl.ds(pl.multiple_of(b * 8, 8), 8), :]
                                          for ref in (qmine, qmate) for h in range(2)], axis=0) for b in bs]
 
@@ -210,7 +212,7 @@
             return out
 
         def mix(pair, st3):
-            bs = [i * BLK + 2 * pair + z for z in range(2)]
+            bs = [i * CB + 2 * pair + z for z in range(2)]
             values = jnp.concatenate([vv[bs[0]], vv[bs[1]]], axis=1)
             mixed = jnp.dot(pr_s[pair % 2], values, preferred_element_type=F32)
             for z in range(2):
@@ -219,47 +221,49 @@
                 bb = 2 * pair + z
                 for h in range(2):
                     hs = slice(h * HALF, (h + 1) * HALF)
-                    ob[pl.ds(h * PIECE + bb, HALF, stride=BLK), :] = o[hs]
-                    st = jnp.where(lane == lrow, peak[hs], jnp.where(lane == lrow + HALF, total[hs], 0.0))
-                    ob[pl.ds(h * PIECE + HALF * BLK + bb, 1), :] = jnp.sum(st, axis=0, keepdims=True)
+                    ob[pl.ds(h * PIECE + bb, HALF, stride=CB), :] = o[hs]
+                    st = jnp.where(lane == lrow // 2, peak[hs], jnp.where(lane == lrow // 2 + HALF // 2, total[hs], 0.0))
+                    for w in range(2):
+                        ob[pl.ds(h * PIECE + HALF * CB + w * CB + bb, 1), :] = jnp.sum(
+                            jnp.where(lrow % 2 == w, st, 0.0), axis=0, keepdims=True)
 
         if first:
             scores(0, i)
             return
-        for pair in range(BLK // 2):
-            if pair + 1 < BLK // 2:
+        for pair in range(CB // 2):
+            if pair + 1 < CB // 2:
                 scores(pair + 1, i)
             else:
-                scores(0, jnp.minimum(i + 1, NBLK - 1))
+                scores(0, jnp.minimum(i + 1, NCB - 1))
             mix(pair, soft(pair))
 
     def combine(i, comb, at):
-        s0 = opart[i, pl.ds(HALF * BLK, BLK), :]
-        s1 = drx[i, pl.ds(HALF * BLK, BLK), :]
+        s0 = opart[i, pl.ds(HALF * CB, 8), :]
+        s1 = drx[i, pl.ds(HALF * CB, 8), :]
         peak = jnp.maximum(s0, s1)
         safe = jnp.where(peak == NEG, 0.0, peak)
         f0 = jnp.exp2((s0 - safe) * EXP_SCALE)
         f1 = jnp.exp2((s1 - safe) * EXP_SCALE)
-        total = f0 * pltpu.roll(s0, HD - HALF, 1) + f1 * pltpu.roll(s1, HD - HALF, 1)
-        comb[at, pl.ds(HALF * BLK, BLK), :] = jnp.where(
-            lane8 < HALF, peak, jnp.where(lane8 < 2 * HALF, pltpu.roll(total, HALF, 1), 0.0))
-        for j in range(HALF):
-            rows = pl.ds(j * BLK, BLK)
-            comb[at, rows, :] = bcast_col(f0, j) * opart[i, rows, :] + bcast_col(f1, j) * drx[i, rows, :]
+        total = f0 * pltpu.roll(s0, HD - HALF // 2, 1) + f1 * pltpu.roll(s1, HD - HALF // 2, 1)
+        comb[at, pl.ds(HALF * CB, 8), :] = jnp.where(
+            lane8 < HALF // 2, peak, jnp.where(lane8 < HALF, pltpu.roll(total, HALF // 2, 1), 0.0))
+        for u in range(HALF // 2):
+            rows = pl.ds(u * 8, 8)
+            comb[at, rows, :] = bcast_col(f0, u) * opart[i, rows, :] + bcast_col(f1, u) * drx[i, rows, :]
 
     def fetch(i):
-        @pl.when(i + 1 < NBLK)
+        @pl.when(i + 1 < NCB)
         def _():
             k_copy(i + 1).wait()
 
         v_copy(i).wait()
 
-        @pl.when(i + AHEAD < NBLK)
+        @pl.when(i + AHEAD < NCB)
         def _():
             k_copy(i + AHEAD).start()
             v_copy(i + AHEAD).start()
 
-        @pl.when(i == NBLK - 1)
+        @pl.when(i == NCB - 1)
         def _():
             for n in range(4):
                 wo_copy(n).start()
@@ -296,8 +300,8 @@
     attend(0, first=True)
     lax.fori_loop(0, LAG, early, 0)
     lax.fori_loop(LAG, LAG + NX, sending, 0)
-    lax.fori_loop(LAG + NX, NBLK, keeping, 0)
-    lax.fori_loop(NBLK - LAG, NBLK, late, 0)
+    lax.fori_loop(LAG + NX, NCB, keeping, 0)
+    lax.fori_loop(NCB - LAG, NCB, late, 0)
 
     for n in range(4):
         wo_copy(n).wait()
@@ -310,7 +314,7 @@
         x_send(i).wait()
         return carry
 
-    lax.fori_loop(0, NBLK, drain, 0)
+    lax.fori_loop(0, NCB, drain, 0)
     lax.fori_loop(0, NX, drain_x, 0)
 
 
@@ -321,15 +325,18 @@
         mine, other = comb[i, rows, :], other_ref[i, rows, :]
         return jnp.where(first, mine, other), jnp.where(first, other, mine)
 
-    s0, s1 = ordered(pl.ds(HALF * BLK, BLK))
+    s0, s1 = ordered(pl.ds(HALF * CB, 8))
     peak = jnp.maximum(s0, s1)
     f0 = jnp.exp2((s0 - peak) * EXP_SCALE)
     f1 = jnp.exp2((s1 - peak) * EXP_SCALE)
-    total = f0 * pltpu.roll(s0, HD - HALF, 1) + f1 * pltpu.roll(s1, HD - HALF, 1)
+    total = f0 * pltpu.roll(s0, HD - HALF // 2, 1) + f1 * pltpu.roll(s1, HD - HALF // 2, 1)
     g0, g1 = f0 / total, f1 / total
-    for j in range(HALF):
-        a, b = ordered(pl.ds(j * BLK, BLK))
-        ofin[at * BLK:(at + 1) * BLK, j * HD:(j + 1) * HD] = bcast_col(g0, j) * a + bcast_col(g1, j) * b
+    for u in range(HALF // 2):
+        a, b = ordered(pl.ds(u * 8, 8))
+        o = bcast_col(g0, u) * a + bcast_col(g1, u) * b
+        for w in range(2):
+            j = 2 * u + w
+            ofin[at * CB:(at + 1) * CB, j * HD:(j + 1) * HD] = o[w * CB:(w + 1) * CB]
 
 
 def block_copies(i, kv, vv, ko, vo, ksem, vsem):
@@ -341,7 +348,7 @@
 def product_kernel(kv, vv, ki, vi, oa, comb_b, xrx_b, wo_v, ko, vo, part, ofin, ksem, vsem):
     for c in block_copies(NA, kv, vv, ko, vo, ksem, vsem):
         c.start()
-    for i in range(NBLK - NX):
+    for i in range(NCB - NX):
         last_merge(lax.axis_index('sp') // 2, comb_b, xrx_b, i, ofin, i)
     lhs = jnp.concatenate([oa[...].astype(BF16), ofin[...].astype(BF16)], axis=0)
     for n in range(4):
@@ -435,7 +442,7 @@
             attend_kernel,
             out_shape=(pltpu.VMEM(rows, BF16), pltpu.VMEM(rows, BF16),
                        pltpu.VMEM((2, SEQS * KVH, HD), F32), pltpu.VMEM((4, HALF * HD, WCH), BF16),
-                       pltpu.VMEM((NX,) + piece, F32), pltpu.VMEM((NBLK - NX,) + piece, F32), pltpu.VMEM((NX,) + piece, F32)),
+                       pltpu.VMEM((NX,) + piece, F32), pltpu.VMEM((NCB - NX,) + piece, F32), pltpu.VMEM((NX,) + piece, F32)),
             in_specs=[hbm] * 12,
             out_specs=(vm,) * 7,
             scratch_shapes=[
@@ -447,11 +454,11 @@
                 pltpu.VMEM((SEQS, HD), F32), pltpu.VMEM((SEQS, HD), F32), pltpu.VMEM((SEQS, HD), F32),
                 pltpu.VMEM((2, SEQS * 8, HD), F32), pltpu.VMEM((2, SEQS * 8, HD), F32),
                 pltpu.VMEM((2 * HALF, ROWS), jnp.int32),
-                pltpu.VMEM((NBLK, 2 * PIECE, HD), F32),
-                pltpu.VMEM((NBLK,) + piece, F32),
+                pltpu.VMEM((NCB, 2 * PIECE, HD), F32),
+                pltpu.VMEM((NCB,) + piece, F32),
                 pltpu.VMEM((2, 4 * HALF, ROWS), F32), pltpu.VMEM((2, 4 * HALF, ROWS), BF16),
-                dma((NW,)), dma((NBLK,)), dma((NBLK,)), dma((4,)), dma((3,)), dma((3,)),
-                dma((NBLK,)), dma((NBLK,)), dma((NX,)), dma((NX,)),
+                dma((NW,)), dma((NCB,)), dma((NCB,)), dma((4,)), dma((3,)), dma((3,)),
+                dma((NCB,)), dma((NCB,)), dma((NX,)), dma((NX,)),
             ],
             compiler_params=pltpu.CompilerParams(collective_id=0, has_side_effects=True, vmem_limit_bytes=VMEM_LIMIT),
             name='attend',
@@ -462,7 +469,7 @@
         k_out, v_out, new_kv, oa, kv, vv, wo_v = pl.pallas_call(
             write_kernel,
             out_shape=(pltpu.HBM(rows, BF16), pltpu.HBM(rows, BF16), pltpu.HBM((SEQS, 2 * KVH, HD), BF16),
-                       pltpu.VMEM((NX * BLK, HALF * HD), F32), pltpu.VMEM(rows, BF16), pltpu.VMEM(rows, BF16),
+                       pltpu.VMEM((NX * CB, HALF * HD), F32), pltpu.VMEM(rows, BF16), pltpu.VMEM(rows, BF16),
                        pltpu.VMEM((4, HALF * HD, WCH), BF16)),
             in_specs=[hbm, vm, vm, vm, vm, vm, vm],
             out_specs=(hbm, hbm, hbm, vm, vm, vm, vm),
@@ -480,7 +487,7 @@
             in_specs=[vm, vm, hbm, hbm, vm, vm, vm, vm],
             out_specs=(hbm, hbm, vm),
             input_output_aliases={2: 0, 3: 1},
-            scratch_shapes=[pltpu.VMEM(((NBLK - NX) * BLK, HALF * HD), F32), dma((NBLK,)), dma((NBLK,))],
+            scratch_shapes=[pltpu.VMEM(((NCB - NX) * CB, HALF * HD), F32), dma((NBLK,)), dma((NBLK,))],
             compiler_params=pltpu.CompilerParams(vmem_limit_bytes=VMEM_LIMIT),
             cost_estimate=pl.CostEstimate(flops=2 * SEQS * DIM * DIM, bytes_accessed=2**22, transcendentals=0),
             name='product',

time: 37.4 us -> 39.4 us (1.053)
  starting transfers between devices: 1.24 us -> 2.76 us
  Pallas kernels: 34.6 us -> 35.1 us
    ppermute x1, starting transfers between devices: 1.13 us -> 2.64 us  [device_step(): xrx_b = lax.ppermute(comb_b, 'sp', [(0, 2), (2, 0), (1, 3), (3, 1)])]
    pallas_call x1, Pallas kernels: 21.6 us -> 22.1 us  [device_step(): pl.pallas_call(attend_kernel, out_shape=(pltpu.VMEM(rows, BF16), pltpu.VM...]
  transfers between devices with their start and end apart: 2 -> 2, of which waited for: 0 -> 0; matrix products, arithmetic and copies ran while one was open for 0% -> 0% of each run, Pallas kernels for 29% -> 28%
where the time goes in v10:
time: 39.4 us; the launch traced here: 39.3 us
  Pallas kernels  35.1 us (89%)
  starting transfers between devices  2.76 us (7%)
  other arithmetic  0.77 us (2%)
  between operations  0.69 us (2%)
    pallas_call x1, Pallas kernels, device_step(): pl.pallas_call(attend_kernel, out_shape=(pltpu.VMEM(rows, BF16), pltpu.VM...  22.1 us
    pallas_call x1, Pallas kernels, device_step(): pl.pallas_call(write_kernel, out_shape=(pltpu.HBM(rows, BF16), pltpu.HBM(...  8.68 us
    ppermute x1, starting transfers between devices, device_step(): xrx_b = lax.ppermute(comb_b, 'sp', [(0, 2), (2, 0), (1, 3), (3, 1)])  2.64 us
    pallas_call x1, Pallas kernels, device_step(): pl.pallas_call(product_kernel, out_shape=(pltpu.HBM(rows, BF16), pltpu.HB...  2.17 us
    pallas_call x1, Pallas kernels, device_step(): pl.pallas_call(rest_kernel, out_shape=(pltpu.HBM(rows, BF16), pltpu.HBM(r...  2.15 us
  transfers between devices with their start and end apart: 2, of which 0 were waited for; matrix products, arithmetic and copies ran while one was open for 0% of the time, Pallas kernels for 28%

profile of v10, /device:TPU:0, one launch (start us, length us, event | category | flops | bytes accessed | tf_op | source)
XLA Modules:
  0.0 39.3 jit_solution(2779925534514716981)
XLA Ops:
  0.6 22.1 %attend.1 = (bf16[64,1024,128]{2,1,0:T(8,128)(2,1)S(1)}, bf16[64,1024,128]{2,1,0:T(8,128)(2,1)S(1)}, f32[2,256,128]{2,1,0:T(8,128)S(1)}, bf16[4,2048,512]{2,1,0:...) custom-call(s32[64]{0:T(128)} %pos_h.3, ...), custom_call_target="tpu_custom_call" | custom-call | tf_op jit(solution)/shard_map/attend/pallas_call | solution.py:441
  22.7 2.6 %collective-permute-start = (f32[8,72,128]{2,1,0:T(8,128)S(1)}, f32[8,72,128]{2,1,0:T(8,128)S(1)}, u32[]{:S(2)}, u32[]{:S(2)}) collective-permute-start(f32[8,72,128]{2,1,0:T(8,128)S(1)} %get-tuple-element.34.comb_b), channel_id=1, source_target_pairs={{0,2},{2,0},{1,3},{3,1},{4,6},{6,4},{5,7},{7,5}} | collective-permute-start | bytes 884744 | tf_op jit(solution)/shard_map/ppermute | solution.py:468
  25.4 8.7 %write.1 = (bf16[64,1024,128]{2,1,0:T(8,128)(2,1)}, bf16[64,1024,128]{2,1,0:T(8,128)(2,1)}, bf16[64,8,128]{2,1,0:T(8,128)(2,1)}, f32[32,2048]{1,0:T(8,128)S(1)},...) custom-call(s32[64]{0:T(128)} %pos_h.3, ...), custom_call_target="tpu_custom_call", output_to_operand_aliasing={{4}: (1, {}), {5}: (2, {}), {6}: (6, {})} | custom-call | flops 10000000000 | bytes 33554432 | tf_op jit(solution)/shard_map/write/pallas_call | solution.py:469
  34.1 0.0 collective-permute-done.xrx_b
  34.1 2.2 %product.1 = (bf16[64,1024,128]{2,1,0:T(8,128)(2,1)}, bf16[64,1024,128]{2,1,0:T(8,128)(2,1)}, f32[64,2048]{1,0:T(8,128)S(1)}) custom-call(bf16[64,1024,128]{2,1,0:T(8,128)(2,1)S(1)} %get-tuple-element.29.kv, bf16[64,1024,128]{2,1,0:T(8,128)(2,1)S(1)} %get-tuple-element.30.vv, ...), custom_call_target="tpu_custom_call", output_to_operand_aliasing={{0}: (2, {}), {1}: (3, {})} | custom-call | flops 536870912 | bytes 4194304 | tf_op jit(solution)/shard_map/product/pallas_call | solution.py:484
  36.3 0.1 collective-permute-start.1
  36.4 0.0 copy-start
  36.4 2.1 %rest.1 = (bf16[64,1024,128]{2,1,0:T(8,128)(2,1)}, bf16[64,1024,128]{2,1,0:T(8,128)(2,1)}) custom-call(bf16[64,1024,128]{2,1,0:T(8,128)(2,1)S(1)} %get-tuple-element.29.kv, bf16[64,1024,128]{2,1,0:T(8,128)(2,1)S(1)} %get-tuple-element.30.vv, bf16[64,1024,128]{2,1,0:T(8,128)(2,1)} %get-tuple-element.37.ki, ...), custom_call_target="tpu_custom_call", output_to_operand_aliasing={{0}: (2, {}), {1}: (3, {})} | custom-call | flops 1000000000 | bytes 4194304 | tf_op jit(solution)/shard_map/rest/pallas_call | solution.py:496
  38.5 0.0 collective-permute-done.1
  38.5 0.0 copy-done
  38.6 0.8 %add_convert_fusion = bf16[64,2048]{1,0:T(8,128)(2,1)} fusion(f32[64,2048]{1,0:T(8,128)S(1)} %get-tuple-element.36, f32[64,2048]{1,0:T(8,128)S(1)} %collective-permute-done.1, bf16[64,2048]{1,0:T(8,128)(2,1)S(1)} %copy-done), kind=kLoop, calls=%fused_computation | loop fusion | flops 524288 | bytes 1572864 | tf_op jit(solution)/shard_map/convert_element_type | solution.py:507
Async XLA Ops:
  22.7 11.3 %collective-permute-start = (f32[8,72,128]{2,1,0:T(8,128)S(1)}, f32[8,72,128]{2,1,0:T(8,128)S(1)}, u32[]{:S(2)}, u32[]{:S(2)}) collective-permute-start(f32[8,72,128]{2,1,0:T(8,128)S(1)} %get-tuple-element.34.comb_b), channel_id=1, source_target_pairs={{0,2},{2,0},{1,3},{3,1},{4,6},{6,4},{5,7},{7,5}} | collective-permute-start | bytes 884744 | tf_op jit(solution)/shard_map/ppermute | solution.py:468
  36.3 2.3 %collective-permute-start.1 = (f32[64,2048]{1,0:T(8,128)S(1)}, f32[64,2048]{1,0:T(8,128)S(1)}, u32[]{:S(2)}, u32[]{:S(2)}) collective-permute-start(f32[64,2048]{1,0:T(8,128)S(1)} %get-tuple-element.36), channel_id=1, source_target_pairs={{0,1},{1,0},{2,3},{3,2},{4,5},{5,4},{6,7},{7,6}} | collective-permute-start | bytes 1572872 | tf_op jit(solution)/shard_map/ppermute | solution.py:495
  36.4 2.2 %copy-start = (bf16[64,2048]{1,0:T(8,128)(2,1)S(1)}, bf16[64,2048]{1,0:T(8,128)(2,1)}, u32[]{:S(2)}) copy-start(bf16[64,2048]{1,0:T(8,128)(2,1)} %tok_h.1) | copy-start | bytes 786436

commit v11 on v9

--- a/solution.py
+++ b/solution.py
@@ -93,7 +93,7 @@
                                             device_id=peer, device_id_type=MESH)
 
     small = [pltpu.make_async_copy(a, b, insem.at[z]) for z, (a, b) in enumerate(
-        ((tok_h, tok), (pos_h, pos_s), (an_h, an), (qn_h, qn), (kn_h, kn), (freq_h, freq)))]
+        ((tok_h, tok), (an_h, an), (pos_h, pos_s), (qn_h, qn), (kn_h, kn), (freq_h, freq)))]
     for c in small:
         c.start()
     for n in range(WAHEAD):
@@ -103,25 +103,8 @@
     for other in (mate, peer):
         pl.semaphore_signal(barrier, inc=1, device_id=other, device_id_type=MESH)
 
-    for c in small[1:]:
-        c.wait()
-    lane1 = lax.broadcasted_iota(jnp.int32, (1, HD), 1)
-
-    def angle(b, carry):
-        ang[pl.ds(b, 1), :] = freq[...] * pos_s[b].astype(F32)
-        return carry
-
-    lax.fori_loop(0, SEQS, angle, 0, unroll=8)
-    cosr[...] = jnp.cos(ang[...])
-    sinr[...] = jnp.sin(ang[...]) * jnp.where(lane1 < HD // 2, -1.0, 1.0)
-
-    row = lax.broadcasted_iota(jnp.int32, (2 * HALF, ROWS), 0)
-    col = lax.broadcasted_iota(jnp.int32, (2 * HALF, ROWS), 1)
-    half_of_row = jnp.where(row < HALF, core, 1 - core)
-    kv_of_row = half_of_row * 2 + lax.rem(row, HALF) // 8
-    colslot[...] = jnp.where(lax.rem(col, KVH) == kv_of_row, col // KVH, 1 << 20)
-
     small[0].wait()
+    small[1].wait()
     t = tok[...].astype(F32)
     inv = lax.rsqrt(jnp.sum(t * t, axis=-1, keepdims=True) * (1.0 / DIM) + NORM_EPS)
     gains = an[...].astype(F32)
@@ -129,8 +112,24 @@
         sl = slice(j * HD, (j + 1) * HD)
         hid[:, sl] = (tok[:, sl].astype(F32) * inv * gains[j:j + 1, :]).astype(BF16)
 
-    qgain = qn[...].astype(F32)
-    kgain = kn[...].astype(F32)
+    def tables():
+        for c in small[2:]:
+            c.wait()
+        lane1 = lax.broadcasted_iota(jnp.int32, (1, HD), 1)
+
+        def angle(b, carry):
+            ang[pl.ds(b, 1), :] = freq[...] * pos_s[b].astype(F32)
+            return carry
+
+        lax.fori_loop(0, SEQS, angle, 0, unroll=8)
+        cosr[...] = jnp.cos(ang[...])
+        sinr[...] = jnp.sin(ang[...]) * jnp.where(lane1 < HD // 2, -1.0, 1.0)
+
+        row = lax.broadcasted_iota(jnp.int32, (2 * HALF, ROWS), 0)
+        col = lax.broadcasted_iota(jnp.int32, (2 * HALF, ROWS), 1)
+        half_of_row = jnp.where(row < HALF, core, 1 - core)
+        kv_of_row = half_of_row * 2 + lax.rem(row, HALF) // 8
+        colslot[...] = jnp.where(lax.rem(col, KVH) == kv_of_row, col // KVH, 1 << 20)
 
     def norm_rope(x, gain):
         y = x * lax.rsqrt(jnp.mean(x * x, axis=-1, keepdims=True) + NORM_EPS) * gain
@@ -145,25 +144,34 @@
             else:
                 rep.at[core][pl.ds(j, SEQS, stride=KVH), :] = jnp.where(core == 0, norm_rope(x, kgain), x)
 
-    for n in range(NW):
+    def multiply(n):
         w_copy(n, wk).wait()
         if n + WAHEAD < NW:
             w_start(n + WAHEAD)
-        elif n + WAHEAD - NW < AHEAD:
-            k_copy(n + WAHEAD - NW).start()
-            v_copy(n + WAHEAD - NW).start()
+        elif n >= NW - 2:
+            k_copy(n - NW + 2).start()
+            v_copy(n - NW + 2).start()
         proj[n % 2] = jnp.dot(hid[...], w_s[n % RING], preferred_element_type=F32)
-        if n > 0:
-            post(n - 1)
-        if n == 2:
-            pl.semaphore_wait(barrier, 2)
-            q_send(0).start()
-        if n == 4:
-            q_send(1).start()
-    for i in range(min(WAHEAD, AHEAD), AHEAD):
+
+    multiply(0)
+    tables()
+    qgain = qn[...].astype(F32)
+    kgain = kn[...].astype(F32)
+    multiply(1)
+    post(0)
+    multiply(2)
+    post(1)
+    pl.semaphore_wait(barrier, 2)
+    q_send(0).start()
+    multiply(3)
+    post(2)
+    post(3)
+    q_send(1).start()
+    multiply(4)
+    for i in range(2, AHEAD):
         k_copy(i).start()
         v_copy(i).start()
-    post(NW - 1)
+    post(4)
     new_send().start()
     start = me * SLOTS
     lane = lax.broadcasted_iota(jnp.int32, (HALF, HD), 1)
@@ -171,7 +179,6 @@
     lane8 = lax.broadcasted_iota(jnp.int32, (BLK, HD), 1)
     for h in range(2):
         q_send(h).wait()
-    new_send().wait()
 
     def attend(i, first=False):
         ob = opart.at[i]
@@ -294,6 +301,7 @@
 
     k_copy(0).wait()
     attend(0, first=True)
+    new_send().wait()
     lax.fori_loop(0, LAG, early, 0)
     lax.fori_loop(LAG, LAG + NX, sending, 0)
     lax.fori_loop(LAG + NX, NBLK, keeping, 0)

time: 37.4 us -> 37.4 us (level)
  Pallas kernels: 34.6 us -> 34.2 us
  starting transfers between devices: 1.24 us -> 1.63 us
    ppermute x1, starting transfers between devices: 1.13 us -> 1.6 us  [device_step(): xrx_b = lax.ppermute(comb_b, 'sp', [(0, 2), (2, 0), (1, 3), (3, 1)])]
    pallas_call x1, Pallas kernels: 21.6 us -> 21.2 us  [device_step(): pl.pallas_call(attend_kernel, out_shape=(pltpu.VMEM(rows, BF16), pltpu.VM...]
where the time goes in v11:
time: 37.4 us; the launch traced here: 37.3 us
  Pallas kernels  34.2 us (91%)
  starting transfers between devices  1.63 us (4%)
  other arithmetic  0.77 us (2%)
  between operations  0.71 us (2%)
    pallas_call x1, Pallas kernels, device_step(): pl.pallas_call(attend_kernel, out_shape=(pltpu.VMEM(rows, BF16), pltpu.VM...  21.2 us
    pallas_call x1, Pallas kernels, device_step(): pl.pallas_call(write_kernel, out_shape=(pltpu.HBM(rows, BF16), pltpu.HBM(...  8.68 us
    pallas_call x1, Pallas kernels, device_step(): pl.pallas_call(product_kernel, out_shape=(pltpu.HBM(rows, BF16), pltpu.HB...  2.17 us
    pallas_call x1, Pallas kernels, device_step(): pl.pallas_call(rest_kernel, out_shape=(pltpu.HBM(rows, BF16), pltpu.HBM(r...  2.16 us
    ppermute x1, starting transfers between devices, device_step(): xrx_b = lax.ppermute(comb_b, 'sp', [(0, 2), (2, 0), (1, 3), (3, 1)])  1.6 us
    convert_element_type x1, other arithmetic, device_step(): block_out = (tokens.astype(F32) + (part + other)).astype(BF16)  0.77 us
  transfers between devices with their start and end apart: 2, of which 0 were waited for; matrix products, arithmetic and copies ran while one was open for 0% of the time, Pallas kernels for 29%

profile of v11, /device:TPU:0, one launch (start us, length us, event | category | flops | bytes accessed | tf_op | source)
XLA Modules:
  0.0 37.3 jit_solution(4601083833140368850)
XLA Ops:
  0.6 21.2 %attend.1 = (bf16[64,1024,128]{2,1,0:T(8,128)(2,1)S(1)}, bf16[64,1024,128]{2,1,0:T(8,128)(2,1)S(1)}, f32[2,256,128]{2,1,0:T(8,128)S(1)}, bf16[4,2048,512]{2,1,0:...) custom-call(s32[64]{0:T(128)} %pos_h.3, ...), custom_call_target="tpu_custom_call" | custom-call | tf_op jit(solution)/shard_map/attend/pallas_call | solution.py:442
  21.8 1.6 %collective-permute-start = (f32[4,136,128]{2,1,0:T(8,128)S(1)}, f32[4,136,128]{2,1,0:T(8,128)S(1)}, u32[]{:S(2)}, u32[]{:S(2)}) collective-permute-start(f32[4,136,128]{2,1,0:T(8,128)S(1)} %get-tuple-element.34.comb_b), channel_id=1, source_target_pairs={{0,2},{2,0},{1,3},{3,1},{4,6},{6,4},{5,7},{7,5}} | collective-permute-start | bytes 835592 | tf_op jit(solution)/shard_map/ppermute | solution.py:469
  23.4 8.7 %write.1 = (bf16[64,1024,128]{2,1,0:T(8,128)(2,1)}, bf16[64,1024,128]{2,1,0:T(8,128)(2,1)}, bf16[64,8,128]{2,1,0:T(8,128)(2,1)}, f32[32,2048]{1,0:T(8,128)S(1)},...) custom-call(s32[64]{0:T(128)} %pos_h.3, ...), custom_call_target="tpu_custom_call", output_to_operand_aliasing={{4}: (1, {}), {5}: (2, {}), {6}: (6, {})} | custom-call | flops 10000000000 | bytes 33554432 | tf_op jit(solution)/shard_map/write/pallas_call | solution.py:470
  32.1 0.0 collective-permute-done.xrx_b
  32.1 2.2 %product.1 = (bf16[64,1024,128]{2,1,0:T(8,128)(2,1)}, bf16[64,1024,128]{2,1,0:T(8,128)(2,1)}, f32[64,2048]{1,0:T(8,128)S(1)}) custom-call(bf16[64,1024,128]{2,1,0:T(8,128)(2,1)S(1)} %get-tuple-element.29.kv, bf16[64,1024,128]{2,1,0:T(8,128)(2,1)S(1)} %get-tuple-element.30.vv, ...), custom_call_target="tpu_custom_call", output_to_operand_aliasing={{0}: (2, {}), {1}: (3, {})} | custom-call | flops 536870912 | bytes 4194304 | tf_op jit(solution)/shard_map/product/pallas_call | solution.py:485
  34.3 0.0 collective-permute-start.1
  34.3 0.0 copy-start
  34.3 2.2 %rest.1 = (bf16[64,1024,128]{2,1,0:T(8,128)(2,1)}, bf16[64,1024,128]{2,1,0:T(8,128)(2,1)}) custom-call(bf16[64,1024,128]{2,1,0:T(8,128)(2,1)S(1)} %get-tuple-element.29.kv, bf16[64,1024,128]{2,1,0:T(8,128)(2,1)S(1)} %get-tuple-element.30.vv, bf16[64,1024,128]{2,1,0:T(8,128)(2,1)} %get-tuple-element.37.ki, ...), custom_call_target="tpu_custom_call", output_to_operand_aliasing={{0}: (2, {}), {1}: (3, {})} | custom-call | flops 1000000000 | bytes 4194304 | tf_op jit(solution)/shard_map/rest/pallas_call | solution.py:497
  36.5 0.0 collective-permute-done.1
  36.5 0.0 copy-done
  36.5 0.8 %add_convert_fusion = bf16[64,2048]{1,0:T(8,128)(2,1)} fusion(f32[64,2048]{1,0:T(8,128)S(1)} %get-tuple-element.36, f32[64,2048]{1,0:T(8,128)S(1)} %collective-permute-done.1, bf16[64,2048]{1,0:T(8,128)(2,1)S(1)} %copy-done), kind=kLoop, calls=%fused_computation | loop fusion | flops 524288 | bytes 1572864 | tf_op jit(solution)/shard_map/convert_element_type | solution.py:508
Async XLA Ops:
  21.8 10.3 %collective-permute-start = (f32[4,136,128]{2,1,0:T(8,128)S(1)}, f32[4,136,128]{2,1,0:T(8,128)S(1)}, u32[]{:S(2)}, u32[]{:S(2)}) collective-permute-start(f32[4,136,128]{2,1,0:T(8,128)S(1)} %get-tuple-element.34.comb_b), channel_id=1, source_target_pairs={{0,2},{2,0},{1,3},{3,1},{4,6},{6,4},{5,7},{7,5}} | collective-permute-start | bytes 835592 | tf_op jit(solution)/shard_map/ppermute | solution.py:469
  34.3 2.2 %collective-permute-start.1 = (f32[64,2048]{1,0:T(8,128)S(1)}, f32[64,2048]{1,0:T(8,128)S(1)}, u32[]{:S(2)}, u32[]{:S(2)}) collective-permute-start(f32[64,2048]{1,0:T(8,128)S(1)} %get-tuple-element.36), channel_id=1, source_target_pairs={{0,1},{1,0},{2,3},{3,2},{4,5},{5,4},{6,7},{7,6}} | collective-permute-start | bytes 1572872 | tf_op jit(solution)/shard_map/ppermute | solution.py:496
  34.3 2.2 %copy-start = (bf16[64,2048]{1,0:T(8,128)(2,1)S(1)}, bf16[64,2048]{1,0:T(8,128)(2,1)}, u32[]{:S(2)}) copy-start(bf16[64,2048]{1,0:T(8,128)(2,1)} %tok_h.1) | copy-start | bytes 786436

commit v12 on v11

--- a/solution.py
+++ b/solution.py
@@ -23,9 +23,9 @@
 ROWS = SLOTS * KVH
 BLK = 8
 NBLK = SEQS // BLK
-AHEAD = 3
-NX = 4
-NA = 6
+AHEAD = 4
+NX = 3
+NA = 7
 NW = 5
 WAHEAD = 3
 RING = 4
@@ -148,9 +148,9 @@
         w_copy(n, wk).wait()
         if n + WAHEAD < NW:
             w_start(n + WAHEAD)
-        elif n >= NW - 2:
-            k_copy(n - NW + 2).start()
-            v_copy(n - NW + 2).start()
+        else:
+            k_copy(n + WAHEAD - NW).start()
+            v_copy(n + WAHEAD - NW).start()
         proj[n % 2] = jnp.dot(hid[...], w_s[n % RING], preferred_element_type=F32)
 
     multiply(0)
@@ -168,7 +168,7 @@
     post(3)
     q_send(1).start()
     multiply(4)
-    for i in range(2, AHEAD):
+    for i in range(WAHEAD, AHEAD):
         k_copy(i).start()
         v_copy(i).start()
     post(4)
@@ -266,7 +266,7 @@
             k_copy(i + AHEAD).start()
             v_copy(i + AHEAD).start()
 
-        @pl.when(i == NBLK - 1)
+        @pl.when(i + AHEAD == NBLK)
         def _():
             for n in range(4):
                 wo_copy(n).start()
@@ -347,22 +347,19 @@
 
 
 def product_kernel(kv, vv, ki, vi, oa, comb_b, xrx_b, wo_v, ko, vo, part, ofin, ksem, vsem):
-    for c in block_copies(NA, kv, vv, ko, vo, ksem, vsem):
-        c.start()
+    block_copies(NA, kv, vv, ko, vo, ksem, vsem)[0].start()
     for i in range(NBLK - NX):
         last_merge(lax.axis_index('sp') // 2, comb_b, xrx_b, i, ofin, i)
     lhs = jnp.concatenate([oa[...].astype(BF16), ofin[...].astype(BF16)], axis=0)
     for n in range(4):
         part[:, n * WCH:(n + 1) * WCH] = jnp.dot(lhs, wo_v[n], preferred_element_type=F32)
-    for c in block_copies(NA, kv, vv, ko, vo, ksem, vsem):
-        c.wait()
+    block_copies(NA, kv, vv, ko, vo, ksem, vsem)[0].wait()
 
 
 def rest_kernel(kv, vv, ki, vi, ko, vo, ksem, vsem):
-    for c in block_copies(NA + 1, kv, vv, ko, vo, ksem, vsem):
-        c.start()
-    for c in block_copies(NA + 1, kv, vv, ko, vo, ksem, vsem):
-        c.wait()
+    copy = block_copies(NA, kv, vv, ko, vo, ksem, vsem)[1]
+    copy.start()
+    copy.wait()
 
 
 def write_kernel(pos_h, kv, vv, rep, comb_a, xrx, wo_v, ko, vo, nkv, oa, kva, vva, wo_a, pos_s, nkv_s, patch, ksem, vsem, psem, osem):

time: 37.4 us -> 36.1 us (0.965)
  Pallas kernels: 34.2 us -> 32.5 us
    pallas_call x1, Pallas kernels: 21.2 us -> 19.2 us  [device_step(): pl.pallas_call(attend_kernel, out_shape=(pltpu.VMEM(rows, BF16), pltpu.VM...]
    pallas_call x1, Pallas kernels: 8.68 us -> 9.94 us  [device_step(): pl.pallas_call(write_kernel, out_shape=(pltpu.HBM(rows, BF16), pltpu.HBM(...]
    pallas_call x1, Pallas kernels: 2.16 us -> 1.46 us  [device_step(): pl.pallas_call(rest_kernel, out_shape=(pltpu.HBM(rows, BF16), pltpu.HBM(r...]
  transfers between devices with their start and end apart: 2 -> 2, of which waited for: 0 -> 1; matrix products, arithmetic and copies ran while one was open for 0% -> 0% of each run, Pallas kernels for 29% -> 32%
where the time goes in v12:
time: 36.1 us; the launch traced here: 36 us
  Pallas kernels  32.5 us (90%)
  starting transfers between devices  1.73 us (5%)
  other arithmetic  0.79 us (2%)
  between operations  0.68 us (2%)
    pallas_call x1, Pallas kernels, device_step(): pl.pallas_call(attend_kernel, out_shape=(pltpu.VMEM(rows, BF16), pltpu.VM...  19.2 us
    pallas_call x1, Pallas kernels, device_step(): pl.pallas_call(write_kernel, out_shape=(pltpu.HBM(rows, BF16), pltpu.HBM(...  9.94 us
    pallas_call x1, Pallas kernels, device_step(): pl.pallas_call(product_kernel, out_shape=(pltpu.HBM(rows, BF16), pltpu.HB...  1.84 us
    ppermute x1, starting transfers between devices, device_step(): xrx_b = lax.ppermute(comb_b, 'sp', [(0, 2), (2, 0), (1, 3), (3, 1)])  1.59 us
    pallas_call x1, Pallas kernels, device_step(): pl.pallas_call(rest_kernel, out_shape=(pltpu.HBM(rows, BF16), pltpu.HBM(r...  1.46 us
    convert_element_type x1, other arithmetic, device_step(): block_out = (tokens.astype(F32) + (part + other)).astype(BF16)  0.79 us
  transfers between devices with their start and end apart: 2, of which 1 were waited for; matrix products, arithmetic and copies ran while one was open for 0% of the time, Pallas kernels for 32%

profile of v12, /device:TPU:0, one launch (start us, length us, event | category | flops | bytes accessed | tf_op | source)
XLA Modules:
  0.0 36.0 jit_solution(12050855028696368077)
XLA Ops:
  0.6 19.2 %attend.1 = (bf16[64,1024,128]{2,1,0:T(8,128)(2,1)S(1)}, bf16[64,1024,128]{2,1,0:T(8,128)(2,1)S(1)}, f32[2,256,128]{2,1,0:T(8,128)S(1)}, bf16[4,2048,512]{2,1,0:...) custom-call(s32[64]{0:T(128)} %pos_h.3, ...), custom_call_target="tpu_custom_call" | custom-call | tf_op jit(solution)/shard_map/attend/pallas_call | solution.py:439
  19.9 1.6 %collective-permute-start = (f32[5,136,128]{2,1,0:T(8,128)S(1)}, f32[5,136,128]{2,1,0:T(8,128)S(1)}, u32[]{:S(2)}, u32[]{:S(2)}) collective-permute-start(f32[5,136,128]{2,1,0:T(8,128)S(1)} %get-tuple-element.34.comb_b), channel_id=1, source_target_pairs={{0,2},{2,0},{1,3},{3,1},{4,6},{6,4},{5,7},{7,5}} | collective-permute-start | bytes 1044488 | tf_op jit(solution)/shard_map/ppermute | solution.py:466
  21.5 9.9 %write.1 = (bf16[64,1024,128]{2,1,0:T(8,128)(2,1)}, bf16[64,1024,128]{2,1,0:T(8,128)(2,1)}, bf16[64,8,128]{2,1,0:T(8,128)(2,1)}, f32[24,2048]{1,0:T(8,128)S(1)},...) custom-call(s32[64]{0:T(128)} %pos_h.3, ...), custom_call_target="tpu_custom_call", output_to_operand_aliasing={{4}: (1, {}), {5}: (2, {}), {6}: (6, {})} | custom-call | flops 10000000000 | bytes 33554432 | tf_op jit(solution)/shard_map/write/pallas_call | solution.py:467
  31.4 0.0 collective-permute-done.xrx_b
  31.4 1.8 %product.1 = (bf16[64,1024,128]{2,1,0:T(8,128)(2,1)}, bf16[64,1024,128]{2,1,0:T(8,128)(2,1)}, f32[64,2048]{1,0:T(8,128)S(1)}) custom-call(bf16[64,1024,128]{2,1,0:T(8,128)(2,1)S(1)} %get-tuple-element.29.kv, bf16[64,1024,128]{2,1,0:T(8,128)(2,1)S(1)} %get-tuple-element.30.vv, ...), custom_call_target="tpu_custom_call", output_to_operand_aliasing={{0}: (2, {}), {1}: (3, {})} | custom-call | flops 536870912 | bytes 4194304 | tf_op jit(solution)/shard_map/product/pallas_call | solution.py:482
  33.3 0.1 collective-permute-start.1
  33.4 0.0 copy-start
  33.4 1.5 %rest.1 = (bf16[64,1024,128]{2,1,0:T(8,128)(2,1)}, bf16[64,1024,128]{2,1,0:T(8,128)(2,1)}) custom-call(bf16[64,1024,128]{2,1,0:T(8,128)(2,1)S(1)} %get-tuple-element.29.kv, bf16[64,1024,128]{2,1,0:T(8,128)(2,1)S(1)} %get-tuple-element.30.vv, bf16[64,1024,128]{2,1,0:T(8,128)(2,1)} %get-tuple-element.37.ki, ...), custom_call_target="tpu_custom_call", output_to_operand_aliasing={{0}: (2, {}), {1}: (3, {})} | custom-call | flops 1000000000 | bytes 4194304 | tf_op jit(solution)/shard_map/rest/pallas_call | solution.py:494
  34.9 0.3 collective-permute-done.1
  35.2 0.0 copy-done
  35.2 0.8 %add_convert_fusion = bf16[64,2048]{1,0:T(8,128)(2,1)} fusion(f32[64,2048]{1,0:T(8,128)S(1)} %get-tuple-element.36, f32[64,2048]{1,0:T(8,128)S(1)} %collective-permute-done.1, bf16[64,2048]{1,0:T(8,128)(2,1)S(1)} %copy-done), kind=kLoop, calls=%fused_computation | loop fusion | flops 524288 | bytes 1572864 | tf_op jit(solution)/shard_map/convert_element_type | solution.py:505
Async XLA Ops:
  19.9 11.5 %collective-permute-start = (f32[5,136,128]{2,1,0:T(8,128)S(1)}, f32[5,136,128]{2,1,0:T(8,128)S(1)}, u32[]{:S(2)}, u32[]{:S(2)}) collective-permute-start(f32[5,136,128]{2,1,0:T(8,128)S(1)} %get-tuple-element.34.comb_b), channel_id=1, source_target_pairs={{0,2},{2,0},{1,3},{3,1},{4,6},{6,4},{5,7},{7,5}} | collective-permute-start | bytes 1044488 | tf_op jit(solution)/shard_map/ppermute | solution.py:466
  33.3 1.9 %collective-permute-start.1 = (f32[64,2048]{1,0:T(8,128)S(1)}, f32[64,2048]{1,0:T(8,128)S(1)}, u32[]{:S(2)}, u32[]{:S(2)}) collective-permute-start(f32[64,2048]{1,0:T(8,128)S(1)} %get-tuple-element.36), channel_id=1, source_target_pairs={{0,1},{1,0},{2,3},{3,2},{4,5},{5,4},{6,7},{7,6}} | collective-permute-start | bytes 1572872 | tf_op jit(solution)/shard_map/ppermute | solution.py:493
  33.4 1.8 %copy-start = (bf16[64,2048]{1,0:T(8,128)(2,1)S(1)}, bf16[64,2048]{1,0:T(8,128)(2,1)}, u32[]{:S(2)}) copy-start(bf16[64,2048]{1,0:T(8,128)(2,1)} %tok_h.1) | copy-start | bytes 786436

commit v13 on v12

--- a/solution.py
+++ b/solution.py
@@ -266,7 +266,7 @@
             k_copy(i + AHEAD).start()
             v_copy(i + AHEAD).start()
 
-        @pl.when(i + AHEAD == NBLK)
+        @pl.when(i == NBLK - 2)
         def _():
             for n in range(4):
                 wo_copy(n).start()

time: 36.1 us -> 36.3 us (level)
  no operation moved by 1% of the time
where the time goes in v13:
time: 36.3 us; the launch traced here: 36.2 us
  Pallas kernels  32.5 us (90%)
  starting transfers between devices  1.82 us (5%)
  other arithmetic  0.79 us (2%)
  between operations  0.69 us (2%)
  waiting for transfers between devices  0.41 us (1%)
    pallas_call x1, Pallas kernels, device_step(): pl.pallas_call(attend_kernel, out_shape=(pltpu.VMEM(rows, BF16), pltpu.VM...  19.2 us
    pallas_call x1, Pallas kernels, device_step(): pl.pallas_call(write_kernel, out_shape=(pltpu.HBM(rows, BF16), pltpu.HBM(...  9.94 us
    pallas_call x1, Pallas kernels, device_step(): pl.pallas_call(product_kernel, out_shape=(pltpu.HBM(rows, BF16), pltpu.HB...  1.84 us
    ppermute x1, starting transfers between devices, device_step(): xrx_b = lax.ppermute(comb_b, 'sp', [(0, 2), (2, 0), (1, 3), (3, 1)])  1.8 us
    pallas_call x1, Pallas kernels, device_step(): pl.pallas_call(rest_kernel, out_shape=(pltpu.HBM(rows, BF16), pltpu.HBM(r...  1.47 us
    convert_element_type x1, other arithmetic, device_step(): block_out = (tokens.astype(F32) + (part + other)).astype(BF16)  0.79 us
  transfers between devices with their start and end apart: 2, of which 1 were waited for; matrix products, arithmetic and copies ran while one was open for 0% of the time, Pallas kernels for 32%

profile of v13, /device:TPU:0, one launch (start us, length us, event | category | flops | bytes accessed | tf_op | source)
XLA Modules:
  0.0 36.2 jit_solution(14014806763059749574)
XLA Ops:
  0.6 19.2 %attend.1 = (bf16[64,1024,128]{2,1,0:T(8,128)(2,1)S(1)}, bf16[64,1024,128]{2,1,0:T(8,128)(2,1)S(1)}, f32[2,256,128]{2,1,0:T(8,128)S(1)}, bf16[4,2048,512]{2,1,0:...) custom-call(s32[64]{0:T(128)} %pos_h.3, ...), custom_call_target="tpu_custom_call" | custom-call | tf_op jit(solution)/shard_map/attend/pallas_call | solution.py:439
  19.9 1.8 %collective-permute-start = (f32[5,136,128]{2,1,0:T(8,128)S(1)}, f32[5,136,128]{2,1,0:T(8,128)S(1)}, u32[]{:S(2)}, u32[]{:S(2)}) collective-permute-start(f32[5,136,128]{2,1,0:T(8,128)S(1)} %get-tuple-element.34.comb_b), channel_id=1, source_target_pairs={{0,2},{2,0},{1,3},{3,1},{4,6},{6,4},{5,7},{7,5}} | collective-permute-start | bytes 1044488 | tf_op jit(solution)/shard_map/ppermute | solution.py:466
  21.7 9.9 %write.1 = (bf16[64,1024,128]{2,1,0:T(8,128)(2,1)}, bf16[64,1024,128]{2,1,0:T(8,128)(2,1)}, bf16[64,8,128]{2,1,0:T(8,128)(2,1)}, f32[24,2048]{1,0:T(8,128)S(1)},...) custom-call(s32[64]{0:T(128)} %pos_h.3, ...), custom_call_target="tpu_custom_call", output_to_operand_aliasing={{4}: (1, {}), {5}: (2, {}), {6}: (6, {})} | custom-call | flops 10000000000 | bytes 33554432 | tf_op jit(solution)/shard_map/write/pallas_call | solution.py:467
  31.6 0.0 collective-permute-done.xrx_b
  31.6 1.8 %product.1 = (bf16[64,1024,128]{2,1,0:T(8,128)(2,1)}, bf16[64,1024,128]{2,1,0:T(8,128)(2,1)}, f32[64,2048]{1,0:T(8,128)S(1)}) custom-call(bf16[64,1024,128]{2,1,0:T(8,128)(2,1)S(1)} %get-tuple-element.29.kv, bf16[64,1024,128]{2,1,0:T(8,128)(2,1)S(1)} %get-tuple-element.30.vv, ...), custom_call_target="tpu_custom_call", output_to_operand_aliasing={{0}: (2, {}), {1}: (3, {})} | custom-call | flops 536870912 | bytes 4194304 | tf_op jit(solution)/shard_map/product/pallas_call | solution.py:482
  33.5 0.0 collective-permute-start.1
  33.5 0.0 copy-start
  33.5 1.5 %rest.1 = (bf16[64,1024,128]{2,1,0:T(8,128)(2,1)}, bf16[64,1024,128]{2,1,0:T(8,128)(2,1)}) custom-call(bf16[64,1024,128]{2,1,0:T(8,128)(2,1)S(1)} %get-tuple-element.29.kv, bf16[64,1024,128]{2,1,0:T(8,128)(2,1)S(1)} %get-tuple-element.30.vv, bf16[64,1024,128]{2,1,0:T(8,128)(2,1)} %get-tuple-element.37.ki, ...), custom_call_target="tpu_custom_call", output_to_operand_aliasing={{0}: (2, {}), {1}: (3, {})} | custom-call | flops 1000000000 | bytes 4194304 | tf_op jit(solution)/shard_map/rest/pallas_call | solution.py:494
  35.0 0.4 %collective-permute-done.1 = f32[64,2048]{1,0:T(8,128)S(1)} collective-permute-done((f32[64,2048]{1,0:T(8,128)S(1)}, f32[64,2048]{1,0:T(8,128)S(1)}, u32[]{:S(2)}, u32[]{:S(2)}) %collective-permute-start.1) | collective-permute-done | bytes 524320 | tf_op jit(solution)/shard_map/ppermute | solution.py:493
  35.4 0.0 copy-done
  35.4 0.8 %add_convert_fusion = bf16[64,2048]{1,0:T(8,128)(2,1)} fusion(f32[64,2048]{1,0:T(8,128)S(1)} %get-tuple-element.36, f32[64,2048]{1,0:T(8,128)S(1)} %collective-permute-done.1, bf16[64,2048]{1,0:T(8,128)(2,1)S(1)} %copy-done), kind=kLoop, calls=%fused_computation | loop fusion | flops 524288 | bytes 1572864 | tf_op jit(solution)/shard_map/convert_element_type | solution.py:505
Async XLA Ops:
  19.9 11.7 %collective-permute-start = (f32[5,136,128]{2,1,0:T(8,128)S(1)}, f32[5,136,128]{2,1,0:T(8,128)S(1)}, u32[]{:S(2)}, u32[]{:S(2)}) collective-permute-start(f32[5,136,128]{2,1,0:T(8,128)S(1)} %get-tuple-element.34.comb_b), channel_id=1, source_target_pairs={{0,2},{2,0},{1,3},{3,1},{4,6},{6,4},{5,7},{7,5}} | collective-permute-start | bytes 1044488 | tf_op jit(solution)/shard_map/ppermute | solution.py:466
  33.5 1.9 %collective-permute-start.1 = (f32[64,2048]{1,0:T(8,128)S(1)}, f32[64,2048]{1,0:T(8,128)S(1)}, u32[]{:S(2)}, u32[]{:S(2)}) collective-permute-start(f32[64,2048]{1,0:T(8,128)S(1)} %get-tuple-element.36), channel_id=1, source_target_pairs={{0,1},{1,0},{2,3},{3,2},{4,5},{5,4},{6,7},{7,6}} | collective-permute-start | bytes 1572872 | tf_op jit(solution)/shard_map/ppermute | solution.py:493
  33.5 1.9 %copy-start = (bf16[64,2048]{1,0:T(8,128)(2,1)S(1)}, bf16[64,2048]{1,0:T(8,128)(2,1)}, u32[]{:S(2)}) copy-start(bf16[64,2048]{1,0:T(8,128)(2,1)} %tok_h.1) | copy-start | bytes 786436

commit v14 on v12

--- a/solution.py
+++ b/solution.py
@@ -25,7 +25,7 @@
 NBLK = SEQS // BLK
 AHEAD = 4
 NX = 3
-NA = 7
+NA = 6
 NW = 5
 WAHEAD = 3
 RING = 4
@@ -279,11 +279,11 @@
 
     def sending(i, carry):
         fetch(i)
-        d_send(i - LAG).wait_recv()
-        combine(i - LAG, comb_a, i - LAG)
         attend(i)
         d_send(i).start()
-        x_send(i - LAG).start()
+        d_send(i - 1).wait_recv()
+        combine(i - 1, comb_a, i - 1)
+        x_send(i - 1).start()
         return carry
 
     def keeping(i, carry):
@@ -302,8 +302,9 @@
     k_copy(0).wait()
     attend(0, first=True)
     new_send().wait()
-    lax.fori_loop(0, LAG, early, 0)
-    lax.fori_loop(LAG, LAG + NX, sending, 0)
+    early(0, 0)
+    lax.fori_loop(1, 1 + NX, sending, 0)
+    lax.fori_loop(1 + NX, LAG + NX, early, 0)
     lax.fori_loop(LAG + NX, NBLK, keeping, 0)
     lax.fori_loop(NBLK - LAG, NBLK, late, 0)
 
@@ -347,19 +348,20 @@
 
 
 def product_kernel(kv, vv, ki, vi, oa, comb_b, xrx_b, wo_v, ko, vo, part, ofin, ksem, vsem):
-    block_copies(NA, kv, vv, ko, vo, ksem, vsem)[0].start()
+    block_copies(NA, kv, vv, ko, vo, ksem, vsem)[1].start()
     for i in range(NBLK - NX):
         last_merge(lax.axis_index('sp') // 2, comb_b, xrx_b, i, ofin, i)
     lhs = jnp.concatenate([oa[...].astype(BF16), ofin[...].astype(BF16)], axis=0)
     for n in range(4):
         part[:, n * WCH:(n + 1) * WCH] = jnp.dot(lhs, wo_v[n], preferred_element_type=F32)
-    block_copies(NA, kv, vv, ko, vo, ksem, vsem)[0].wait()
+    block_copies(NA, kv, vv, ko, vo, ksem, vsem)[1].wait()
 
 
 def rest_kernel(kv, vv, ki, vi, ko, vo, ksem, vsem):
-    copy = block_copies(NA, kv, vv, ko, vo, ksem, vsem)[1]
-    copy.start()
-    copy.wait()
+    for c in block_copies(NA + 1, kv, vv, ko, vo, ksem, vsem):
+        c.start()
+    for c in block_copies(NA + 1, kv, vv, ko, vo, ksem, vsem):
+        c.wait()
 
 
 def write_kernel(pos_h, kv, vv, rep, comb_a, xrx, wo_v, ko, vo, nkv, oa, kva, vva, wo_a, pos_s, nkv_s, patch, ksem, vsem, psem, osem):
@@ -408,6 +410,7 @@
         if 1 < i <= NA:
             for c in copies(i - 1):
                 c.start()
+    copies(NA)[0].start()
     nkv_copy = pltpu.make_async_copy(nkv_s, nkv, osem.at[1])
     nkv_copy.start()
     each(0, stage)
@@ -421,6 +424,7 @@
     for i in range(1, NA):
         for c in copies(i):
             c.wait()
+    copies(NA)[0].wait()
 
 
 def solution(mesh):

time: 36.1 us -> 36.1 us (level)
  starting transfers between devices: 1.73 us -> 2.77 us
  Pallas kernels: 32.5 us -> 31.7 us
    ppermute x1, starting transfers between devices: 1.59 us -> 2.67 us  [device_step(): xrx_b = lax.ppermute(comb_b, 'sp', [(0, 2), (2, 0), (1, 3), (3, 1)])]
    pallas_call x1, Pallas kernels: 19.2 us -> 18.4 us  [device_step(): pl.pallas_call(attend_kernel, out_shape=(pltpu.VMEM(rows, BF16), pltpu.VM...]
    pallas_call x1, Pallas kernels: 1.46 us -> 2.15 us  [device_step(): pl.pallas_call(rest_kernel, out_shape=(pltpu.HBM(rows, BF16), pltpu.HBM(r...]
    pallas_call x1, Pallas kernels: 9.94 us -> 9.31 us  [device_step(): pl.pallas_call(write_kernel, out_shape=(pltpu.HBM(rows, BF16), pltpu.HBM(...]
  transfers between devices with their start and end apart: 2 -> 2, of which waited for: 1 -> 0; matrix products, arithmetic and copies ran while one was open for 0% -> 0% of each run, Pallas kernels for 32% -> 32%
where the time goes in v14:
time: 36.1 us; the launch traced here: 36 us
  Pallas kernels  31.7 us (88%)
  starting transfers between devices  2.77 us (8%)
  other arithmetic  0.79 us (2%)
  between operations  0.69 us (2%)
    pallas_call x1, Pallas kernels, device_step(): pl.pallas_call(attend_kernel, out_shape=(pltpu.VMEM(rows, BF16), pltpu.VM...  18.4 us
    pallas_call x1, Pallas kernels, device_step(): pl.pallas_call(write_kernel, out_shape=(pltpu.HBM(rows, BF16), pltpu.HBM(...  9.31 us
    ppermute x1, starting transfers between devices, device_step(): xrx_b = lax.ppermute(comb_b, 'sp', [(0, 2), (2, 0), (1, 3), (3, 1)])  2.67 us
    pallas_call x1, Pallas kernels, device_step(): pl.pallas_call(rest_kernel, out_shape=(pltpu.HBM(rows, BF16), pltpu.HBM(r...  2.15 us
    pallas_call x1, Pallas kernels, device_step(): pl.pallas_call(product_kernel, out_shape=(pltpu.HBM(rows, BF16), pltpu.HB...  1.84 us
    convert_element_type x1, other arithmetic, device_step(): block_out = (tokens.astype(F32) + (part + other)).astype(BF16)  0.79 us
  transfers between devices with their start and end apart: 2, of which 0 were waited for; matrix products, arithmetic and copies ran while one was open for 0% of the time, Pallas kernels for 32%

profile of v14, /device:TPU:0, one launch (start us, length us, event | category | flops | bytes accessed | tf_op | source)
XLA Modules:
  0.0 36.0 jit_solution(2432001371203193841)
XLA Ops:
  0.6 18.4 %attend.1 = (bf16[64,1024,128]{2,1,0:T(8,128)(2,1)S(1)}, bf16[64,1024,128]{2,1,0:T(8,128)(2,1)S(1)}, f32[2,256,128]{2,1,0:T(8,128)S(1)}, bf16[4,2048,512]{2,1,0:...) custom-call(s32[64]{0:T(128)} %pos_h.3, ...), custom_call_target="tpu_custom_call" | custom-call | tf_op jit(solution)/shard_map/attend/pallas_call | solution.py:443
  19.1 2.7 %collective-permute-start = (f32[5,136,128]{2,1,0:T(8,128)S(1)}, f32[5,136,128]{2,1,0:T(8,128)S(1)}, u32[]{:S(2)}, u32[]{:S(2)}) collective-permute-start(f32[5,136,128]{2,1,0:T(8,128)S(1)} %get-tuple-element.34.comb_b), channel_id=1, source_target_pairs={{0,2},{2,0},{1,3},{3,1},{4,6},{6,4},{5,7},{7,5}} | collective-permute-start | bytes 1044488 | tf_op jit(solution)/shard_map/ppermute | solution.py:470
  21.7 9.3 %write.1 = (bf16[64,1024,128]{2,1,0:T(8,128)(2,1)}, bf16[64,1024,128]{2,1,0:T(8,128)(2,1)}, bf16[64,8,128]{2,1,0:T(8,128)(2,1)}, f32[24,2048]{1,0:T(8,128)S(1)},...) custom-call(s32[64]{0:T(128)} %pos_h.3, ...), custom_call_target="tpu_custom_call", output_to_operand_aliasing={{4}: (1, {}), {5}: (2, {}), {6}: (6, {})} | custom-call | flops 10000000000 | bytes 33554432 | tf_op jit(solution)/shard_map/write/pallas_call | solution.py:471
  31.1 0.0 collective-permute-done.xrx_b
  31.1 1.8 %product.1 = (bf16[64,1024,128]{2,1,0:T(8,128)(2,1)}, bf16[64,1024,128]{2,1,0:T(8,128)(2,1)}, f32[64,2048]{1,0:T(8,128)S(1)}) custom-call(bf16[64,1024,128]{2,1,0:T(8,128)(2,1)S(1)} %get-tuple-element.29.kv, bf16[64,1024,128]{2,1,0:T(8,128)(2,1)S(1)} %get-tuple-element.30.vv, ...), custom_call_target="tpu_custom_call", output_to_operand_aliasing={{0}: (2, {}), {1}: (3, {})} | custom-call | flops 536870912 | bytes 4194304 | tf_op jit(solution)/shard_map/product/pallas_call | solution.py:486
  32.9 0.1 collective-permute-start.1
  33.0 0.0 copy-start
  33.0 2.1 %rest.1 = (bf16[64,1024,128]{2,1,0:T(8,128)(2,1)}, bf16[64,1024,128]{2,1,0:T(8,128)(2,1)}) custom-call(bf16[64,1024,128]{2,1,0:T(8,128)(2,1)S(1)} %get-tuple-element.29.kv, bf16[64,1024,128]{2,1,0:T(8,128)(2,1)S(1)} %get-tuple-element.30.vv, bf16[64,1024,128]{2,1,0:T(8,128)(2,1)} %get-tuple-element.37.ki, ...), custom_call_target="tpu_custom_call", output_to_operand_aliasing={{0}: (2, {}), {1}: (3, {})} | custom-call | flops 1000000000 | bytes 4194304 | tf_op jit(solution)/shard_map/rest/pallas_call | solution.py:498
  35.2 0.0 collective-permute-done.1
  35.2 0.0 copy-done
  35.2 0.8 %add_convert_fusion = bf16[64,2048]{1,0:T(8,128)(2,1)} fusion(f32[64,2048]{1,0:T(8,128)S(1)} %get-tuple-element.36, f32[64,2048]{1,0:T(8,128)S(1)} %collective-permute-done.1, bf16[64,2048]{1,0:T(8,128)(2,1)S(1)} %copy-done), kind=kLoop, calls=%fused_computation | loop fusion | flops 524288 | bytes 1572864 | tf_op jit(solution)/shard_map/convert_element_type | solution.py:509
Async XLA Ops:
  19.1 12.0 %collective-permute-start = (f32[5,136,128]{2,1,0:T(8,128)S(1)}, f32[5,136,128]{2,1,0:T(8,128)S(1)}, u32[]{:S(2)}, u32[]{:S(2)}) collective-permute-start(f32[5,136,128]{2,1,0:T(8,128)S(1)} %get-tuple-element.34.comb_b), channel_id=1, source_target_pairs={{0,2},{2,0},{1,3},{3,1},{4,6},{6,4},{5,7},{7,5}} | collective-permute-start | bytes 1044488 | tf_op jit(solution)/shard_map/ppermute | solution.py:470
  32.9 2.3 %collective-permute-start.1 = (f32[64,2048]{1,0:T(8,128)S(1)}, f32[64,2048]{1,0:T(8,128)S(1)}, u32[]{:S(2)}, u32[]{:S(2)}) collective-permute-start(f32[64,2048]{1,0:T(8,128)S(1)} %get-tuple-element.36), channel_id=1, source_target_pairs={{0,1},{1,0},{2,3},{3,2},{4,5},{5,4},{6,7},{7,6}} | collective-permute-start | bytes 1572872 | tf_op jit(solution)/shard_map/ppermute | solution.py:497
  33.0 2.2 %copy-start = (bf16[64,2048]{1,0:T(8,128)(2,1)S(1)}, bf16[64,2048]{1,0:T(8,128)(2,1)}, u32[]{:S(2)}) copy-start(bf16[64,2048]{1,0:T(8,128)(2,1)} %tok_h.1) | copy-start | bytes 786436

commit v15 on v14

--- a/solution.py
+++ b/solution.py
@@ -26,6 +26,7 @@
 AHEAD = 4
 NX = 3
 NA = 6
+WSPLIT = 2
 NW = 5
 WAHEAD = 3
 RING = 4
@@ -41,6 +42,11 @@
     return jnp.broadcast_to(tile[:, col:col + 1], (tile.shape[0], HD))
 
 
+def out_weight_copy(n, core, wo, wo_v, wosem):
+    src = wo.at[pl.ds(pl.multiple_of(core * (HALF * HD), HD), HALF * HD), pl.ds(n * WCH, WCH)]
+    return pltpu.make_async_copy(src, wo_v.at[n], wosem.at[n])
+
+
 def attend_kernel(pos_h, tok_h, an_h, qn_h, kn_h, freq_h, wq, wk, wv, wo, kc, vc,
                   kv, vv, rep, wo_v, comb_a, comb_b, xrx,
                   pos_s, tok, an, qn, kn, freq, insem, proj, w_s, hid, ang, cosr, sinr, qmine, qmate, colslot, opart, drx, sc, pr_s,
@@ -69,8 +75,7 @@
                 w_copy(n, wv).start()
 
     def wo_copy(n):
-        src = wo.at[pl.ds(pl.multiple_of(core * (HALF * HD), HD), HALF * HD), pl.ds(n * WCH, WCH)]
-        return pltpu.make_async_copy(src, wo_v.at[n], wosem.at[n])
+        return out_weight_copy(n, core, wo, wo_v, wosem)
 
     def k_copy(i):
         return pltpu.make_async_copy(kc.at[pl.ds(i * BLK, BLK)], kv.at[pl.ds(i * BLK, BLK)], ksem.at[i])
@@ -268,7 +273,7 @@
 
         @pl.when(i + AHEAD == NBLK)
         def _():
-            for n in range(4):
+            for n in range(WSPLIT):
                 wo_copy(n).start()
 
     def early(i, carry):
@@ -308,7 +313,7 @@
     lax.fori_loop(LAG + NX, NBLK, keeping, 0)
     lax.fori_loop(NBLK - LAG, NBLK, late, 0)
 
-    for n in range(4):
+    for n in range(WSPLIT):
         wo_copy(n).wait()
 
     def drain(i, carry):
@@ -348,13 +353,15 @@
 
 
 def product_kernel(kv, vv, ki, vi, oa, comb_b, xrx_b, wo_v, ko, vo, part, ofin, ksem, vsem):
-    block_copies(NA, kv, vv, ko, vo, ksem, vsem)[1].start()
+    for c in block_copies(NA, kv, vv, ko, vo, ksem, vsem):
+        c.start()
     for i in range(NBLK - NX):
         last_merge(lax.axis_index('sp') // 2, comb_b, xrx_b, i, ofin, i)
     lhs = jnp.concatenate([oa[...].astype(BF16), ofin[...].astype(BF16)], axis=0)
     for n in range(4):
         part[:, n * WCH:(n + 1) * WCH] = jnp.dot(lhs, wo_v[n], preferred_element_type=F32)
-    block_copies(NA, kv, vv, ko, vo, ksem, vsem)[1].wait()
+    for c in block_copies(NA, kv, vv, ko, vo, ksem, vsem):
+        c.wait()
 
 
 def rest_kernel(kv, vv, ki, vi, ko, vo, ksem, vsem):
@@ -364,7 +371,7 @@
         c.wait()
 
 
-def write_kernel(pos_h, kv, vv, rep, comb_a, xrx, wo_v, ko, vo, nkv, oa, kva, vva, wo_a, pos_s, nkv_s, patch, ksem, vsem, psem, osem):
+def write_kernel(pos_h, kv, vv, rep, comb_a, xrx, wo_v, wo, ko, vo, nkv, oa, kva, vva, wo_a, pos_s, nkv_s, patch, ksem, vsem, psem, osem, wosem):
     start = lax.axis_index('sp') * SLOTS
     slot16 = lax.broadcasted_iota(jnp.int32, (4 * KVH, HD), 0) // KVH
 
@@ -410,7 +417,9 @@
         if 1 < i <= NA:
             for c in copies(i - 1):
                 c.start()
-    copies(NA)[0].start()
+    core = lax.rem(lax.axis_index('sp'), 2)
+    for n in range(WSPLIT, 4):
+        out_weight_copy(n, core, wo, wo_v, wosem).start()
     nkv_copy = pltpu.make_async_copy(nkv_s, nkv, osem.at[1])
     nkv_copy.start()
     each(0, stage)
@@ -424,7 +433,8 @@
     for i in range(1, NA):
         for c in copies(i):
             c.wait()
-    copies(NA)[0].wait()
+    for n in range(WSPLIT, 4):
+        out_weight_copy(n, core, wo, wo_v, wosem).wait()
 
 
 def solution(mesh):
@@ -473,16 +483,16 @@
             out_shape=(pltpu.HBM(rows, BF16), pltpu.HBM(rows, BF16), pltpu.HBM((SEQS, 2 * KVH, HD), BF16),
                        pltpu.VMEM((NX * BLK, HALF * HD), F32), pltpu.VMEM(rows, BF16), pltpu.VMEM(rows, BF16),
                        pltpu.VMEM((4, HALF * HD, WCH), BF16)),
-            in_specs=[hbm, vm, vm, vm, vm, vm, vm],
+            in_specs=[hbm, vm, vm, vm, vm, vm, vm, hbm],
             out_specs=(hbm, hbm, hbm, vm, vm, vm, vm),
             input_output_aliases={1: 4, 2: 5, 6: 6},
             scratch_shapes=[pltpu.SMEM((SEQS,), jnp.int32), pltpu.VMEM((SEQS, 2 * KVH, HD), BF16),
                             pltpu.VMEM((2, BLK, 4 * KVH, HD), BF16),
-                            dma((NBLK,)), dma((NBLK,)), dma((2, BLK)), dma((2,))],
+                            dma((NBLK,)), dma((NBLK,)), dma((2, BLK)), dma((2,)), dma((4,))],
             compiler_params=pltpu.CompilerParams(vmem_limit_bytes=VMEM_LIMIT),
             cost_estimate=pl.CostEstimate(flops=10**10, bytes_accessed=2**25, transcendentals=0),
             name='write',
-        )(in_hbm(positions), in_vmem(kv), in_vmem(vv), in_vmem(rep), in_vmem(comb_a), in_vmem(xrx_a), in_vmem(wo_v))
+        )(in_hbm(positions), in_vmem(kv), in_vmem(vv), in_vmem(rep), in_vmem(comb_a), in_vmem(xrx_a), in_vmem(wo_v), in_hbm(w_o))
         k_out, v_out, part = pl.pallas_call(
             product_kernel,
             out_shape=(pltpu.HBM(rows, BF16), pltpu.HBM(rows, BF16), pltpu.VMEM((SEQS, DIM), F32)),

time: 36.1 us -> 36.8 us (1.019)
  Pallas kernels: 31.7 us -> 32.4 us
    pallas_call x1, Pallas kernels: 9.31 us -> 9.69 us  [device_step(): pl.pallas_call(write_kernel, out_shape=(pltpu.HBM(rows, BF16), pltpu.HBM(...]
where the time goes in v15:
time: 36.8 us; the launch traced here: 36.7 us
  Pallas kernels  32.4 us (88%)
  starting transfers between devices  2.78 us (8%)
  other arithmetic  0.79 us (2%)
  between operations  0.69 us (2%)
    pallas_call x1, Pallas kernels, device_step(): pl.pallas_call(attend_kernel, out_shape=(pltpu.VMEM(rows, BF16), pltpu.VM...  18.4 us
    pallas_call x1, Pallas kernels, device_step(): pl.pallas_call(write_kernel, out_shape=(pltpu.HBM(rows, BF16), pltpu.HBM(...  9.69 us
    ppermute x1, starting transfers between devices, device_step(): xrx_b = lax.ppermute(comb_b, 'sp', [(0, 2), (2, 0), (1, 3), (3, 1)])  2.67 us
    pallas_call x1, Pallas kernels, device_step(): pl.pallas_call(product_kernel, out_shape=(pltpu.HBM(rows, BF16), pltpu.HB...  2.17 us
    pallas_call x1, Pallas kernels, device_step(): pl.pallas_call(rest_kernel, out_shape=(pltpu.HBM(rows, BF16), pltpu.HBM(r...  2.15 us
    convert_element_type x1, other arithmetic, device_step(): block_out = (tokens.astype(F32) + (part + other)).astype(BF16)  0.79 us
  transfers between devices with their start and end apart: 2, of which 0 were waited for; matrix products, arithmetic and copies ran while one was open for 0% of the time, Pallas kernels for 32%

profile of v15, /device:TPU:0, one launch (start us, length us, event | category | flops | bytes accessed | tf_op | source)
XLA Modules:
  0.0 36.7 jit_solution(17479608339055046339)
XLA Ops:
  0.6 18.4 %attend.1 = (bf16[64,1024,128]{2,1,0:T(8,128)(2,1)S(1)}, bf16[64,1024,128]{2,1,0:T(8,128)(2,1)S(1)}, f32[2,256,128]{2,1,0:T(8,128)S(1)}, bf16[4,2048,512]{2,1,0:...) custom-call(s32[64]{0:T(128)} %pos_h.3, ...), custom_call_target="tpu_custom_call" | custom-call | tf_op jit(solution)/shard_map/attend/pallas_call | solution.py:453
  19.1 2.7 %collective-permute-start = (f32[5,136,128]{2,1,0:T(8,128)S(1)}, f32[5,136,128]{2,1,0:T(8,128)S(1)}, u32[]{:S(2)}, u32[]{:S(2)}) collective-permute-start(f32[5,136,128]{2,1,0:T(8,128)S(1)} %get-tuple-element.34.comb_b), channel_id=1, source_target_pairs={{0,2},{2,0},{1,3},{3,1},{4,6},{6,4},{5,7},{7,5}} | collective-permute-start | bytes 1044488 | tf_op jit(solution)/shard_map/ppermute | solution.py:480
  21.7 9.7 %write.1 = (bf16[64,1024,128]{2,1,0:T(8,128)(2,1)}, bf16[64,1024,128]{2,1,0:T(8,128)(2,1)}, bf16[64,8,128]{2,1,0:T(8,128)(2,1)}, f32[24,2048]{1,0:T(8,128)S(1)},...) custom-call(s32[64]{0:T(128)} %pos_h.3, ...), custom_call_target="tpu_custom_call", output_to_operand_aliasing={{4}: (1, {}), {5}: (2, {}), {6}: (6, {})} | custom-call | flops 10000000000 | bytes 33554432 | tf_op jit(solution)/shard_map/write/pallas_call | solution.py:481
  31.4 0.0 collective-permute-done.xrx_b
  31.4 2.2 %product.1 = (bf16[64,1024,128]{2,1,0:T(8,128)(2,1)}, bf16[64,1024,128]{2,1,0:T(8,128)(2,1)}, f32[64,2048]{1,0:T(8,128)S(1)}) custom-call(bf16[64,1024,128]{2,1,0:T(8,128)(2,1)S(1)} %get-tuple-element.29.kv, bf16[64,1024,128]{2,1,0:T(8,128)(2,1)S(1)} %get-tuple-element.30.vv, ...), custom_call_target="tpu_custom_call", output_to_operand_aliasing={{0}: (2, {}), {1}: (3, {})} | custom-call | flops 536870912 | bytes 4194304 | tf_op jit(solution)/shard_map/product/pallas_call | solution.py:496
  33.6 0.1 collective-permute-start.1
  33.7 0.0 copy-start
  33.7 2.1 %rest.1 = (bf16[64,1024,128]{2,1,0:T(8,128)(2,1)}, bf16[64,1024,128]{2,1,0:T(8,128)(2,1)}) custom-call(bf16[64,1024,128]{2,1,0:T(8,128)(2,1)S(1)} %get-tuple-element.29.kv, bf16[64,1024,128]{2,1,0:T(8,128)(2,1)S(1)} %get-tuple-element.30.vv, bf16[64,1024,128]{2,1,0:T(8,128)(2,1)} %get-tuple-element.37.ki, ...), custom_call_target="tpu_custom_call", output_to_operand_aliasing={{0}: (2, {}), {1}: (3, {})} | custom-call | flops 1000000000 | bytes 4194304 | tf_op jit(solution)/shard_map/rest/pallas_call | solution.py:508
  35.9 0.0 collective-permute-done.1
  35.9 0.0 copy-done
  35.9 0.8 %add_convert_fusion = bf16[64,2048]{1,0:T(8,128)(2,1)} fusion(f32[64,2048]{1,0:T(8,128)S(1)} %get-tuple-element.36, f32[64,2048]{1,0:T(8,128)S(1)} %collective-permute-done.1, bf16[64,2048]{1,0:T(8,128)(2,1)S(1)} %copy-done), kind=kLoop, calls=%fused_computation | loop fusion | flops 524288 | bytes 1572864 | tf_op jit(solution)/shard_map/convert_element_type | solution.py:519
Async XLA Ops:
  19.1 12.4 %collective-permute-start = (f32[5,136,128]{2,1,0:T(8,128)S(1)}, f32[5,136,128]{2,1,0:T(8,128)S(1)}, u32[]{:S(2)}, u32[]{:S(2)}) collective-permute-start(f32[5,136,128]{2,1,0:T(8,128)S(1)} %get-tuple-element.34.comb_b), channel_id=1, source_target_pairs={{0,2},{2,0},{1,3},{3,1},{4,6},{6,4},{5,7},{7,5}} | collective-permute-start | bytes 1044488 | tf_op jit(solution)/shard_map/ppermute | solution.py:480
  33.6 2.3 %collective-permute-start.1 = (f32[64,2048]{1,0:T(8,128)S(1)}, f32[64,2048]{1,0:T(8,128)S(1)}, u32[]{:S(2)}, u32[]{:S(2)}) collective-permute-start(f32[64,2048]{1,0:T(8,128)S(1)} %get-tuple-element.36), channel_id=1, source_target_pairs={{0,1},{1,0},{2,3},{3,2},{4,5},{5,4},{6,7},{7,6}} | collective-permute-start | bytes 1572872 | tf_op jit(solution)/shard_map/ppermute | solution.py:507
  33.7 2.2 %copy-start = (bf16[64,2048]{1,0:T(8,128)(2,1)S(1)}, bf16[64,2048]{1,0:T(8,128)(2,1)}, u32[]{:S(2)}) copy-start(bf16[64,2048]{1,0:T(8,128)(2,1)} %tok_h.1) | copy-start | bytes 786436

commit v16 on v15

--- a/solution.py
+++ b/solution.py
@@ -24,9 +24,9 @@
 BLK = 8
 NBLK = SEQS // BLK
 AHEAD = 4
-NX = 3
+NX = 4
 NA = 6
-WSPLIT = 2
+WSPLIT = 4
 NW = 5
 WAHEAD = 3
 RING = 4
@@ -149,13 +149,15 @@
             else:
                 rep.at[core][pl.ds(j, SEQS, stride=KVH), :] = jnp.where(core == 0, norm_rope(x, kgain), x)
 
+    def cache_start(t):
+        (v_copy if t % 2 else k_copy)(t // 2).start()
+
     def multiply(n):
         w_copy(n, wk).wait()
         if n + WAHEAD < NW:
             w_start(n + WAHEAD)
         else:
-            k_copy(n + WAHEAD - NW).start()
-            v_copy(n + WAHEAD - NW).start()
+            cache_start(n + WAHEAD - NW)
         proj[n % 2] = jnp.dot(hid[...], w_s[n % RING], preferred_element_type=F32)
 
     multiply(0)
@@ -173,11 +175,12 @@
     post(3)
     q_send(1).start()
     multiply(4)
-    for i in range(WAHEAD, AHEAD):
-        k_copy(i).start()
-        v_copy(i).start()
+    cache_start(WAHEAD)
+    cache_start(WAHEAD + 1)
     post(4)
     new_send().start()
+    for t in range(WAHEAD + 2, 2 * AHEAD):
+        cache_start(t)
     start = me * SLOTS
     lane = lax.broadcasted_iota(jnp.int32, (HALF, HD), 1)
     lrow = lax.broadcasted_iota(jnp.int32, (HALF, HD), 0)

time: 36.8 us -> 36 us (0.978)
  starting transfers between devices: 2.78 us -> 1.71 us
    pallas_call x1, Pallas kernels: 18.4 us -> 19.7 us  [device_step(): pl.pallas_call(attend_kernel, out_shape=(pltpu.VMEM(rows, BF16), pltpu.VM...]
    ppermute x1, starting transfers between devices: 2.67 us -> 1.57 us  [device_step(): xrx_b = lax.ppermute(comb_b, 'sp', [(0, 2), (2, 0), (1, 3), (3, 1)])]
    pallas_call x1, Pallas kernels: 9.69 us -> 8.71 us  [device_step(): pl.pallas_call(write_kernel, out_shape=(pltpu.HBM(rows, BF16), pltpu.HBM(...]
  transfers between devices with their start and end apart: 2 -> 2, of which waited for: 0 -> 0; matrix products, arithmetic and copies ran while one was open for 0% -> 0% of each run, Pallas kernels for 32% -> 30%
where the time goes in v16:
time: 36 us; the launch traced here: 35.9 us
  Pallas kernels  32.7 us (91%)
  starting transfers between devices  1.71 us (5%)
  other arithmetic  0.77 us (2%)
  between operations  0.69 us (2%)
    pallas_call x1, Pallas kernels, device_step(): pl.pallas_call(attend_kernel, out_shape=(pltpu.VMEM(rows, BF16), pltpu.VM...  19.7 us
    pallas_call x1, Pallas kernels, device_step(): pl.pallas_call(write_kernel, out_shape=(pltpu.HBM(rows, BF16), pltpu.HBM(...  8.71 us
    pallas_call x1, Pallas kernels, device_step(): pl.pallas_call(product_kernel, out_shape=(pltpu.HBM(rows, BF16), pltpu.HB...  2.17 us
    pallas_call x1, Pallas kernels, device_step(): pl.pallas_call(rest_kernel, out_shape=(pltpu.HBM(rows, BF16), pltpu.HBM(r...  2.15 us
    ppermute x1, starting transfers between devices, device_step(): xrx_b = lax.ppermute(comb_b, 'sp', [(0, 2), (2, 0), (1, 3), (3, 1)])  1.57 us
    convert_element_type x1, other arithmetic, device_step(): block_out = (tokens.astype(F32) + (part + other)).astype(BF16)  0.77 us
  transfers between devices with their start and end apart: 2, of which 0 were waited for; matrix products, arithmetic and copies ran while one was open for 0% of the time, Pallas kernels for 30%

profile of v16, /device:TPU:0, one launch (start us, length us, event | category | flops | bytes accessed | tf_op | source)
XLA Modules:
  0.0 35.9 jit_solution(1782748362864828176)
XLA Ops:
  0.6 19.7 %attend.1 = (bf16[64,1024,128]{2,1,0:T(8,128)(2,1)S(1)}, bf16[64,1024,128]{2,1,0:T(8,128)(2,1)S(1)}, f32[2,256,128]{2,1,0:T(8,128)S(1)}, bf16[4,2048,512]{2,1,0:...) custom-call(s32[64]{0:T(128)} %pos_h.3, ...), custom_call_target="tpu_custom_call" | custom-call | tf_op jit(solution)/shard_map/attend/pallas_call | solution.py:456
  20.3 1.6 %collective-permute-start = (f32[4,136,128]{2,1,0:T(8,128)S(1)}, f32[4,136,128]{2,1,0:T(8,128)S(1)}, u32[]{:S(2)}, u32[]{:S(2)}) collective-permute-start(f32[4,136,128]{2,1,0:T(8,128)S(1)} %get-tuple-element.34.comb_b), channel_id=1, source_target_pairs={{0,2},{2,0},{1,3},{3,1},{4,6},{6,4},{5,7},{7,5}} | collective-permute-start | bytes 835592 | tf_op jit(solution)/shard_map/ppermute | solution.py:483
  21.9 8.7 %write.1 = (bf16[64,1024,128]{2,1,0:T(8,128)(2,1)}, bf16[64,1024,128]{2,1,0:T(8,128)(2,1)}, bf16[64,8,128]{2,1,0:T(8,128)(2,1)}, f32[32,2048]{1,0:T(8,128)S(1)},...) custom-call(s32[64]{0:T(128)} %pos_h.3, ...), custom_call_target="tpu_custom_call", output_to_operand_aliasing={{4}: (1, {}), {5}: (2, {}), {6}: (6, {})} | custom-call | flops 10000000000 | bytes 33554432 | tf_op jit(solution)/shard_map/write/pallas_call | solution.py:484
  30.6 0.0 collective-permute-done.xrx_b
  30.6 2.2 %product.1 = (bf16[64,1024,128]{2,1,0:T(8,128)(2,1)}, bf16[64,1024,128]{2,1,0:T(8,128)(2,1)}, f32[64,2048]{1,0:T(8,128)S(1)}) custom-call(bf16[64,1024,128]{2,1,0:T(8,128)(2,1)S(1)} %get-tuple-element.29.kv, bf16[64,1024,128]{2,1,0:T(8,128)(2,1)S(1)} %get-tuple-element.30.vv, ...), custom_call_target="tpu_custom_call", output_to_operand_aliasing={{0}: (2, {}), {1}: (3, {})} | custom-call | flops 536870912 | bytes 4194304 | tf_op jit(solution)/shard_map/product/pallas_call | solution.py:499
  32.8 0.1 collective-permute-start.1
  32.9 0.0 copy-start
  32.9 2.1 %rest.1 = (bf16[64,1024,128]{2,1,0:T(8,128)(2,1)}, bf16[64,1024,128]{2,1,0:T(8,128)(2,1)}) custom-call(bf16[64,1024,128]{2,1,0:T(8,128)(2,1)S(1)} %get-tuple-element.29.kv, bf16[64,1024,128]{2,1,0:T(8,128)(2,1)S(1)} %get-tuple-element.30.vv, bf16[64,1024,128]{2,1,0:T(8,128)(2,1)} %get-tuple-element.37.ki, ...), custom_call_target="tpu_custom_call", output_to_operand_aliasing={{0}: (2, {}), {1}: (3, {})} | custom-call | flops 1000000000 | bytes 4194304 | tf_op jit(solution)/shard_map/rest/pallas_call | solution.py:511
  35.1 0.0 collective-permute-done.1
  35.1 0.0 copy-done
  35.1 0.8 %add_convert_fusion = bf16[64,2048]{1,0:T(8,128)(2,1)} fusion(f32[64,2048]{1,0:T(8,128)S(1)} %get-tuple-element.36, f32[64,2048]{1,0:T(8,128)S(1)} %collective-permute-done.1, bf16[64,2048]{1,0:T(8,128)(2,1)S(1)} %copy-done), kind=kLoop, calls=%fused_computation | loop fusion | flops 524288 | bytes 1572864 | tf_op jit(solution)/shard_map/convert_element_type | solution.py:522
Async XLA Ops:
  20.3 10.3 %collective-permute-start = (f32[4,136,128]{2,1,0:T(8,128)S(1)}, f32[4,136,128]{2,1,0:T(8,128)S(1)}, u32[]{:S(2)}, u32[]{:S(2)}) collective-permute-start(f32[4,136,128]{2,1,0:T(8,128)S(1)} %get-tuple-element.34.comb_b), channel_id=1, source_target_pairs={{0,2},{2,0},{1,3},{3,1},{4,6},{6,4},{5,7},{7,5}} | collective-permute-start | bytes 835592 | tf_op jit(solution)/shard_map/ppermute | solution.py:483
  32.8 2.3 %collective-permute-start.1 = (f32[64,2048]{1,0:T(8,128)S(1)}, f32[64,2048]{1,0:T(8,128)S(1)}, u32[]{:S(2)}, u32[]{:S(2)}) collective-permute-start(f32[64,2048]{1,0:T(8,128)S(1)} %get-tuple-element.36), channel_id=1, source_target_pairs={{0,1},{1,0},{2,3},{3,2},{4,5},{5,4},{6,7},{7,6}} | collective-permute-start | bytes 1572872 | tf_op jit(solution)/shard_map/ppermute | solution.py:510
  32.9 2.2 %copy-start = (bf16[64,2048]{1,0:T(8,128)(2,1)S(1)}, bf16[64,2048]{1,0:T(8,128)(2,1)}, u32[]{:S(2)}) copy-start(bf16[64,2048]{1,0:T(8,128)(2,1)} %tok_h.1) | copy-start | bytes 786436

commit v17 on v16

--- a/solution.py
+++ b/solution.py
@@ -156,8 +156,8 @@
         w_copy(n, wk).wait()
         if n + WAHEAD < NW:
             w_start(n + WAHEAD)
-        else:
-            cache_start(n + WAHEAD - NW)
+        if n > 0:
+            cache_start(n - 1)
         proj[n % 2] = jnp.dot(hid[...], w_s[n % RING], preferred_element_type=F32)
 
     multiply(0)
@@ -175,11 +175,11 @@
     post(3)
     q_send(1).start()
     multiply(4)
-    cache_start(WAHEAD)
-    cache_start(WAHEAD + 1)
+    cache_start(NW - 1)
+    cache_start(NW)
     post(4)
     new_send().start()
-    for t in range(WAHEAD + 2, 2 * AHEAD):
+    for t in range(NW + 1, 2 * AHEAD):
         cache_start(t)
     start = me * SLOTS
     lane = lax.broadcasted_iota(jnp.int32, (HALF, HD), 1)

time: 36 us -> 36.5 us (1.014)
  Pallas kernels: 32.7 us -> 33.2 us
    pallas_call x1, Pallas kernels: 19.7 us -> 20.2 us  [device_step(): pl.pallas_call(attend_kernel, out_shape=(pltpu.VMEM(rows, BF16), pltpu.VM...]
where the time goes in v17:
time: 36.5 us; the launch traced here: 36.4 us
  Pallas kernels  33.2 us (91%)
  starting transfers between devices  1.71 us (5%)
  other arithmetic  0.77 us (2%)
  between operations  0.69 us (2%)
    pallas_call x1, Pallas kernels, device_step(): pl.pallas_call(attend_kernel, out_shape=(pltpu.VMEM(rows, BF16), pltpu.VM...  20.2 us
    pallas_call x1, Pallas kernels, device_step(): pl.pallas_call(write_kernel, out_shape=(pltpu.HBM(rows, BF16), pltpu.HBM(...  8.71 us
    pallas_call x1, Pallas kernels, device_step(): pl.pallas_call(product_kernel, out_shape=(pltpu.HBM(rows, BF16), pltpu.HB...  2.17 us
    pallas_call x1, Pallas kernels, device_step(): pl.pallas_call(rest_kernel, out_shape=(pltpu.HBM(rows, BF16), pltpu.HBM(r...  2.15 us
    ppermute x1, starting transfers between devices, device_step(): xrx_b = lax.ppermute(comb_b, 'sp', [(0, 2), (2, 0), (1, 3), (3, 1)])  1.56 us
    convert_element_type x1, other arithmetic, device_step(): block_out = (tokens.astype(F32) + (part + other)).astype(BF16)  0.77 us
  transfers between devices with their start and end apart: 2, of which 0 were waited for; matrix products, arithmetic and copies ran while one was open for 0% of the time, Pallas kernels for 30%

profile of v17, /device:TPU:0, one launch (start us, length us, event | category | flops | bytes accessed | tf_op | source)
XLA Modules:
  0.0 36.4 jit_solution(9359384900155073042)
XLA Ops:
  0.6 20.2 %attend.1 = (bf16[64,1024,128]{2,1,0:T(8,128)(2,1)S(1)}, bf16[64,1024,128]{2,1,0:T(8,128)(2,1)S(1)}, f32[2,256,128]{2,1,0:T(8,128)S(1)}, bf16[4,2048,512]{2,1,0:...) custom-call(s32[64]{0:T(128)} %pos_h.3, ...), custom_call_target="tpu_custom_call" | custom-call | tf_op jit(solution)/shard_map/attend/pallas_call | solution.py:456
  20.9 1.6 %collective-permute-start = (f32[4,136,128]{2,1,0:T(8,128)S(1)}, f32[4,136,128]{2,1,0:T(8,128)S(1)}, u32[]{:S(2)}, u32[]{:S(2)}) collective-permute-start(f32[4,136,128]{2,1,0:T(8,128)S(1)} %get-tuple-element.34.comb_b), channel_id=1, source_target_pairs={{0,2},{2,0},{1,3},{3,1},{4,6},{6,4},{5,7},{7,5}} | collective-permute-start | bytes 835592 | tf_op jit(solution)/shard_map/ppermute | solution.py:483
  22.4 8.7 %write.1 = (bf16[64,1024,128]{2,1,0:T(8,128)(2,1)}, bf16[64,1024,128]{2,1,0:T(8,128)(2,1)}, bf16[64,8,128]{2,1,0:T(8,128)(2,1)}, f32[32,2048]{1,0:T(8,128)S(1)},...) custom-call(s32[64]{0:T(128)} %pos_h.3, ...), custom_call_target="tpu_custom_call", output_to_operand_aliasing={{4}: (1, {}), {5}: (2, {}), {6}: (6, {})} | custom-call | flops 10000000000 | bytes 33554432 | tf_op jit(solution)/shard_map/write/pallas_call | solution.py:484
  31.1 0.0 collective-permute-done.xrx_b
  31.2 2.2 %product.1 = (bf16[64,1024,128]{2,1,0:T(8,128)(2,1)}, bf16[64,1024,128]{2,1,0:T(8,128)(2,1)}, f32[64,2048]{1,0:T(8,128)S(1)}) custom-call(bf16[64,1024,128]{2,1,0:T(8,128)(2,1)S(1)} %get-tuple-element.29.kv, bf16[64,1024,128]{2,1,0:T(8,128)(2,1)S(1)} %get-tuple-element.30.vv, ...), custom_call_target="tpu_custom_call", output_to_operand_aliasing={{0}: (2, {}), {1}: (3, {})} | custom-call | flops 536870912 | bytes 4194304 | tf_op jit(solution)/shard_map/product/pallas_call | solution.py:499
  33.3 0.1 collective-permute-start.1
  33.5 0.0 copy-start
  33.5 2.1 %rest.1 = (bf16[64,1024,128]{2,1,0:T(8,128)(2,1)}, bf16[64,1024,128]{2,1,0:T(8,128)(2,1)}) custom-call(bf16[64,1024,128]{2,1,0:T(8,128)(2,1)S(1)} %get-tuple-element.29.kv, bf16[64,1024,128]{2,1,0:T(8,128)(2,1)S(1)} %get-tuple-element.30.vv, bf16[64,1024,128]{2,1,0:T(8,128)(2,1)} %get-tuple-element.37.ki, ...), custom_call_target="tpu_custom_call", output_to_operand_aliasing={{0}: (2, {}), {1}: (3, {})} | custom-call | flops 1000000000 | bytes 4194304 | tf_op jit(solution)/shard_map/rest/pallas_call | solution.py:511
  35.6 0.0 collective-permute-done.1
  35.6 0.0 copy-done
  35.7 0.8 %add_convert_fusion = bf16[64,2048]{1,0:T(8,128)(2,1)} fusion(f32[64,2048]{1,0:T(8,128)S(1)} %get-tuple-element.36, f32[64,2048]{1,0:T(8,128)S(1)} %collective-permute-done.1, bf16[64,2048]{1,0:T(8,128)(2,1)S(1)} %copy-done), kind=kLoop, calls=%fused_computation | loop fusion | flops 524288 | bytes 1572864 | tf_op jit(solution)/shard_map/convert_element_type | solution.py:522
Async XLA Ops:
  20.9 10.3 %collective-permute-start = (f32[4,136,128]{2,1,0:T(8,128)S(1)}, f32[4,136,128]{2,1,0:T(8,128)S(1)}, u32[]{:S(2)}, u32[]{:S(2)}) collective-permute-start(f32[4,136,128]{2,1,0:T(8,128)S(1)} %get-tuple-element.34.comb_b), channel_id=1, source_target_pairs={{0,2},{2,0},{1,3},{3,1},{4,6},{6,4},{5,7},{7,5}} | collective-permute-start | bytes 835592 | tf_op jit(solution)/shard_map/ppermute | solution.py:483
  33.3 2.3 %collective-permute-start.1 = (f32[64,2048]{1,0:T(8,128)S(1)}, f32[64,2048]{1,0:T(8,128)S(1)}, u32[]{:S(2)}, u32[]{:S(2)}) collective-permute-start(f32[64,2048]{1,0:T(8,128)S(1)} %get-tuple-element.36), channel_id=1, source_target_pairs={{0,1},{1,0},{2,3},{3,2},{4,5},{5,4},{6,7},{7,6}} | collective-permute-start | bytes 1572872 | tf_op jit(solution)/shard_map/ppermute | solution.py:510
  33.5 2.2 %copy-start = (bf16[64,2048]{1,0:T(8,128)(2,1)S(1)}, bf16[64,2048]{1,0:T(8,128)(2,1)}, u32[]{:S(2)}) copy-start(bf16[64,2048]{1,0:T(8,128)(2,1)} %tok_h.1) | copy-start | bytes 786436

commit v18 on v16

--- a/solution.py
+++ b/solution.py
@@ -23,7 +23,7 @@
 ROWS = SLOTS * KVH
 BLK = 8
 NBLK = SEQS // BLK
-AHEAD = 4
+AHEAD = 2
 NX = 4
 NA = 6
 WSPLIT = 4
@@ -176,10 +176,9 @@
     q_send(1).start()
     multiply(4)
     cache_start(WAHEAD)
-    cache_start(WAHEAD + 1)
     post(4)
     new_send().start()
-    for t in range(WAHEAD + 2, 2 * AHEAD):
+    for t in range(WAHEAD + 1, 2 * AHEAD):
         cache_start(t)
     start = me * SLOTS
     lane = lax.broadcasted_iota(jnp.int32, (HALF, HD), 1)

time: 36 us -> 39.1 us (1.086)
  Pallas kernels: 32.7 us -> 34.6 us
  starting transfers between devices: 1.71 us -> 2.85 us
    pallas_call x1, Pallas kernels: 19.7 us -> 21.6 us  [device_step(): pl.pallas_call(attend_kernel, out_shape=(pltpu.VMEM(rows, BF16), pltpu.VM...]
    ppermute x1, starting transfers between devices: 1.57 us -> 2.82 us  [device_step(): xrx_b = lax.ppermute(comb_b, 'sp', [(0, 2), (2, 0), (1, 3), (3, 1)])]
  transfers between devices with their start and end apart: 2 -> 2, of which waited for: 0 -> 0; matrix products, arithmetic and copies ran while one was open for 0% -> 0% of each run, Pallas kernels for 30% -> 28%
where the time goes in v18:
time: 39.1 us; the launch traced here: 39 us
  Pallas kernels  34.6 us (88%)
  starting transfers between devices  2.85 us (7%)
  other arithmetic  0.77 us (2%)
  between operations  0.71 us (2%)
    pallas_call x1, Pallas kernels, device_step(): pl.pallas_call(attend_kernel, out_shape=(pltpu.VMEM(rows, BF16), pltpu.VM...  21.6 us
    pallas_call x1, Pallas kernels, device_step(): pl.pallas_call(write_kernel, out_shape=(pltpu.HBM(rows, BF16), pltpu.HBM(...  8.71 us
    ppermute x1, starting transfers between devices, device_step(): xrx_b = lax.ppermute(comb_b, 'sp', [(0, 2), (2, 0), (1, 3), (3, 1)])  2.82 us
    pallas_call x1, Pallas kernels, device_step(): pl.pallas_call(product_kernel, out_shape=(pltpu.HBM(rows, BF16), pltpu.HB...  2.17 us
    pallas_call x1, Pallas kernels, device_step(): pl.pallas_call(rest_kernel, out_shape=(pltpu.HBM(rows, BF16), pltpu.HBM(r...  2.16 us
  transfers between devices with their start and end apart: 2, of which 0 were waited for; matrix products, arithmetic and copies ran while one was open for 0% of the time, Pallas kernels for 28%

profile of v18, /device:TPU:0, one launch (start us, length us, event | category | flops | bytes accessed | tf_op | source)
XLA Modules:
  0.0 39.0 jit_solution(2030414746441884613)
XLA Ops:
  0.6 21.6 %attend.1 = (bf16[64,1024,128]{2,1,0:T(8,128)(2,1)S(1)}, bf16[64,1024,128]{2,1,0:T(8,128)(2,1)S(1)}, f32[2,256,128]{2,1,0:T(8,128)S(1)}, bf16[4,2048,512]{2,1,0:...) custom-call(s32[64]{0:T(128)} %pos_h.3, ...), custom_call_target="tpu_custom_call" | custom-call | tf_op jit(solution)/shard_map/attend/pallas_call | solution.py:455
  22.2 2.8 %collective-permute-start = (f32[4,136,128]{2,1,0:T(8,128)S(1)}, f32[4,136,128]{2,1,0:T(8,128)S(1)}, u32[]{:S(2)}, u32[]{:S(2)}) collective-permute-start(f32[4,136,128]{2,1,0:T(8,128)S(1)} %get-tuple-element.34.comb_b), channel_id=1, source_target_pairs={{0,2},{2,0},{1,3},{3,1},{4,6},{6,4},{5,7},{7,5}} | collective-permute-start | bytes 835592 | tf_op jit(solution)/shard_map/ppermute | solution.py:482
  25.0 8.7 %write.1 = (bf16[64,1024,128]{2,1,0:T(8,128)(2,1)}, bf16[64,1024,128]{2,1,0:T(8,128)(2,1)}, bf16[64,8,128]{2,1,0:T(8,128)(2,1)}, f32[32,2048]{1,0:T(8,128)S(1)},...) custom-call(s32[64]{0:T(128)} %pos_h.3, ...), custom_call_target="tpu_custom_call", output_to_operand_aliasing={{4}: (1, {}), {5}: (2, {}), {6}: (6, {})} | custom-call | flops 10000000000 | bytes 33554432 | tf_op jit(solution)/shard_map/write/pallas_call | solution.py:483
  33.8 0.0 collective-permute-done.xrx_b
  33.8 2.2 %product.1 = (bf16[64,1024,128]{2,1,0:T(8,128)(2,1)}, bf16[64,1024,128]{2,1,0:T(8,128)(2,1)}, f32[64,2048]{1,0:T(8,128)S(1)}) custom-call(bf16[64,1024,128]{2,1,0:T(8,128)(2,1)S(1)} %get-tuple-element.29.kv, bf16[64,1024,128]{2,1,0:T(8,128)(2,1)S(1)} %get-tuple-element.30.vv, ...), custom_call_target="tpu_custom_call", output_to_operand_aliasing={{0}: (2, {}), {1}: (3, {})} | custom-call | flops 536870912 | bytes 4194304 | tf_op jit(solution)/shard_map/product/pallas_call | solution.py:498
  36.0 0.0 collective-permute-start.1
  36.0 0.0 copy-start
  36.0 2.2 %rest.1 = (bf16[64,1024,128]{2,1,0:T(8,128)(2,1)}, bf16[64,1024,128]{2,1,0:T(8,128)(2,1)}) custom-call(bf16[64,1024,128]{2,1,0:T(8,128)(2,1)S(1)} %get-tuple-element.29.kv, bf16[64,1024,128]{2,1,0:T(8,128)(2,1)S(1)} %get-tuple-element.30.vv, bf16[64,1024,128]{2,1,0:T(8,128)(2,1)} %get-tuple-element.37.ki, ...), custom_call_target="tpu_custom_call", output_to_operand_aliasing={{0}: (2, {}), {1}: (3, {})} | custom-call | flops 1000000000 | bytes 4194304 | tf_op jit(solution)/shard_map/rest/pallas_call | solution.py:510
  38.2 0.0 collective-permute-done.1
  38.2 0.0 copy-done
  38.2 0.8 %add_convert_fusion = bf16[64,2048]{1,0:T(8,128)(2,1)} fusion(f32[64,2048]{1,0:T(8,128)S(1)} %get-tuple-element.36, f32[64,2048]{1,0:T(8,128)S(1)} %collective-permute-done.1, bf16[64,2048]{1,0:T(8,128)(2,1)S(1)} %copy-done), kind=kLoop, calls=%fused_computation | loop fusion | flops 524288 | bytes 1572864 | tf_op jit(solution)/shard_map/convert_element_type | solution.py:521
Async XLA Ops:
  22.2 11.5 %collective-permute-start = (f32[4,136,128]{2,1,0:T(8,128)S(1)}, f32[4,136,128]{2,1,0:T(8,128)S(1)}, u32[]{:S(2)}, u32[]{:S(2)}) collective-permute-start(f32[4,136,128]{2,1,0:T(8,128)S(1)} %get-tuple-element.34.comb_b), channel_id=1, source_target_pairs={{0,2},{2,0},{1,3},{3,1},{4,6},{6,4},{5,7},{7,5}} | collective-permute-start | bytes 835592 | tf_op jit(solution)/shard_map/ppermute | solution.py:482
  36.0 2.2 %collective-permute-start.1 = (f32[64,2048]{1,0:T(8,128)S(1)}, f32[64,2048]{1,0:T(8,128)S(1)}, u32[]{:S(2)}, u32[]{:S(2)}) collective-permute-start(f32[64,2048]{1,0:T(8,128)S(1)} %get-tuple-element.36), channel_id=1, source_target_pairs={{0,1},{1,0},{2,3},{3,2},{4,5},{5,4},{6,7},{7,6}} | collective-permute-start | bytes 1572872 | tf_op jit(solution)/shard_map/ppermute | solution.py:509
  36.0 2.2 %copy-start = (bf16[64,2048]{1,0:T(8,128)(2,1)S(1)}, bf16[64,2048]{1,0:T(8,128)(2,1)}, u32[]{:S(2)}) copy-start(bf16[64,2048]{1,0:T(8,128)(2,1)} %tok_h.1) | copy-start | bytes 786436

commit v19 on v16

--- a/solution.py
+++ b/solution.py
@@ -23,7 +23,7 @@
 ROWS = SLOTS * KVH
 BLK = 8
 NBLK = SEQS // BLK
-AHEAD = 4
+AHEAD = 6
 NX = 4
 NA = 6
 WSPLIT = 4
@@ -179,7 +179,7 @@
     cache_start(WAHEAD + 1)
     post(4)
     new_send().start()
-    for t in range(WAHEAD + 2, 2 * AHEAD):
+    for t in range(WAHEAD + 2, 2 * 4):
         cache_start(t)
     start = me * SLOTS
     lane = lax.broadcasted_iota(jnp.int32, (HALF, HD), 1)
@@ -274,7 +274,7 @@
             k_copy(i + AHEAD).start()
             v_copy(i + AHEAD).start()
 
-        @pl.when(i + AHEAD == NBLK)
+        @pl.when(i == NBLK - 4)
         def _():
             for n in range(WSPLIT):
                 wo_copy(n).start()
@@ -310,6 +310,8 @@
     k_copy(0).wait()
     attend(0, first=True)
     new_send().wait()
+    for t in range(2 * 4, 2 * AHEAD):
+        cache_start(t)
     early(0, 0)
     lax.fori_loop(1, 1 + NX, sending, 0)
     lax.fori_loop(1 + NX, LAG + NX, early, 0)

time: 36 us -> 36 us (level)
  no operation moved by 1% of the time
where the time goes in v19:
time: 36 us; the launch traced here: 35.9 us
  Pallas kernels  32.7 us (91%)
  starting transfers between devices  1.71 us (5%)
  other arithmetic  0.77 us (2%)
  between operations  0.69 us (2%)
    pallas_call x1, Pallas kernels, device_step(): pl.pallas_call(attend_kernel, out_shape=(pltpu.VMEM(rows, BF16), pltpu.VM...  19.7 us
    pallas_call x1, Pallas kernels, device_step(): pl.pallas_call(write_kernel, out_shape=(pltpu.HBM(rows, BF16), pltpu.HBM(...  8.71 us
    pallas_call x1, Pallas kernels, device_step(): pl.pallas_call(product_kernel, out_shape=(pltpu.HBM(rows, BF16), pltpu.HB...  2.17 us
    pallas_call x1, Pallas kernels, device_step(): pl.pallas_call(rest_kernel, out_shape=(pltpu.HBM(rows, BF16), pltpu.HBM(r...  2.15 us
    ppermute x1, starting transfers between devices, device_step(): xrx_b = lax.ppermute(comb_b, 'sp', [(0, 2), (2, 0), (1, 3), (3, 1)])  1.57 us
    convert_element_type x1, other arithmetic, device_step(): block_out = (tokens.astype(F32) + (part + other)).astype(BF16)  0.77 us
  transfers between devices with their start and end apart: 2, of which 0 were waited for; matrix products, arithmetic and copies ran while one was open for 0% of the time, Pallas kernels for 30%

profile of v19, /device:TPU:0, one launch (start us, length us, event | category | flops | bytes accessed | tf_op | source)
XLA Modules:
  0.0 35.9 jit_solution(4184131609487842926)
XLA Ops:
  0.6 19.7 %attend.1 = (bf16[64,1024,128]{2,1,0:T(8,128)(2,1)S(1)}, bf16[64,1024,128]{2,1,0:T(8,128)(2,1)S(1)}, f32[2,256,128]{2,1,0:T(8,128)S(1)}, bf16[4,2048,512]{2,1,0:...) custom-call(s32[64]{0:T(128)} %pos_h.3, ...), custom_call_target="tpu_custom_call" | custom-call | tf_op jit(solution)/shard_map/attend/pallas_call | solution.py:458
  20.3 1.6 %collective-permute-start = (f32[4,136,128]{2,1,0:T(8,128)S(1)}, f32[4,136,128]{2,1,0:T(8,128)S(1)}, u32[]{:S(2)}, u32[]{:S(2)}) collective-permute-start(f32[4,136,128]{2,1,0:T(8,128)S(1)} %get-tuple-element.34.comb_b), channel_id=1, source_target_pairs={{0,2},{2,0},{1,3},{3,1},{4,6},{6,4},{5,7},{7,5}} | collective-permute-start | bytes 835592 | tf_op jit(solution)/shard_map/ppermute | solution.py:485
  21.9 8.7 %write.1 = (bf16[64,1024,128]{2,1,0:T(8,128)(2,1)}, bf16[64,1024,128]{2,1,0:T(8,128)(2,1)}, bf16[64,8,128]{2,1,0:T(8,128)(2,1)}, f32[32,2048]{1,0:T(8,128)S(1)},...) custom-call(s32[64]{0:T(128)} %pos_h.3, ...), custom_call_target="tpu_custom_call", output_to_operand_aliasing={{4}: (1, {}), {5}: (2, {}), {6}: (6, {})} | custom-call | flops 10000000000 | bytes 33554432 | tf_op jit(solution)/shard_map/write/pallas_call | solution.py:486
  30.6 0.0 collective-permute-done.xrx_b
  30.6 2.2 %product.1 = (bf16[64,1024,128]{2,1,0:T(8,128)(2,1)}, bf16[64,1024,128]{2,1,0:T(8,128)(2,1)}, f32[64,2048]{1,0:T(8,128)S(1)}) custom-call(bf16[64,1024,128]{2,1,0:T(8,128)(2,1)S(1)} %get-tuple-element.29.kv, bf16[64,1024,128]{2,1,0:T(8,128)(2,1)S(1)} %get-tuple-element.30.vv, ...), custom_call_target="tpu_custom_call", output_to_operand_aliasing={{0}: (2, {}), {1}: (3, {})} | custom-call | flops 536870912 | bytes 4194304 | tf_op jit(solution)/shard_map/product/pallas_call | solution.py:501
  32.8 0.1 collective-permute-start.1
  32.9 0.0 copy-start
  32.9 2.1 %rest.1 = (bf16[64,1024,128]{2,1,0:T(8,128)(2,1)}, bf16[64,1024,128]{2,1,0:T(8,128)(2,1)}) custom-call(bf16[64,1024,128]{2,1,0:T(8,128)(2,1)S(1)} %get-tuple-element.29.kv, bf16[64,1024,128]{2,1,0:T(8,128)(2,1)S(1)} %get-tuple-element.30.vv, bf16[64,1024,128]{2,1,0:T(8,128)(2,1)} %get-tuple-element.37.ki, ...), custom_call_target="tpu_custom_call", output_to_operand_aliasing={{0}: (2, {}), {1}: (3, {})} | custom-call | flops 1000000000 | bytes 4194304 | tf_op jit(solution)/shard_map/rest/pallas_call | solution.py:513
  35.1 0.0 collective-permute-done.1
  35.1 0.0 copy-done
  35.1 0.8 %add_convert_fusion = bf16[64,2048]{1,0:T(8,128)(2,1)} fusion(f32[64,2048]{1,0:T(8,128)S(1)} %get-tuple-element.36, f32[64,2048]{1,0:T(8,128)S(1)} %collective-permute-done.1, bf16[64,2048]{1,0:T(8,128)(2,1)S(1)} %copy-done), kind=kLoop, calls=%fused_computation | loop fusion | flops 524288 | bytes 1572864 | tf_op jit(solution)/shard_map/convert_element_type | solution.py:524
Async XLA Ops:
  20.3 10.3 %collective-permute-start = (f32[4,136,128]{2,1,0:T(8,128)S(1)}, f32[4,136,128]{2,1,0:T(8,128)S(1)}, u32[]{:S(2)}, u32[]{:S(2)}) collective-permute-start(f32[4,136,128]{2,1,0:T(8,128)S(1)} %get-tuple-element.34.comb_b), channel_id=1, source_target_pairs={{0,2},{2,0},{1,3},{3,1},{4,6},{6,4},{5,7},{7,5}} | collective-permute-start | bytes 835592 | tf_op jit(solution)/shard_map/ppermute | solution.py:485
  32.8 2.3 %collective-permute-start.1 = (f32[64,2048]{1,0:T(8,128)S(1)}, f32[64,2048]{1,0:T(8,128)S(1)}, u32[]{:S(2)}, u32[]{:S(2)}) collective-permute-start(f32[64,2048]{1,0:T(8,128)S(1)} %get-tuple-element.36), channel_id=1, source_target_pairs={{0,1},{1,0},{2,3},{3,2},{4,5},{5,4},{6,7},{7,6}} | collective-permute-start | bytes 1572872 | tf_op jit(solution)/shard_map/ppermute | solution.py:512
  32.9 2.2 %copy-start = (bf16[64,2048]{1,0:T(8,128)(2,1)S(1)}, bf16[64,2048]{1,0:T(8,128)(2,1)}, u32[]{:S(2)}) copy-start(bf16[64,2048]{1,0:T(8,128)(2,1)} %tok_h.1) | copy-start | bytes 786436
